TPU v7x, 32 devices: a whole 2x2x4 slice. The times are simulated.
32 devices in a mesh: col: 16 (over z, x, core), row: 2 (over y).
Axes of the slice: x: 2, y: 2, z: 4, core: 2. Of those that a mesh axis runs over, the one named last changes fastest.
Arguments:
- hidden: bfloat16 [32768, 768], P(('col', 'row')), may hold values from -6 to 6
- cotangent: bfloat16 [32768, 768], P(('col', 'row')), may hold values from -6 to 6
- rand_blocks: int32 [32, 14, 12, 3], P(('col', 'row')), may hold values from 1 to 14, as said below
- w_query: bfloat16 [768, 768], P('col', 'row'), may hold values from -0.21875 to 0.21875
- w_key: bfloat16 [768, 768], P('col', 'row'), may hold values from -0.21875 to 0.21875
- w_value: bfloat16 [768, 768], P('col', 'row'), may hold values from -0.21875 to 0.21875
- w_out: bfloat16 [768, 768], P('row', 'col'), may hold values from -2.5 to 2.5
- w_up: bfloat16 [768, 3072], P('col', 'row'), may hold values from -0.21875 to 0.21875
- w_down: bfloat16 [3072, 768], P('row', 'col'), may hold values from -0.109375 to 0.109375
- query_bias: bfloat16 [768], P('row'), may hold values from -3 to 3
- value_bias: bfloat16 [768], P('row'), may hold values from -3 to 3
- out_bias: bfloat16 [768], P('row'), may hold values from -2 to 2
- up_bias: bfloat16 [3072], P('row'), may hold values from -3 to 3
- down_bias: bfloat16 [768], P('row'), may hold values from -2 to 2
- norm1_gain: bfloat16 [768], P('row'), may hold values from 0.5 to 1.5
- norm1_shift: bfloat16 [768], P('row'), may hold values from -2 to 2
- norm2_gain: bfloat16 [768], P('row'), may hold values from 0.5 to 1.5
- norm2_shift: bfloat16 [768], P('row'), may hold values from -2 to 2
Outputs:
- output: float32 [32768, 768], P(('col', 'row'))
- hidden_grad: float32 [32768, 768], P(('col', 'row'))
- grad_query: float32 [768, 768], P('col', 'row')
- grad_key: float32 [768, 768], P('col', 'row')
- grad_value: float32 [768, 768], P('col', 'row')
- grad_out: float32 [768, 768], P('row', 'col')
- grad_up: float32 [768, 3072], P('col', 'row')
- grad_down: float32 [3072, 768], P('row', 'col')
- grad_query_bias: float32 [768], P('row')
- grad_value_bias: float32 [768], P('row')
- grad_out_bias: float32 [768], P('row')
- grad_up_bias: float32 [3072], P('row')
- grad_down_bias: float32 [768], P('row')
- grad_norm1_gain: float32 [768], P('row')
- grad_norm1_shift: float32 [768], P('row')
- grad_norm2_gain: float32 [768], P('row')
- grad_norm2_shift: float32 [768], P('row')
Inputs may be any that keep to these rules, and one draw needn't show every extreme that they name: `rand_blocks`: for sequence s, middle query block i (entry i - 1 of the second dimension) and head h, the 3 entries are different blocks, none of them 0, 15, i - 1, i or i + 1.
All inputs are finite; a program needn't handle non-finite values.
Results may differ from a plain program's by a relative error of at most 0.019.
Values may be sent and summed in bfloat16 or wider, within the bound.
A program may use at most 384 MiB of HBM per device.

v0:
```python
import jax
import jax.numpy as jnp
from jax import lax
from jax.sharding import PartitionSpec as P

D = 768
H = 12
BLK = 64
LENGTH = 1024


EPS = 1e-12
NEG = -1e30


def product(left, right):
    return jnp.dot(left, right, preferred_element_type=jnp.float32)


def left_product(left, right):
    return lax.dot_general(
        left, right, (((0,), (0,)), ((), ())), preferred_element_type=jnp.float32
    )


def right_product(left, right):
    return lax.dot_general(
        left, right, (((1,), (1,)), ((), ())), preferred_element_type=jnp.float32
    )


def split_heads(field):
    sequences = field.shape[0]
    return field.reshape(sequences, LENGTH // BLK, BLK, H, D // H).transpose(0, 3, 1, 2, 4)


def join_heads(field):
    sequences = field.shape[0]
    return field.transpose(0, 2, 3, 1, 4).reshape(sequences, LENGTH, D)


def key_slots(rand_blocks, blocks):
    rows = jnp.arange(1, blocks - 1, dtype=jnp.int32)
    fixed = jnp.stack(
        [jnp.zeros_like(rows), jnp.full_like(rows, blocks - 1), rows - 1, rows, rows + 1], axis=1
    )
    chosen = jnp.transpose(rand_blocks, (0, 2, 1, 3))
    fixed = jnp.broadcast_to(fixed, chosen.shape[:3] + (5,))
    slots = jnp.concatenate([fixed, chosen], axis=3)
    always = rows >= 0
    keep = jnp.stack(
        [always, always, rows - 1 != 0, always, rows + 1 != blocks - 1]
        + [always] * chosen.shape[3],
        axis=1,
    )
    return (slots, keep)


def pick_blocks(heads_field, slots):
    sequences, heads_count, blocks = heads_field.shape[:3]
    flat = heads_field.reshape(sequences, heads_count, blocks, -1)
    taken = jnp.take_along_axis(flat, slots.reshape(sequences, heads_count, -1, 1), axis=2)
    return taken.reshape(sequences, heads_count, slots.shape[2], slots.shape[3] * BLK, -1)


def spread_blocks(grads, slots, blocks):
    sequences, heads_count = slots.shape[:2]
    flat = grads.reshape(sequences, heads_count, slots.shape[2] * slots.shape[3], -1)
    onehot = (
        slots.reshape(sequences, heads_count, -1)[..., None] == jnp.arange(blocks, dtype=jnp.int32)
    ).astype(jnp.float32)
    placed = jnp.einsum(
        "shmb,shmx->shbx",
        onehot,
        flat,
        precision=lax.Precision.HIGHEST,
        preferred_element_type=jnp.float32,
    )
    return placed.reshape(sequences, heads_count, blocks, BLK, -1)


def prepare(query, key, value, rand_blocks):
    blocks = LENGTH // BLK
    scale = (D // H) ** (-0.5)
    sequences = query.shape[0]
    query_heads, key_heads, value_heads = (split_heads(query), split_heads(key), split_heads(value))
    slots, keep = key_slots(rand_blocks, blocks)
    near_keys = pick_blocks(key_heads, slots)
    near_values = pick_blocks(value_heads, slots)
    all_keys = key_heads.reshape(sequences, H, LENGTH, D // H)
    all_values = value_heads.reshape(sequences, H, LENGTH, D // H)
    middle = (
        jnp.einsum(
            "shmqd,shmkd->shmqk",
            query_heads[:, :, 1 : blocks - 1],
            near_keys,
            preferred_element_type=jnp.float32,
        )
        * scale
    )
    middle = jnp.where(jnp.repeat(keep, BLK, axis=1)[:, None, :], middle, NEG)
    end_queries = jnp.stack([query_heads[:, :, 0], query_heads[:, :, blocks - 1]], axis=2)
    ends = (
        jnp.einsum("shgqd,shkd->shgqk", end_queries, all_keys, preferred_element_type=jnp.float32)
        * scale
    )
    return (
        query_heads,
        slots,
        near_keys,
        near_values,
        all_keys,
        all_values,
        middle,
        ends,
        end_queries,
    )


def attend_forward(query, key, value, rand_blocks):
    query_heads, slots, near_keys, near_values, all_keys, all_values, middle, ends, end_queries = (
        prepare(query, key, value, rand_blocks)
    )
    middle_top = jnp.max(middle, axis=-1, keepdims=True)
    middle_exp = jnp.exp(middle - middle_top)
    middle_total = jnp.sum(middle_exp, axis=-1, keepdims=True)
    ends_top = jnp.max(ends, axis=-1, keepdims=True)
    ends_exp = jnp.exp(ends - ends_top)
    ends_total = jnp.sum(ends_exp, axis=-1, keepdims=True)
    middle_weights = (middle_exp / middle_total).astype(jnp.bfloat16)
    ends_weights = (ends_exp / ends_total).astype(jnp.bfloat16)
    middle_context = jnp.einsum(
        "shmqk,shmkd->shmqd", middle_weights, near_values, preferred_element_type=jnp.float32
    )
    ends_context = jnp.einsum(
        "shgqk,shkd->shgqd", ends_weights, all_values, preferred_element_type=jnp.float32
    )
    context = jnp.concatenate(
        [ends_context[:, :, :1], middle_context, ends_context[:, :, 1:]], axis=2
    )
    return (
        join_heads(context),
        (middle_top + jnp.log(middle_total), ends_top + jnp.log(ends_total)),
    )


def attend_backward(query, key, value, rand_blocks, log_totals, context_grad):
    blocks = LENGTH // BLK
    scale = (D // H) ** (-0.5)
    query_heads, slots, near_keys, near_values, all_keys, all_values, middle, ends, end_queries = (
        prepare(query, key, value, rand_blocks)
    )
    middle_weights = jnp.exp(middle - log_totals[0])
    ends_weights = jnp.exp(ends - log_totals[1])
    grad_heads = split_heads(context_grad)
    grad_middle = grad_heads[:, :, 1 : blocks - 1]
    grad_ends = jnp.stack([grad_heads[:, :, 0], grad_heads[:, :, blocks - 1]], axis=2)
    middle_dots = jnp.einsum(
        "shmqd,shmkd->shmqk", grad_middle, near_values, preferred_element_type=jnp.float32
    )
    middle_scores = (
        middle_weights
        * (middle_dots - jnp.sum(middle_dots * middle_weights, axis=-1, keepdims=True))
    ).astype(jnp.bfloat16)
    ends_dots = jnp.einsum(
        "shgqd,shkd->shgqk", grad_ends, all_values, preferred_element_type=jnp.float32
    )
    ends_scores = (
        ends_weights * (ends_dots - jnp.sum(ends_dots * ends_weights, axis=-1, keepdims=True))
    ).astype(jnp.bfloat16)
    query_middle = (
        jnp.einsum(
            "shmqk,shmkd->shmqd", middle_scores, near_keys, preferred_element_type=jnp.float32
        )
        * scale
    )
    query_ends = (
        jnp.einsum("shgqk,shkd->shgqd", ends_scores, all_keys, preferred_element_type=jnp.float32)
        * scale
    )
    near_key_grad = (
        jnp.einsum(
            "shmqk,shmqd->shmkd",
            middle_scores,
            query_heads[:, :, 1 : blocks - 1],
            preferred_element_type=jnp.float32,
        )
        * scale
    )
    near_value_grad = jnp.einsum(
        "shmqk,shmqd->shmkd",
        middle_weights.astype(jnp.bfloat16),
        grad_middle,
        preferred_element_type=jnp.float32,
    )
    all_key_grad = (
        jnp.einsum(
            "shgqk,shgqd->shkd", ends_scores, end_queries, preferred_element_type=jnp.float32
        )
        * scale
    )
    all_value_grad = jnp.einsum(
        "shgqk,shgqd->shkd",
        ends_weights.astype(jnp.bfloat16),
        grad_ends,
        preferred_element_type=jnp.float32,
    )
    query_grad = jnp.concatenate([query_ends[:, :, :1], query_middle, query_ends[:, :, 1:]], axis=2)
    block_shape = query_heads.shape
    key_grad = spread_blocks(near_key_grad, slots, blocks) + all_key_grad.reshape(block_shape)
    value_grad = spread_blocks(near_value_grad, slots, blocks) + all_value_grad.reshape(block_shape)
    return (join_heads(query_grad), join_heads(key_grad), join_heads(value_grad))


def row_features(local):
    return lax.all_gather(local, "row", axis=1, tiled=True)


def row_sum(partial_value):
    return lax.psum_scatter(partial_value, "row", scatter_dimension=1, tiled=True)


def row_totals(first, second):
    return lax.psum((first, second), "row")


def grid_norm(total_in, gain, shift):
    total, squares = row_totals(
        jnp.sum(total_in, axis=1, keepdims=True),
        jnp.sum(total_in * total_in, axis=1, keepdims=True),
    )
    mean = total / D
    inverse = lax.rsqrt(squares / D - mean * mean + EPS)
    unit = (total_in - mean) * inverse
    return (unit * gain + shift, unit, inverse)


def grid_norm_back(grad, unit, inverse, gain):
    scaled = grad * gain
    total, along = row_totals(
        jnp.sum(scaled, axis=1, keepdims=True), jnp.sum(scaled * unit, axis=1, keepdims=True)
    )
    return inverse * (scaled - total / D - unit * (along / D))


def whole_columns(query_part, key_part, value_part, up_part, out_part, down_part):
    return (
        lax.all_gather(query_part, "col", axis=0, tiled=True),
        lax.all_gather(key_part, "col", axis=0, tiled=True),
        lax.all_gather(value_part, "col", axis=0, tiled=True),
        lax.all_gather(up_part, "col", axis=0, tiled=True),
        lax.all_gather(out_part, "col", axis=1, tiled=True),
        lax.all_gather(down_part, "col", axis=1, tiled=True),
    )


def summed_columns(query_part, key_part, value_part, up_part, out_part, down_part):
    return (
        lax.psum_scatter(
            query_part.astype(jnp.bfloat16), "col", scatter_dimension=0, tiled=True
        ).astype(jnp.float32),
        lax.psum_scatter(
            key_part.astype(jnp.bfloat16), "col", scatter_dimension=0, tiled=True
        ).astype(jnp.float32),
        lax.psum_scatter(
            value_part.astype(jnp.bfloat16), "col", scatter_dimension=0, tiled=True
        ).astype(jnp.float32),
        lax.psum_scatter(
            up_part.astype(jnp.bfloat16), "col", scatter_dimension=0, tiled=True
        ).astype(jnp.float32),
        lax.psum_scatter(
            out_part.astype(jnp.bfloat16), "col", scatter_dimension=1, tiled=True
        ).astype(jnp.float32),
        lax.psum_scatter(
            down_part.astype(jnp.bfloat16), "col", scatter_dimension=1, tiled=True
        ).astype(jnp.float32),
    )


def summed_vectors(
    query_bias_grad,
    value_bias_grad,
    out_bias_grad,
    up_bias_grad,
    down_bias_grad,
    gain_first,
    shift_first,
    gain_second,
    shift_second,
):
    return lax.psum(
        (
            query_bias_grad,
            value_bias_grad,
            out_bias_grad,
            up_bias_grad,
            down_bias_grad,
            gain_first,
            shift_first,
            gain_second,
            shift_second,
        ),
        "col",
    )


def column_sums(field):
    return jnp.sum(field.astype(jnp.float32), axis=0)


def gelu_back(before, grad):
    unused, pullback = jax.vjp(lambda inner: jax.nn.gelu(inner, approximate=False), before)
    return pullback(grad)[0]


def grid_layer(
    hidden,
    cotangent,
    rand_blocks,
    w_query,
    w_key,
    w_value,
    w_out,
    w_up,
    w_down,
    query_bias,
    value_bias,
    out_bias,
    up_bias,
    down_bias,
    norm1_gain,
    norm1_shift,
    norm2_gain,
    norm2_shift,
):
    sequences = rand_blocks.shape[0]
    seq_shape = (sequences, LENGTH, D)
    whole_query, whole_key, whole_value, whole_up, whole_out, whole_down = whole_columns(
        w_query, w_key, w_value, w_up, w_out, w_down
    )
    inputs = lax.all_gather(hidden, "row", axis=0, tiled=True)
    feature_width = D // lax.axis_size("row")
    hidden_local = lax.dynamic_slice_in_dim(
        inputs, lax.axis_index("row") * feature_width, feature_width, 1
    )
    query_local = (product(inputs, whole_query) + query_bias).astype(jnp.bfloat16)
    key_local = product(inputs, whole_key).astype(jnp.bfloat16)
    value_local = (product(inputs, whole_value) + value_bias).astype(jnp.bfloat16)
    query_seq, key_seq, value_seq = (
        lax.all_to_all(query_local, "row", split_axis=0, concat_axis=1, tiled=True),
        lax.all_to_all(key_local, "row", split_axis=0, concat_axis=1, tiled=True),
        lax.all_to_all(value_local, "row", split_axis=0, concat_axis=1, tiled=True),
    )
    query_seq, key_seq, value_seq = (
        query_seq.reshape(seq_shape),
        key_seq.reshape(seq_shape),
        value_seq.reshape(seq_shape),
    )
    context, log_totals = attend_forward(query_seq, key_seq, value_seq, rand_blocks)
    context_seq = context.astype(jnp.bfloat16).reshape(sequences * LENGTH, D)
    context_local = lax.all_to_all(context_seq, "row", split_axis=1, concat_axis=0, tiled=True)
    attention = row_sum(product(context_local, whole_out)) + out_bias
    first, first_unit, first_inverse = grid_norm(
        hidden_local.astype(jnp.float32) + attention, norm1_gain, norm1_shift
    )
    first_all = row_features(first.astype(jnp.bfloat16))
    before = product(first_all, whole_up) + up_bias
    activated = jax.nn.gelu(before, approximate=False).astype(jnp.bfloat16)
    branch = row_sum(product(activated, whole_down)) + down_bias
    output, second_unit, second_inverse = grid_norm(first + branch, norm2_gain, norm2_shift)
    cotangent_local = lax.all_to_all(cotangent, "row", split_axis=1, concat_axis=0, tiled=True)
    outer_grad = cotangent_local.astype(jnp.float32)
    grad_second = grid_norm_back(outer_grad, second_unit, second_inverse, norm2_gain)
    gain_second = jnp.sum(outer_grad * second_unit, axis=0)
    shift_second = jnp.sum(outer_grad, axis=0)
    branch_grad = grad_second.astype(jnp.bfloat16)
    down_bias_grad = column_sums(branch_grad)
    branch_all = row_features(branch_grad)
    down_grad = left_product(activated, branch_all)
    before_grad = gelu_back(before, right_product(branch_all, whole_down)).astype(jnp.bfloat16)
    up_bias_grad = column_sums(before_grad)
    up_grad = left_product(first_all, before_grad)
    first_grad = grad_second + row_sum(right_product(before_grad, whole_up))
    gain_first = jnp.sum(first_grad * first_unit, axis=0)
    shift_first = jnp.sum(first_grad, axis=0)
    resid_grad = grid_norm_back(first_grad, first_unit, first_inverse, norm1_gain)
    attention_grad = resid_grad.astype(jnp.bfloat16)
    out_bias_grad = column_sums(attention_grad)
    attention_all = row_features(attention_grad)
    out_grad = left_product(context_local, attention_all)
    context_grad = right_product(attention_all, whole_out).astype(jnp.bfloat16)
    context_grad_seq = lax.all_to_all(context_grad, "row", split_axis=0, concat_axis=1, tiled=True)
    query_grad, key_grad, value_grad = attend_backward(
        query_seq, key_seq, value_seq, rand_blocks, log_totals, context_grad_seq.reshape(seq_shape)
    )
    flat_shape = (sequences * LENGTH, D)
    query_grad_local, key_grad_local, value_grad_local = (
        lax.all_to_all(
            query_grad.astype(jnp.bfloat16).reshape(flat_shape),
            "row",
            split_axis=1,
            concat_axis=0,
            tiled=True,
        ),
        lax.all_to_all(
            key_grad.astype(jnp.bfloat16).reshape(flat_shape),
            "row",
            split_axis=1,
            concat_axis=0,
            tiled=True,
        ),
        lax.all_to_all(
            value_grad.astype(jnp.bfloat16).reshape(flat_shape),
            "row",
            split_axis=1,
            concat_axis=0,
            tiled=True,
        ),
    )
    query_bias_grad = column_sums(query_grad_local)
    value_bias_grad = column_sums(value_grad_local)
    input_part = (
        right_product(query_grad_local, whole_query)
        + right_product(key_grad_local, whole_key)
        + right_product(value_grad_local, whole_value)
    )
    hidden_grad = resid_grad + row_sum(input_part)
    output_rows, hidden_grad_rows = (
        lax.all_to_all(
            output.astype(jnp.bfloat16), "row", split_axis=0, concat_axis=1, tiled=True
        ).astype(output.dtype),
        lax.all_to_all(
            hidden_grad.astype(jnp.bfloat16), "row", split_axis=0, concat_axis=1, tiled=True
        ).astype(hidden_grad.dtype),
    )
    query_weight_grad = left_product(inputs, query_grad_local)
    key_weight_grad = left_product(inputs, key_grad_local)
    value_weight_grad = left_product(inputs, value_grad_local)
    matrices = summed_columns(
        query_weight_grad, key_weight_grad, value_weight_grad, up_grad, out_grad, down_grad
    )
    vectors = summed_vectors(
        query_bias_grad,
        value_bias_grad,
        out_bias_grad,
        up_bias_grad,
        down_bias_grad,
        gain_first,
        shift_first,
        gain_second,
        shift_second,
    )
    return (
        output_rows,
        hidden_grad_rows,
        matrices[0],
        matrices[1],
        matrices[2],
        matrices[4],
        matrices[3],
        matrices[5],
        vectors[0],
        vectors[1],
        vectors[2],
        vectors[3],
        vectors[4],
        vectors[5],
        vectors[6],
        vectors[7],
        vectors[8],
    )


def on_device(
    hidden,
    cotangent,
    rand_blocks,
    w_query,
    w_key,
    w_value,
    w_out,
    w_up,
    w_down,
    query_bias,
    value_bias,
    out_bias,
    up_bias,
    down_bias,
    norm1_gain,
    norm1_shift,
    norm2_gain,
    norm2_shift,
):
    return grid_layer(
        hidden,
        cotangent,
        rand_blocks,
        w_query,
        w_key,
        w_value,
        w_out,
        w_up,
        w_down,
        query_bias,
        value_bias,
        out_bias,
        up_bias,
        down_bias,
        norm1_gain,
        norm1_shift,
        norm2_gain,
        norm2_shift,
    )


def solution(mesh):
    placed = (
        P(("col", "row"), None),
        P(("col", "row"), None),
        P(("col", "row"), None, None, None),
        P("col", "row"),
        P("col", "row"),
        P("col", "row"),
        P("row", "col"),
        P("col", "row"),
        P("row", "col"),
        P("row"),
        P("row"),
        P("row"),
        P("row"),
        P("row"),
        P("row"),
        P("row"),
        P("row"),
        P("row"),
    )
    return jax.shard_map(
        on_device,
        mesh=mesh,
        in_specs=placed,
        out_specs=(
            P(("col", "row"), None),
            P(("col", "row"), None),
            P("col", "row"),
            P("col", "row"),
            P("col", "row"),
            P("row", "col"),
            P("col", "row"),
            P("row", "col"),
            P("row"),
            P("row"),
            P("row"),
            P("row"),
            P("row"),
            P("row"),
            P("row"),
            P("row"),
            P("row"),
        ),
        check_vma=False,
    )
```

profile of v0, /device:TPU:0, one launch (start us, length us, event | category | flops | bytes accessed | tf_op | source)
XLA Modules:
  0.0 1837.7 jit_solution(5926472592006307026)
XLA Ops:
  9.4 25.1 %all_gather.33 = bf16[768,384]{1,0:T(8,128)(2,1)S(1)} all-gather(bf16[48,384]{1,0:T(8,128)(2,1)} %param.25), channel_id=1, replica_groups=mesh['col'=16,'row'=2] {'col'}, dimensions={0}, use_global_device_ids=true | all-gather | bytes 626688 | tf_op jit(solution)/shard_map/all_gather | solution.py:250
  34.5 23.5 %all-gather.7.cloned.1.call-done = bf16[2048,768]{1,0:T(8,128)(2,1)} async-done(((bf16[1024,768]{1,0:T(8,128)(2,1)}), bf16[2048,768]{1,0:T(8,128)(2,1)}) %all-gather.7.cloned.1.call-update) | async-done | bytes 3145744 | tf_op jit(solution)/shard_map/all_gather | solution.py:341
  67.1 23.1 %all_gather.32 = bf16[768,384]{1,0:T(8,128)(2,1)S(1)} all-gather(bf16[48,384]{1,0:T(8,128)(2,1)S(1)} %copy-done.35), channel_id=1, replica_groups=mesh['col'=16,'row'=2] {'col'}, dimensions={0}, use_global_device_ids=true | all-gather | bytes 626688 | tf_op jit(solution)/shard_map/all_gather | solution.py:249
  99.5 19.1 %all_gather.31 = bf16[768,384]{1,0:T(8,128)(2,1)S(1)} all-gather(bf16[48,384]{1,0:T(8,128)(2,1)S(1)} %copy-done.36), channel_id=1, replica_groups=mesh['col'=16,'row'=2] {'col'}, dimensions={0}, use_global_device_ids=true | all-gather | bytes 626688 | tf_op jit(solution)/shard_map/all_gather | solution.py:248
  182.3 53.2 %gather_fusion = bf16[1344,4096]{1,0:T(8,128)(2,1)} fusion(bf16[12,16,4096]{2,1,0:T(8,128)(2,1)S(1)} %reshape.490, s32[1344]{0:T(1024)S(1)} %reshape.492), kind=kCustom, calls=%fused_computation.clone | custom fusion | bytes 22030848 | tf_op jit(solution)/shard_map/jit(take_along_axis)/gather | solution.py:62
  235.6 53.1 %gather_fusion.1 = bf16[1344,4096]{1,0:T(8,128)(2,1)} fusion(bf16[12,16,4096]{2,1,0:T(8,128)(2,1)S(1)} %reshape.496, s32[1344]{0:T(1024)S(1)} %reshape.492), kind=kCustom, calls=%fused_computation.1.clone | custom fusion | bytes 22030848 | tf_op jit(solution)/shard_map/jit(take_along_axis)/gather | solution.py:62
  304.5 30.3 %reshape.445 = bf16[12,14,512,64]{3,2,1,0:T(8,128)(2,1)} reshape(bf16[1,12,112,4096]{3,2,1,0:T(8,128)(2,1)} %get-tuple-element.138) | data formatting | bytes 22020096 | tf_op jit(solution)/shard_map/reshape.15
  334.7 30.4 %reshape.447 = bf16[12,14,512,64]{3,2,1,0:T(8,128)(2,1)} reshape(bf16[1,12,112,4096]{3,2,1,0:T(8,128)(2,1)} %get-tuple-element.139) | data formatting | bytes 22020096 | tf_op jit(solution)/shard_map/reshape.20
  365.1 19.5 %fusion.12 = (f32[12,14,64]{2,1,0:T(8,128)S(1)}, f32[12,14,64,512]{3,2,1,0:T(8,128)}) fusion(pred[14,512]{1,0:T(8,128)(4,1)S(1)} %broadcast_in_dim_reshape.2, bf16[12,14,512,64]{3,2,1,0:T(8,128)(2,1)} %reshape.445, bf16[1,12,16,64,64]{4,3,2,1,0:T(8,128)(2,1)S(1)} %bitcast.271), kind=kOutput, calls=%fused_computation.34 | convolution fusion | flops 721147392 | bytes 35833856 | tf_op jit(solution)/shard_map/shmqd,shmkd->shmqk/dot_general | solution.py:93
  425.2 21.8 %all_gather.34 = bf16[384,768]{0,1:T(8,128)(2,1)} all-gather(bf16[384,48]{0,1:T(8,128)(2,1)S(1)} %copy-done.37), channel_id=1, replica_groups=mesh['col'=16,'row'=2] {'col'}, dimensions={1}, use_global_device_ids=true | all-gather | bytes 626688 | tf_op jit(solution)/shard_map/all_gather | solution.py:252
  454.6 74.4 %reduce-scatter.17.cloned.1.call-done = f32[2048,384]{1,0:T(8,128)} async-done(((f32[2048,768]{1,0:T(8,128)}), f32[2048,384]{1,0:T(8,128)}) %reduce-scatter.17.cloned.1.call-update) | async-done | bytes 3145744 | tf_op jit(solution)/shard_map/reduce_scatter | solution.py:220
  541.4 45.4 %all-gather.9.cloned.1.call-done = bf16[2048,768]{1,0:T(8,128)(2,1)} async-done(((bf16[2048,384]{1,0:T(8,128)(2,1)}), bf16[2048,768]{1,0:T(8,128)(2,1)}) %all-gather.9.cloned.1.call-update) | async-done | bytes 3145744 | tf_op jit(solution)/shard_map/all_gather | solution.py:216
  586.8 35.3 %multiply_convert_fusion.1 = (bf16[2048,1536]{1,0:T(8,128)(2,1)}, f32[2048,1536]{1,0:T(8,128)}, f32[2048,1536]{1,0:T(8,128)}) fusion(f32[1536]{0:T(1024)S(1)} %convert_element_type.247, bf16[2048,768]{1,0:T(8,128)(2,1)} %all-gather.9.cloned.1.call-done, bf16[768,1536]{1,0:T(8,128)(2,1)} %all-gather.11.cloned.1.call-done), kind=kOutput, calls=%fused_computation.14 | convolution fusion | flops 5039456256 | bytes 36968448 | tf_op jit(solution)/shard_map/dot_general | solution.py:17
  648.7 37.3 %all-to-all-done.5 = bf16[1024,2,384]{2,0,1:T(8,128)(2,1)} async-done(((bf16[1024,2,384]{2,0,1:T(8,128)(2,1)}), bf16[1024,2,384]{2,0,1:T(8,128)(2,1)}, u32[]{:S(2)}, u32[]{:S(2)}) %all-to-all-start.5) | async-done | bytes 1572896 | tf_op jit(solution)/shard_map/all_to_all | solution.py:371
  688.7 44.8 %reduce-scatter.19.cloned.1.call-done = f32[2048,384]{1,0:T(8,128)} async-done(((f32[2048,768]{1,0:T(8,128)}), f32[2048,384]{1,0:T(8,128)}) %reduce-scatter.19.cloned.1.call-update) | async-done | bytes 3145744 | tf_op jit(solution)/shard_map/reduce_scatter | solution.py:220
  761.0 45.0 %all-gather.15.cloned.1.call-done = bf16[2048,768]{1,0:T(8,128)(2,1)} async-done(((bf16[2048,384]{1,0:T(8,128)(2,1)}), bf16[2048,768]{1,0:T(8,128)(2,1)}) %all-gather.15.cloned.1.call-update) | async-done | bytes 3145744 | tf_op jit(solution)/shard_map/all_gather | solution.py:216
  833.9 76.6 %reduce-scatter.21.cloned.1.call-done = f32[2048,384]{1,0:T(8,128)} async-done(((f32[2048,768]{1,0:T(8,128)}), f32[2048,384]{1,0:T(8,128)}) %reduce-scatter.21.cloned.1.call-update) | async-done | bytes 3145744 | tf_op jit(solution)/shard_map/reduce_scatter | solution.py:220
  931.2 46.1 %all-gather.17.cloned.1.call-done = bf16[2048,768]{1,0:T(8,128)(2,1)} async-done(((bf16[2048,384]{1,0:T(8,128)(2,1)}), bf16[2048,768]{1,0:T(8,128)(2,1)}) %all-gather.17.cloned.1.call-update) | async-done | bytes 3145744 | tf_op jit(solution)/shard_map/all_gather | solution.py:216
  986.6 19.1 %all-to-all-done.6 = bf16[2,1024,384]{1,2,0:T(8,128)(2,1)S(1)} async-done(((bf16[2,1024,384]{1,2,0:T(8,128)(2,1)}), bf16[2,1024,384]{1,2,0:T(8,128)(2,1)S(1)}, u32[]{:S(2)}, u32[]{:S(2)}) %all-to-all-start.6) | async-done | bytes 1572896 | tf_op jit(solution)/shard_map/all_to_all | solution.py:392
  1025.2 23.9 %multiply_reduce_fusion = (f32[12,14,64]{2,1,0:T(8,128)S(1)}, f32[12,14,64,512]{3,2,1,0:T(8,128)}) fusion(f32[12,14,64]{2,1,0:T(8,128)S(1)} %log_add_fusion, f32[12,14,64,512]{3,2,1,0:T(8,128)} %get-tuple-element.143, pred[14,512]{1,0:T(8,128)(4,1)S(1)} %copy-done.23, bf16[12,14,512,64]{3,2,1,0:T(8,128)(2,1)} %reshape.447, ...), kind=kOutput, calls=%fused_computation.3 | convolution fusion | flops 732157440 | bytes 68905984 | tf_op jit(solution)/shard_map/shmqd,shmkd->shmqk/dot_general | solution.py:158
  1049.0 18.8 %multiply_convert_fusion = bf16[12,14,64,512]{3,2,1,0:T(8,128)(2,1)} fusion(f32[12,14,64,512]{3,2,1,0:T(8,128)} %get-tuple-element.148, f32[12,14,64]{2,1,0:T(8,128)S(1)} %get-tuple-element.147, f32[12,14,64]{2,1,0:T(8,128)S(1)} %log_add_fusion, f32[12,14,64,512]{3,2,1,0:T(8,128)} %get-tuple-element.143, pred[14,512]{1,0:T(8,128)(4,1)S(1)} %copy-done.23), kind=kLoop, calls=%fused_computation.2 | loop fusion | flops 33030144 | bytes 55143424 | tf_op jit(solution)/shard_map/convert_element_type | solution.py:164
  1095.5 24.2 %fusion.8 = f32[12,14,512,64]{3,2,1,0:T(8,128)} fusion(f32[12,14,64]{2,1,0:T(8,128)S(1)} %log_add_fusion, f32[12,14,64,512]{3,2,1,0:T(8,128)} %get-tuple-element.143, pred[14,512]{1,0:T(8,128)(4,1)S(1)} %copy-done.23, bf16[1,12,16,64,64]{4,3,2,1,0:T(8,128)(2,1)} %bitcast.277), kind=kOutput, calls=%fused_computation.28 | convolution fusion | flops 726663168 | bytes 46842880 | tf_op jit(solution)/shard_map/shmqk,shmqd->shmkd/dot_general | solution.py:190
  1145.3 35.9 %reshape.453 = f32[12,112,4096]{2,1,0:T(8,128)} reshape(f32[12,14,512,64]{3,2,1,0:T(8,128)} %fusion.8) | data formatting | bytes 44040192 | tf_op jit(solution)/shard_map/reshape.106
  1218.9 29.8 %copy.136 = f32[12,14,512,64]{3,2,1,0:T(8,128)} copy(f32[12,14,512,64]{2,3,1,0:T(8,128)} %broadcast_multiply_fusion) | data formatting | bytes 44040192 | tf_op jit(solution)/shard_map/mul | solution.py:182
  1248.7 35.8 %reshape.450 = f32[12,112,4096]{2,1,0:T(8,128)} reshape(f32[12,14,512,64]{3,2,1,0:T(8,128)} %copy.136) | data formatting | bytes 44040192 | tf_op jit(solution)/shard_map/reshape.78
  1420.4 44.2 %reduce-scatter.23.cloned.1.call-done = f32[2048,384]{1,0:T(8,128)} async-done(((f32[2048,768]{1,0:T(8,128)}), f32[2048,384]{1,0:T(8,128)}) %reduce-scatter.23.cloned.1.call-update) | async-done | bytes 3145744 | tf_op jit(solution)/shard_map/reduce_scatter | solution.py:220
  1473.5 58.1 %reduce-scatter.29.cloned.1.call-done = bf16[1536,48]{0,1:T(8,128)(2,1)} async-done(((bf16[1536,768]{0,1:T(8,128)(2,1)}), bf16[1536,48]{0,1:T(8,128)(2,1)}) %reduce-scatter.29.cloned.1.call-update) | async-done | bytes 147472 | tf_op jit(solution)/shard_map/reduce_scatter | solution.py:274
  1533.2 65.0 %reduce-scatter.27.cloned.1.call-done = bf16[48,1536]{1,0:T(8,128)(2,1)} async-done(((bf16[768,1536]{1,0:T(8,128)(2,1)}), bf16[48,1536]{1,0:T(8,128)(2,1)}) %reduce-scatter.27.cloned.1.call-update) | async-done | bytes 147472 | tf_op jit(solution)/shard_map/reduce_scatter | solution.py:268
  1603.4 51.4 %reduce-scatter.25.cloned.1.call-done = bf16[384,48]{0,1:T(8,128)(2,1)} async-done(((bf16[384,768]{0,1:T(8,128)(2,1)}), bf16[384,48]{0,1:T(8,128)(2,1)}) %reduce-scatter.25.cloned.1.call-update) | async-done | bytes 36880 | tf_op jit(solution)/shard_map/reduce_scatter | solution.py:271
  1656.9 57.7 %all-reduce = (f32[384]{0:T(512)}, f32[384]{0:T(512)}, f32[384]{0:T(512)}, f32[1536]{0:T(1024)}, f32[384]{0:T(512)}, /*index=5*/f32[384]{0:T(512)}, f32[384]{0:T(512)}, f32[384]{0:T(512)}, f32[384]{0:T(512)}) all-reduce(f32[384]{0:T(512)S(1)} %convert_reduce_fusion.5, ...), channel_id=1, replica_groups=mesh['col'=16,'row'=2] {'col'}, use_global_device_ids=true, to_apply=%region_33.35 | all-reduce | flops 4608 | bytes 36864 | tf_op jit(solution)/shard_map/psum | solution.py:291
  1716.2 52.0 %reduce-scatter.35.cloned.1.call-done = bf16[48,384]{1,0:T(8,128)(2,1)} async-done(((bf16[768,384]{1,0:T(8,128)(2,1)}), bf16[48,384]{1,0:T(8,128)(2,1)}) %reduce-scatter.35.cloned.1.call-update) | async-done | bytes 36880
  1769.9 55.1 %reduce-scatter.33.cloned.1.call-done = bf16[48,384]{1,0:T(8,128)(2,1)} async-done(((bf16[768,384]{1,0:T(8,128)(2,1)}), bf16[48,384]{1,0:T(8,128)(2,1)}) %reduce-scatter.33.cloned.1.call-update) | async-done | bytes 36880
  (320 shorter events, 545.9 us)
Async XLA Ops:
  8.0 50.0 %all-gather.7.cloned.1.call-start = ((), (), s32[]{:S(2)}) async-start(), calls=%async_computation.21 | async-start | bytes 4718592 | tf_op jit(solution)/shard_map/all_gather | solution.py:341
  63.4 32.4 %all-to-all-start.2 = ((bf16[2,1024,384]{1,2,0:T(8,128)(2,1)}), bf16[2,1024,384]{1,2,0:T(8,128)(2,1)S(1)}, u32[]{:S(2)}, u32[]{:S(2)}) async-start(bf16[2,1024,384]{1,2,0:T(8,128)(2,1)} %copy.119), calls=%async_computation.2 | async-start | bytes 3145728 | tf_op jit(solution)/shard_map/all_to_all | solution.py:352
  95.8 30.5 %all-to-all-start.1 = ((bf16[2,1024,384]{1,2,0:T(8,128)(2,1)}), bf16[2,1024,384]{1,2,0:T(8,128)(2,1)S(1)}, u32[]{:S(2)}, u32[]{:S(2)}) async-start(bf16[2,1024,384]{1,2,0:T(8,128)(2,1)} %copy.118), calls=%async_computation.1 | async-start | bytes 3145728 | tf_op jit(solution)/shard_map/all_to_all | solution.py:351
  126.3 28.5 %all-to-all-start = ((bf16[2,1024,384]{1,2,0:T(8,128)(2,1)}), bf16[2,1024,384]{1,2,0:T(8,128)(2,1)}, u32[]{:S(2)}, u32[]{:S(2)}) async-start(bf16[2,1024,384]{1,2,0:T(8,128)(2,1)} %copy.116), calls=%async_computation | async-start | bytes 3145728 | tf_op jit(solution)/shard_map/all_to_all | solution.py:350
  131.4 264.1 %copy-start.22 = (pred[14,512]{1,0:T(8,128)(4,1)}, pred[14,512]{1,0:T(8,128)(4,1)S(1)}, u32[]{:S(2)}) copy-start(pred[14,512]{1,0:T(8,128)(4,1)S(1)} %broadcast_in_dim_reshape.2) | copy-start | bytes 21508
  421.5 25.5 %all-to-all-start.3 = ((bf16[1024,2,384]{0,2,1:T(8,128)(2,1)}), bf16[1024,2,384]{0,2,1:T(8,128)(2,1)S(1)}, u32[]{:S(2)}, u32[]{:S(2)}) async-start(bf16[1024,2,384]{0,2,1:T(8,128)(2,1)} %convert_element_type.242), calls=%async_computation.3 | async-start | bytes 3145728 | tf_op jit(solution)/shard_map/all_to_all | solution.py:361
  425.1 103.8 %reduce-scatter.17.cloned.1.call-start = ((), (), s32[]{:S(2)}) async-start(), calls=%async_computation.22 | async-start | bytes 9437184 | tf_op jit(solution)/shard_map/reduce_scatter | solution.py:220
  453.9 87.5 %all-gather.11.cloned.1.call-start = ((), (), s32[]{:S(2)}) async-start(), calls=%async_computation.24 | async-start | bytes 2506752 | tf_op jit(solution)/shard_map/all_gather | solution.py:251
  454.5 132.3 %all-gather.9.cloned.1.call-start = ((), (), s32[]{:S(2)}) async-start(), calls=%async_computation.23 | async-start | bytes 4718592 | tf_op jit(solution)/shard_map/all_gather | solution.py:216
  540.7 90.9 %all-gather.13.cloned.1.call-start = ((), (), s32[]{:S(2)}) async-start(), calls=%async_computation.25 | async-start | bytes 2506752 | tf_op jit(solution)/shard_map/all_gather | solution.py:253
  541.3 192.2 %reduce-scatter.19.cloned.1.call-start = ((), (), s32[]{:S(2)}) async-start(), calls=%async_computation.26 | async-start | bytes 9437184 | tf_op jit(solution)/shard_map/reduce_scatter | solution.py:220
  643.8 42.1 %all-to-all-start.5 = ((bf16[1024,2,384]{2,0,1:T(8,128)(2,1)}), bf16[1024,2,384]{2,0,1:T(8,128)(2,1)}, u32[]{:S(2)}, u32[]{:S(2)}) async-start(bf16[1024,2,384]{2,0,1:T(8,128)(2,1)} %bitcast.293), calls=%async_computation.7 | async-start | bytes 3145728 | tf_op jit(solution)/shard_map/all_to_all | solution.py:371
  648.6 157.4 %all-gather.15.cloned.1.call-start = ((), (), s32[]{:S(2)}) async-start(), calls=%async_computation.27 | async-start | bytes 4718592 | tf_op jit(solution)/shard_map/all_gather | solution.py:216
  761.0 149.5 %reduce-scatter.21.cloned.1.call-start = ((), (), s32[]{:S(2)}) async-start(), calls=%async_computation.28 | async-start | bytes 9437184 | tf_op jit(solution)/shard_map/reduce_scatter | solution.py:220
  833.2 144.0 %all-gather.17.cloned.1.call-start = ((), (), s32[]{:S(2)}) async-start(), calls=%async_computation.29 | async-start | bytes 4718592 | tf_op jit(solution)/shard_map/all_gather | solution.py:216
  982.7 22.9 %all-to-all-start.6 = ((bf16[2,1024,384]{1,2,0:T(8,128)(2,1)}), bf16[2,1024,384]{1,2,0:T(8,128)(2,1)S(1)}, u32[]{:S(2)}, u32[]{:S(2)}) async-start(bf16[2,1024,384]{1,2,0:T(8,128)(2,1)} %copy.129), calls=%async_computation.9 | async-start | bytes 3145728 | tf_op jit(solution)/shard_map/all_to_all | solution.py:392
  1141.6 155.1 %all-to-all-start.7 = ((bf16[1024,2,384]{0,2,1:T(8,128)(2,1)}), bf16[1024,2,384]{0,2,1:T(8,128)(2,1)S(1)}, u32[]{:S(2)}, u32[]{:S(2)}) async-start(bf16[1024,2,384]{0,2,1:T(8,128)(2,1)} %convert_element_type.267), calls=%async_computation.10 | async-start | bytes 3145728 | tf_op jit(solution)/shard_map/all_to_all | solution.py:398
  1296.7 39.6 %all-to-all-start.9 = ((bf16[1024,2,384]{0,2,1:T(8,128)(2,1)}), bf16[1024,2,384]{0,2,1:T(8,128)(2,1)S(1)}, u32[]{:S(2)}, u32[]{:S(2)}) async-start(bf16[1024,2,384]{0,2,1:T(8,128)(2,1)} %convert_element_type.275), calls=%async_computation.12 | async-start | bytes 3145728 | tf_op jit(solution)/shard_map/all_to_all | solution.py:412
  1336.2 23.1 %all-to-all-start.8 = ((bf16[1024,2,384]{0,2,1:T(8,128)(2,1)}), bf16[1024,2,384]{0,2,1:T(8,128)(2,1)}, u32[]{:S(2)}, u32[]{:S(2)}) async-start(bf16[1024,2,384]{0,2,1:T(8,128)(2,1)} %convert_element_type.270), calls=%async_computation.11 | async-start | bytes 3145728 | tf_op jit(solution)/shard_map/all_to_all | solution.py:405
  1340.8 123.7 %reduce-scatter.23.cloned.1.call-start = ((), (), s32[]{:S(2)}) async-start(), calls=%async_computation.30 | async-start | bytes 9437184 | tf_op jit(solution)/shard_map/reduce_scatter | solution.py:220
  1370.5 161.1 %reduce-scatter.29.cloned.1.call-start = ((), (), s32[]{:S(2)}) async-start(), calls=%async_computation.33 | async-start | bytes 2506752 | tf_op jit(solution)/shard_map/reduce_scatter | solution.py:274
  1380.2 218.0 %reduce-scatter.27.cloned.1.call-start = ((), (), s32[]{:S(2)}) async-start(), calls=%async_computation.32 | async-start | bytes 2506752 | tf_op jit(solution)/shard_map/reduce_scatter | solution.py:268
  1389.8 265.1 %reduce-scatter.25.cloned.1.call-start = ((), (), s32[]{:S(2)}) async-start(), calls=%async_computation.31 | async-start | bytes 626688 | tf_op jit(solution)/shard_map/reduce_scatter | solution.py:271
  1394.9 319.7 %reduce-scatter.31.cloned.1.call-start = ((), (), s32[]{:S(2)}) async-start(), calls=%async_computation.34 | async-start | bytes 626688
  1401.7 366.5 %reduce-scatter.35.cloned.1.call-start = ((), (), s32[]{:S(2)}) async-start(), calls=%async_computation.36 | async-start | bytes 626688
  1408.6 60.3 %all-to-all-start.4 = ((bf16[2,1024,384]{2,1,0:T(8,128)(2,1)}), bf16[2,1024,384]{2,1,0:T(8,128)(2,1)}, u32[]{:S(2)}, u32[]{:S(2)}) async-start(bf16[2,1024,384]{2,1,0:T(8,128)(2,1)} %bitcast.298), calls=%async_computation.6 | async-start | bytes 3145728 | tf_op jit(solution)/shard_map/all_to_all | solution.py:429
  1413.2 411.8 %reduce-scatter.33.cloned.1.call-start = ((), (), s32[]{:S(2)}) async-start(), calls=%async_computation.35 | async-start | bytes 626688
  1468.9 357.7 %all-to-all-start.10 = ((bf16[2,1024,384]{2,1,0:T(8,128)(2,1)}), bf16[2,1024,384]{2,1,0:T(8,128)(2,1)}, u32[]{:S(2)}, u32[]{:S(2)}) async-start(bf16[2,1024,384]{2,1,0:T(8,128)(2,1)} %bitcast.297), calls=%async_computation.14 | async-start | bytes 3145728 | tf_op jit(solution)/shard_map/all_to_all | solution.py:432
  1603.4 53.5 %copy-start.42 = (f32[384]{0:T(512)S(1)}, f32[384]{0:T(512)}, u32[]{:S(2)}) copy-start(f32[384]{0:T(512)} %get-tuple-element.117) | copy-start | bytes 4612
  1603.4 53.5 %copy-start.44 = (f32[1536]{0:T(1024)S(1)}, f32[1536]{0:T(1024)}, u32[]{:S(2)}) copy-start(f32[1536]{0:T(1024)} %get-tuple-element.149) | copy-start | bytes 18436
  1603.4 53.5 %copy-start.45 = (f32[384]{0:T(512)S(1)}, f32[384]{0:T(512)}, u32[]{:S(2)}) copy-start(f32[384]{0:T(512)} %get-tuple-element.86) | copy-start | bytes 4612
  1603.4 53.5 %copy-start.46 = (f32[384]{0:T(512)S(1)}, f32[384]{0:T(512)}, u32[]{:S(2)}) copy-start(f32[384]{0:T(512)} %get-tuple-element.91) | copy-start | bytes 4612
  (56 other events, 604.8 us)
Sparse Core Ops, SparseCore 0:
  10.4 47.6 all-gather.6
  454.0 74.8 reduce-scatter.16
  761.1 44.8 all-gather.14
  833.3 77.1 reduce-scatter.20
Sparse Core Ops, SparseCore 1:
  456.7 40.1 all-gather.10
  540.8 45.9 all-gather.8
  588.9 42.6 all-gather.12
  641.1 92.3 reduce-scatter.18
  931.2 46.0 all-gather.16
  1370.6 93.9 reduce-scatter.22
  1468.2 63.4 reduce-scatter.28
  1535.8 62.4 reduce-scatter.26
  1601.7 53.1 reduce-scatter.24
  1658.4 53.1 reduce-scatter.30
  1715.1 53.1 reduce-scatter.34
  1771.8 53.1 reduce-scatter.32
where the time goes:
time: 1850 us; the launch traced here: 1840 us
  waiting for transfers between devices  759 us (41%)
  local copies, waits for them, and re-layouts  426 us (23%)
  matrix products  299 us (16%)
  blocking collectives  176 us (10%)
  other arithmetic  115 us (6%)
  starting transfers between devices  46.3 us (3%)
    reduce_scatter x4, waiting for transfers between devices, row_sum(): lax.psum_scatter(partial_value, 'row', scatter_dimension=1, tiled=True)  240 us
    another operation x8, local copies, waits for them, and re-layouts  139 us
    all_gather x3, waiting for transfers between devices, row_features(): return lax.all_gather(local, 'row', axis=1, tiled=True)  136 us
    unnamed x19, waiting for transfers between devices  109 us
    gather x3, local copies, waits for them, and re-layouts, pick_blocks(): jnp.take_along_axis(flat, slots.reshape(sequences, heads_count, -1, 1), a...  106 us
    reduce_scatter x1, waiting for transfers between devices, summed_columns(): lax.psum_scatter(up_part.astype(jnp.bfloat16), 'col', scatter_dimension=0...  65 us
    dot_general x6, matrix products, product(): return jnp.dot(left, right, preferred_element_type=jnp.float32)  63.4 us
    reduce_scatter x1, waiting for transfers between devices, summed_columns(): lax.psum_scatter(down_part.astype(jnp.bfloat16), 'col', scatter_dimension...  58.1 us
  transfers between devices with their start and end apart: 27, of which 17 were waited for; matrix products, arithmetic and copies ran while one was open for 19% of the time, Pallas kernels for 0%

commit v1 on v0

v1 whole, which is shorter than its diff:
```python
import functools

import jax
import jax.numpy as jnp
from jax import lax
from jax.experimental import pallas as pl
from jax.experimental.pallas import tpu as pltpu
from jax.sharding import PartitionSpec as P

D = 768
H = 12
FF = 3072
BLK = 64
LENGTH = 1024
BLOCKS = LENGTH // BLK
HD = D // H
RAND = 3
EPS = 1e-12
NEG = -1e30
VMEM_BYTES = 64 * 1000 * 1000

HALF = D // 2
FHALF = FF // 2
QKV_W = 3 * HALF
REST_W = HALF + 2 * FHALF
VEC_W = 8 * HALF + FHALF
V_QB, V_VB, V_OB, V_UB = 0, HALF, 2 * HALF, 3 * HALF
V_DB = V_UB + FHALF
V_G1, V_S1, V_G2, V_S2 = V_DB + HALF, V_DB + 2 * HALF, V_DB + 3 * HALF, V_DB + 4 * HALF

f32 = jnp.float32
bf16 = jnp.bfloat16


def dot(a, b):
    return jnp.dot(a, b, preferred_element_type=f32)


def dot_nt(a, b):
    return lax.dot_general(a, b, (((1,), (1,)), ((), ())), preferred_element_type=f32)


def dot_tn(a, b):
    return lax.dot_general(a, b, (((0,), (0,)), ((), ())), preferred_element_type=f32)


def params(**kw):
    return pltpu.CompilerParams(vmem_limit_bytes=VMEM_BYTES, **kw)


def qkv_kernel(x_ref, w_ref, vec_ref, q_ref, k_ref, v_ref):
    r = pl.program_id(0)
    j = pl.program_id(1)
    acc = dot(x_ref[...], w_ref[0])
    vec = vec_ref[0]

    @pl.when(j == 0)
    def _():
        q_ref[...] = ((acc + vec[:, V_QB : V_QB + HALF]).astype(bf16).astype(f32) * 0.125).astype(bf16)

    @pl.when(j == 1)
    def _():
        k_ref[...] = acc.astype(bf16)

    @pl.when(j == 2)
    def _():
        v_ref[...] = (acc + vec[:, V_VB : V_VB + HALF]).astype(bf16)


def qkv(x, w, vec):
    out = jax.ShapeDtypeStruct((LENGTH, D), bf16)
    col = pl.BlockSpec((LENGTH, HALF), lambda r, j: (0, r))
    return pl.pallas_call(
        qkv_kernel,
        grid=(2, 3),
        in_specs=[
            pl.BlockSpec((LENGTH, D), lambda r, j: (0, 0)),
            pl.BlockSpec((1, D, HALF), lambda r, j: (r, 0, j)),
            pl.BlockSpec((1, 1, VEC_W), lambda r, j: (r, 0, 0)),
        ],
        out_specs=[col, col, col],
        out_shape=[out, out, out],
        compiler_params=params(),
        name="qkv",
    )(x, w, vec)


def softmax_bf16(s):
    top = jnp.max(s, axis=-1, keepdims=True)
    e = jnp.exp(s - top)
    total = jnp.sum(e, axis=-1, keepdims=True)
    return (e * (1.0 / total)).astype(bf16)


def head_mask(a, rows):
    lane = lax.broadcasted_iota(jnp.int32, (rows, 2 * HD), 1)
    return (lane < HD) if a == 0 else (lane >= HD)


def only_head(a, x):
    return jnp.where(head_mask(a, x.shape[0]), x, jnp.zeros_like(x))


def key_rows(ref, rand_ref, head, i):
    near = ref[pl.ds(pl.multiple_of((i - 1) * BLK, BLK), 3 * BLK), :]
    parts = [ref[0:BLK, :], ref[LENGTH - BLK :, :], near]
    for n in range(RAND):
        b = rand_ref[((i - 1) * H + head) * RAND + n]
        parts.append(ref[pl.ds(pl.multiple_of(b * BLK, BLK), BLK), :])
    return jnp.concatenate(parts, axis=0)


def edge_mask(s, i):
    col = lax.broadcasted_iota(jnp.int32, s.shape, 1)
    start = jnp.where(i == 1, 2 * BLK, jnp.where(i == BLOCKS - 2, 4 * BLK, -BLK))
    return jnp.where((col >= start) & (col < start + BLK), NEG, s)


def attend_kernel(rand_ref, q_ref, k_ref, v_ref, c_ref, pm_ref, pe_ref):
    pair = pl.program_id(0)
    kall = k_ref[...]
    vall = v_ref[...]
    qe = jnp.concatenate([q_ref[0:BLK, :], q_ref[LENGTH - BLK :, :]], axis=0)
    ends = []
    for a in range(2):
        p = softmax_bf16(dot_nt(only_head(a, qe), kall))
        pe_ref[a] = p
        ends.append(dot(p, vall))
    ce = jnp.where(head_mask(0, 2 * BLK), ends[0], ends[1]).astype(bf16)
    c_ref[0:BLK, :] = ce[:BLK]
    c_ref[LENGTH - BLK :, :] = ce[BLK:]

    def block(i):
        row = pl.multiple_of(i * BLK, BLK)
        qi = q_ref[pl.ds(row, BLK), :]
        outs = []
        for a in range(2):
            kk = key_rows(k_ref, rand_ref, pair * 2 + a, i)
            vv = key_rows(v_ref, rand_ref, pair * 2 + a, i)
            p = softmax_bf16(edge_mask(dot_nt(only_head(a, qi), kk), i))
            pm_ref[a, i - 1] = p
            outs.append(dot(p, vv))
        c_ref[pl.ds(row, BLK), :] = jnp.where(head_mask(0, BLK), outs[0], outs[1]).astype(bf16)

    @pl.loop(0, (BLOCKS - 2) // 2)
    def _(n):
        block(1 + 2 * n)
        block(2 + 2 * n)


def attend(q, k, v, rand):
    pair = pl.BlockSpec((LENGTH, 2 * HD), lambda h, r: (0, h))
    return pl.pallas_call(
        attend_kernel,
        grid_spec=pltpu.PrefetchScalarGridSpec(
            num_scalar_prefetch=1,
            grid=(H // 2,),
            in_specs=[pair, pair, pair],
            out_specs=[
                pair,
                pl.BlockSpec((2, BLOCKS - 2, BLK, 8 * BLK), lambda h, r: (h, 0, 0, 0)),
                pl.BlockSpec((2, 2 * BLK, LENGTH), lambda h, r: (h, 0, 0)),
            ],
        ),
        out_shape=[
            jax.ShapeDtypeStruct((LENGTH, D), bf16),
            jax.ShapeDtypeStruct((H, BLOCKS - 2, BLK, 8 * BLK), bf16),
            jax.ShapeDtypeStruct((H, 2 * BLK, LENGTH), bf16),
        ],
        compiler_params=params(),
        name="attend",
    )(rand, q, k, v)


def score_grad(p, dots):
    pf = p.astype(f32)
    along = jnp.sum(dots * pf, axis=-1, keepdims=True)
    return (pf * (dots - along)).astype(bf16)


def attend_back_kernel(
    rand_ref, q_ref, k_ref, v_ref, d_ref, pm_ref, pe_ref, dq_ref, dk_ref, dv_ref, dk_s, dv_s
):
    pair = pl.program_id(0)
    kall = k_ref[...]
    vall = v_ref[...]
    qe = jnp.concatenate([q_ref[0:BLK, :], q_ref[LENGTH - BLK :, :]], axis=0)
    de = jnp.concatenate([d_ref[0:BLK, :], d_ref[LENGTH - BLK :, :]], axis=0)
    dss, dqs = [], []
    for a in range(2):
        ds = score_grad(pe_ref[a], dot_nt(only_head(a, de), vall))
        dss.append(ds)
        dqs.append(dot(ds, kall))
    dqe = (jnp.where(head_mask(0, 2 * BLK), dqs[0], dqs[1]) * 0.125).astype(bf16)
    dq_ref[0:BLK, :] = dqe[:BLK]
    dq_ref[LENGTH - BLK :, :] = dqe[BLK:]
    q2 = jnp.concatenate([only_head(0, qe), only_head(1, qe)], axis=0)
    d2 = jnp.concatenate([only_head(0, de), only_head(1, de)], axis=0)
    dk_s[...] = dot_tn(jnp.concatenate(dss, axis=0), q2)
    dv_s[...] = dot_tn(jnp.concatenate([pe_ref[0], pe_ref[1]], axis=0), d2)

    def block(i):
        row = pl.multiple_of(i * BLK, BLK)
        qi = q_ref[pl.ds(row, BLK), :]
        di = d_ref[pl.ds(row, BLK), :]
        dss, dqs, ps, qm, dm = [], [], [], [], []
        for a in range(2):
            kk = key_rows(k_ref, rand_ref, pair * 2 + a, i)
            vv = key_rows(v_ref, rand_ref, pair * 2 + a, i)
            p = pm_ref[a, i - 1]
            dm.append(only_head(a, di))
            qm.append(only_head(a, qi))
            ds = score_grad(p, dot_nt(dm[a], vv))
            ps.append(p)
            dss.append(ds)
            dqs.append(dot(ds, kk))
        dq_ref[pl.ds(row, BLK), :] = (
            jnp.where(head_mask(0, BLK), dqs[0], dqs[1]) * 0.125
        ).astype(bf16)
        q2 = jnp.concatenate(qm, axis=0)
        d2 = jnp.concatenate(dm, axis=0)
        fixed = 5 * BLK
        for acc, left, right, each in ((dk_s, dss, q2, qm), (dv_s, ps, d2, dm)):
            both = dot_tn(jnp.concatenate([x[:, :fixed] for x in left], axis=0), right)
            acc[0:BLK, :] += both[0:BLK]
            acc[LENGTH - BLK :, :] += both[BLK : 2 * BLK]
            acc[pl.ds(pl.multiple_of((i - 1) * BLK, BLK), 3 * BLK), :] += both[2 * BLK :]
            for a in range(2):
                own = dot_tn(left[a][:, fixed:], each[a])
                for n in range(RAND):
                    b = rand_ref[((i - 1) * H + pair * 2 + a) * RAND + n]
                    acc[pl.ds(pl.multiple_of(b * BLK, BLK), BLK), :] += own[n * BLK : (n + 1) * BLK]

    @pl.loop(1, BLOCKS - 1)
    def _(i):
        block(i)

    dk_ref[...] = dk_s[...].astype(bf16)
    dv_ref[...] = dv_s[...].astype(bf16)


def attend_back(q, k, v, d, pm, pe, rand):
    pair = pl.BlockSpec((LENGTH, 2 * HD), lambda h, r: (0, h))
    out = jax.ShapeDtypeStruct((LENGTH, D), bf16)
    return pl.pallas_call(
        attend_back_kernel,
        grid_spec=pltpu.PrefetchScalarGridSpec(
            num_scalar_prefetch=1,
            grid=(H // 2,),
            in_specs=[
                pair,
                pair,
                pair,
                pair,
                pl.BlockSpec((2, BLOCKS - 2, BLK, 8 * BLK), lambda h, r: (h, 0, 0, 0)),
                pl.BlockSpec((2, 2 * BLK, LENGTH), lambda h, r: (h, 0, 0)),
            ],
            out_specs=[pair, pair, pair],
            scratch_shapes=[
                pltpu.VMEM((LENGTH, 2 * HD), f32),
                pltpu.VMEM((LENGTH, 2 * HD), f32),
            ],
        ),
        out_shape=[out, out, out],
        compiler_params=params(),
        name="attend_back",
    )(rand, q, k, v, d, pm, pe)


TOK = 256
TSTEPS = LENGTH // TOK
FC = 768
TILES = REST_W // HALF


def gelu_parts(x):
    z = jnp.abs(x) * 0.7071067811865476
    t = 1.0 / (1.0 + 0.5 * z)
    poly = 0.17087277
    for c in (
        -0.82215223,
        1.48851587,
        -1.13520398,
        0.27886807,
        -0.18628806,
        0.09678418,
        0.37409196,
        1.00002368,
        -1.26551223,
    ):
        poly = poly * t + c
    tail = 0.5 * t * jnp.exp(poly - z * z)
    cdf = jnp.where(x >= 0, 1.0 - tail, tail)
    pdf = jnp.exp(-0.5 * x * x) * 0.3989422804014327
    return cdf, pdf


def norm(z, gain, shift):
    mean = jnp.mean(z, axis=1, keepdims=True)
    cen = z - mean
    var = jnp.mean(cen * cen, axis=1, keepdims=True)
    inv = lax.rsqrt(var + EPS)
    unit = cen * inv
    return unit * gain + shift, unit, inv


def norm_back(grad, unit, inv, gain):
    g = grad * gain
    return inv * (
        g - jnp.mean(g, axis=1, keepdims=True) - unit * jnp.mean(g * unit, axis=1, keepdims=True)
    )


def mid_kernel(
    ctx_ref,
    hid_ref,
    cot_ref,
    w_ref,
    vec_ref,
    out_ref,
    resid_ref,
    dctx_ref,
    dw_ref,
    vs_ref,
    act_s,
    bg_s,
    dg_s,
    flT_s,
    brT_s,
    agT_s,
):
    step = pl.program_id(0)

    def vec(off, width=HALF):
        return jnp.concatenate(
            [vec_ref[0, :, off : off + width], vec_ref[1, :, off : off + width]], axis=1
        )

    def add_vec(off, value, width=HALF):
        total = jnp.sum(value, axis=0, keepdims=True)
        vs_ref[0, :, off : off + width] += total[:, :width]
        vs_ref[1, :, off : off + width] += total[:, width:]

    @pl.when(step == 0)
    def _():
        vs_ref[...] = jnp.zeros_like(vs_ref)

    @pl.when(step < TSTEPS)
    def _():
        rows = pl.ds(pl.multiple_of(step * TOK, TOK), TOK)
        ctx = ctx_ref[rows, :]
        att = dot_nt(ctx[:, :HALF], w_ref[0, :, :HALF]) + dot_nt(
            ctx[:, HALF:], w_ref[1, :, :HALF]
        )
        z = hid_ref[...].astype(f32) + (att + vec(V_OB))
        gain1 = vec(V_G1)
        first, unit1, inv1 = norm(z, gain1, vec(V_S1))
        low = first.astype(bf16)
        flT_s[:, rows] = low.T
        branch = None
        for r in range(2):
            for c in range(0, FHALF, FC):
                at = r * FHALF + c
                before = (
                    dot(low, w_ref[r, :, HALF + c : HALF + c + FC])
                    + vec_ref[r, :, V_UB + c : V_UB + c + FC]
                )
                cdf, pdf = gelu_parts(before)
                act = (before * cdf).astype(bf16)
                act_s[rows, at : at + FC] = act
                dg_s[:, at : at + FC] = cdf + before * pdf
                part = dot_nt(act, w_ref[r, :, HALF + FHALF + c : HALF + FHALF + c + FC])
                branch = part if branch is None else branch + part
        gain2 = vec(V_G2)
        output, unit2, inv2 = norm(first + (branch + vec(V_DB)), gain2, vec(V_S2))
        out_ref[...] = output
        cot = cot_ref[...].astype(f32)
        grad2 = norm_back(cot, unit2, inv2, gain2)
        add_vec(V_G2, cot * unit2)
        add_vec(V_S2, cot)
        bgrad = grad2.astype(bf16)
        add_vec(V_DB, bgrad.astype(f32))
        brT_s[:, rows] = bgrad.T
        fgrad = grad2
        for r in range(2):
            for c in range(0, FHALF, FC):
                at = r * FHALF + c
                dact = dot(bgrad, w_ref[r, :, HALF + FHALF + c : HALF + FHALF + c + FC])
                dbef = (dact * dg_s[:, at : at + FC]).astype(bf16)
                bg_s[rows, at : at + FC] = dbef
                vs_ref[r, :, V_UB + c : V_UB + c + FC] += jnp.sum(
                    dbef.astype(f32), axis=0, keepdims=True
                )
                fgrad = fgrad + dot_nt(dbef, w_ref[r, :, HALF + c : HALF + c + FC])
        add_vec(V_G1, fgrad * unit1)
        add_vec(V_S1, fgrad)
        resid = norm_back(fgrad, unit1, inv1, gain1)
        resid_ref[...] = resid
        agrad = resid.astype(bf16)
        add_vec(V_OB, agrad.astype(f32))
        agT_s[:, rows] = agrad.T
        for r in range(2):
            dctx_ref[:, r * HALF : (r + 1) * HALF] = dot(agrad, w_ref[r, :, :HALF]).astype(bf16)

    idx = step - TSTEPS
    r = idx // TILES
    j = idx % TILES

    @pl.when((idx >= 0) & (j == 0))
    def _():
        cols = pl.ds(pl.multiple_of(r * HALF, HALF), HALF)
        dw_ref[0] = dot(agT_s[...], ctx_ref[:, cols]).astype(bf16)

    @pl.when((idx >= 0) & (j >= 1) & (j <= 4))
    def _():
        cols = pl.ds(pl.multiple_of(r * FHALF + (j - 1) * HALF, HALF), HALF)
        dw_ref[0] = dot(flT_s[...], bg_s[:, cols]).astype(bf16)

    @pl.when((idx >= 0) & (j >= 5))
    def _():
        cols = pl.ds(pl.multiple_of(r * FHALF + (j - 5) * HALF, HALF), HALF)
        dw_ref[0] = dot(brT_s[...], act_s[:, cols]).astype(bf16)


def middle(ctx, hid, cot, w, vec):
    def tok(s):
        return (jnp.minimum(s, TSTEPS - 1), 0)

    def tile(s):
        idx = jnp.maximum(s - TSTEPS, 0)
        return (idx // TILES, 0, idx % TILES)

    rows = pl.BlockSpec((TOK, D), tok)
    return pl.pallas_call(
        mid_kernel,
        grid=(TSTEPS + 2 * TILES,),
        in_specs=[
            pl.BlockSpec((LENGTH, D), lambda s: (0, 0), pipeline_mode=pl.Buffered(1)),
            rows,
            rows,
            pl.BlockSpec((2, D, REST_W), lambda s: (0, 0, 0), pipeline_mode=pl.Buffered(1)),
            pl.BlockSpec((2, 1, VEC_W), lambda s: (0, 0, 0), pipeline_mode=pl.Buffered(1)),
        ],
        out_specs=[
            rows,
            rows,
            rows,
            pl.BlockSpec((1, D, HALF), tile),
            pl.BlockSpec((2, 1, VEC_W), lambda s: (0, 0, 0)),
        ],
        out_shape=[
            jax.ShapeDtypeStruct((LENGTH, D), f32),
            jax.ShapeDtypeStruct((LENGTH, D), f32),
            jax.ShapeDtypeStruct((LENGTH, D), bf16),
            jax.ShapeDtypeStruct((2, D, REST_W), bf16),
            jax.ShapeDtypeStruct((2, 1, VEC_W), f32),
        ],
        scratch_shapes=[
            pltpu.VMEM((LENGTH, FF), bf16),
            pltpu.VMEM((LENGTH, FF), bf16),
            pltpu.VMEM((TOK, FF), f32),
            pltpu.VMEM((D, LENGTH), bf16),
            pltpu.VMEM((D, LENGTH), bf16),
            pltpu.VMEM((D, LENGTH), bf16),
        ],
        compiler_params=params(),
        name="middle",
    )(ctx, hid, cot, w, vec)


LTOK = 512
LSTEPS = LENGTH // LTOK


def last_kernel(hid_ref, dq_ref, dk_ref, dv_ref, resid_ref, w_ref, hg_ref, dw_ref, vs_ref, hT_s):
    step = pl.program_id(0)

    @pl.when(step == 0)
    def _():
        hT_s[...] = hid_ref[...].T
        for ref, off in ((dq_ref, 0), (dv_ref, HALF)):
            total = jnp.sum(ref[...].astype(f32), axis=0, keepdims=True)
            vs_ref[0, :, off : off + HALF] = total[:, :HALF]
            vs_ref[1, :, off : off + HALF] = total[:, HALF:]

    @pl.when(step < LSTEPS)
    def _():
        rows = pl.ds(pl.multiple_of(step * LTOK, LTOK), LTOK)
        acc = resid_ref[...]
        for m, ref in enumerate((dq_ref, dk_ref, dv_ref)):
            for r in range(2):
                acc = acc + dot_nt(
                    ref[rows, r * HALF : (r + 1) * HALF],
                    w_ref[r, :, m * HALF : (m + 1) * HALF],
                )
        hg_ref[...] = acc

    idx = step - LSTEPS
    cols = pl.ds(pl.multiple_of(jnp.maximum(idx, 0) // 3 * HALF, HALF), HALF)
    for m, ref in enumerate((dq_ref, dk_ref, dv_ref)):

        @pl.when((idx >= 0) & (idx % 3 == m))
        def _(ref=ref):
            dw_ref[0] = dot(hT_s[...], ref[:, cols]).astype(bf16)


def last(hid, dq, dk, dv, resid, w):
    whole = pl.BlockSpec((LENGTH, D), lambda s: (0, 0), pipeline_mode=pl.Buffered(1))
    rows = pl.BlockSpec((LTOK, D), lambda s: (jnp.minimum(s, LSTEPS - 1), 0))

    def tile(s):
        idx = jnp.maximum(s - LSTEPS, 0)
        return (idx // 3, 0, idx % 3)

    return pl.pallas_call(
        last_kernel,
        grid=(LSTEPS + 6,),
        in_specs=[
            whole,
            whole,
            whole,
            whole,
            rows,
            pl.BlockSpec((2, D, QKV_W), lambda s: (0, 0, 0), pipeline_mode=pl.Buffered(1)),
        ],
        out_specs=[
            rows,
            pl.BlockSpec((1, D, HALF), tile),
            pl.BlockSpec((2, 1, 2 * HALF), lambda s: (0, 0, 0)),
        ],
        out_shape=[
            jax.ShapeDtypeStruct((LENGTH, D), f32),
            jax.ShapeDtypeStruct((2, D, QKV_W), bf16),
            jax.ShapeDtypeStruct((2, 1, 2 * HALF), f32),
        ],
        scratch_shapes=[pltpu.VMEM((D, LENGTH), bf16)],
        compiler_params=params(),
        name="last",
    )(hid, dq, dk, dv, resid, w)


def gather_parts(parts, rows_n, cols_n):
    packed = jnp.concatenate(parts, axis=1)
    every = lax.all_gather(packed, ("row", "col"), axis=0, tiled=True)
    every = every.reshape(rows_n, D, packed.shape[1])
    if rows_n == 2:
        return every
    pieces, at = [], 0
    for part in parts:
        width = part.shape[1]
        one = every[:, :, at : at + width].reshape(2, rows_n // 2, D, width)
        pieces.append(one.transpose(0, 2, 1, 3).reshape(2, D, rows_n // 2 * width))
        at += width
    return jnp.concatenate(pieces, axis=2)


def scatter_parts(full, halves, rows_n, cols_n):
    widths = [h * 2 // rows_n for h in halves]
    if rows_n != 2:
        pieces, at = [], 0
        for half, width in zip(halves, widths):
            one = full[:, :, at : at + half].reshape(2, D, rows_n // 2, width)
            pieces.append(one.transpose(0, 2, 1, 3).reshape(rows_n, D, width))
            at += half
        full = jnp.concatenate(pieces, axis=2)
    flat = full.reshape(rows_n * D, sum(widths))
    mine = lax.psum_scatter(flat, ("row", "col"), scatter_dimension=0, tiled=True)
    mine = mine.astype(f32)
    out, at = [], 0
    for width in widths:
        out.append(mine[:, at : at + width])
        at += width
    return out


VEC_HALVES = (HALF, HALF, HALF, FHALF, HALF, HALF, HALF, HALF, HALF)


def on_device(
    rows_n,
    cols_n,
    hidden,
    cotangent,
    rand_blocks,
    w_query,
    w_key,
    w_value,
    w_out,
    w_up,
    w_down,
    *vectors,
):
    vec = lax.all_gather(jnp.concatenate(vectors).astype(f32), "row", axis=0, tiled=False)
    if rows_n != 2:
        pieces, at = [], 0
        for half in VEC_HALVES:
            width = half * 2 // rows_n
            pieces.append(vec[:, at : at + width].reshape(2, half))
            at += width
        vec = jnp.concatenate(pieces, axis=1)
    vec = vec.reshape(2, 1, VEC_W)
    w1 = gather_parts([w_query, w_key, w_value], rows_n, cols_n)
    w2 = gather_parts([w_out.T, w_up, w_down.T], rows_n, cols_n)
    rand = rand_blocks.reshape(-1)
    q, k, v = qkv(hidden, w1, vec)
    ctx, pm, pe = attend(q, k, v, rand)
    output, resid, dctx, dw2, vs2 = middle(ctx, hidden, cotangent, w2, vec)
    dq, dk, dv = attend_back(q, k, v, dctx, pm, pe, rand)
    hgrad, dw1, vs1 = last(hidden, dq, dk, dv, resid, w1)
    g_out, g_up, g_down = scatter_parts(dw2, (HALF, FHALF, FHALF), rows_n, cols_n)
    g_q, g_k, g_v = scatter_parts(dw1, (HALF, HALF, HALF), rows_n, cols_n)
    vs = jnp.concatenate([vs1, vs2[:, :, 2 * HALF :]], axis=2).reshape(2, VEC_W)
    vs = lax.psum(vs, ("col", "row"))
    row = lax.axis_index("row")
    sums, at = [], 0
    for half in VEC_HALVES:
        width = half * 2 // rows_n
        both = vs[:, at : at + half].reshape(rows_n, width)
        sums.append(lax.dynamic_index_in_dim(both, row, 0, keepdims=False))
        at += half
    return (output, hgrad, g_q, g_k, g_v, g_out.T, g_up, g_down.T, *sums)


def solution(mesh):
    rows_n, cols_n = mesh.shape["row"], mesh.shape["col"]
    tokens = P(("col", "row"), None)
    placed = (
        tokens,
        tokens,
        P(("col", "row"), None, None, None),
        P("col", "row"),
        P("col", "row"),
        P("col", "row"),
        P("row", "col"),
        P("col", "row"),
        P("row", "col"),
    ) + (P("row"),) * 9
    return jax.shard_map(
        functools.partial(on_device, rows_n, cols_n),
        mesh=mesh,
        in_specs=placed,
        out_specs=(
            tokens,
            tokens,
            P("col", "row"),
            P("col", "row"),
            P("col", "row"),
            P("row", "col"),
            P("col", "row"),
            P("row", "col"),
        )
        + (P("row"),) * 9,
        check_vma=False,
    )
```

time: 1850 us -> 593 us (0.32)
  waiting for transfers between devices: 759 us -> 268 us
  local copies, waits for them, and re-layouts: 426 us -> 8.75 us
  matrix products: 299 us -> 0 us
  Pallas kernels: 0 us -> 252 us
  blocking collectives: 176 us -> 45.2 us
  other arithmetic: 115 us -> 4.34 us
  starting transfers between devices: 46.3 us -> 0.16 us
    dot_general x32 -> x0, matrix products: 299 us -> none  [the longest x6 63.4 us: product(): return jnp.dot(left, right, preferred_element_type=jnp.float32)]
    pallas_call x0 -> x5, Pallas kernels: none -> 252 us  [the longest x1 83 us: attend_back(): pl.pallas_call(attend_back_kernel, grid_spec=pltpu.PrefetchScalarGridSpec...]
    reduce_scatter x7 -> x2, waiting for transfers between devices: 415 us -> 204 us  [scatter_parts(): lax.psum_scatter(flat, ('row', 'col'), scatter_dimension=0, tiled=True)]
    another operation x19 -> x0, local copies, waits for them, and re-layouts: 174 us -> none
    unnamed x19 -> x4, waiting for transfers between devices: 109 us -> 0.55 us
    all_gather x6 -> x2, waiting for transfers between devices: 170 us -> 62.9 us  [gather_parts(): every = lax.all_gather(packed, ('row', 'col'), axis=0, tiled=True)]
    gather x3 -> x0, local copies, waits for them, and re-layouts: 106 us -> none  [pick_blocks(): jnp.take_along_axis(flat, slots.reshape(sequences, heads_count, -1, 1), a...]
    all_gather x4 -> x1, blocking collectives: 89 us -> 5.49 us  [on_device(): lax.all_gather(jnp.concatenate(vectors).astype(f32), 'row', axis=0, tiled...]
  transfers between devices with their start and end apart: 27 -> 4, of which waited for: 17 -> 4; matrix products, arithmetic and copies ran while one was open for 19% -> 1% of each run, Pallas kernels for 0% -> 14%
where the time goes in v1:
time: 593 us
  waiting for transfers between devices  268 us (45%)
  Pallas kernels  252 us (42%)
  blocking collectives  45.2 us (8%)
  between operations  14 us (2%)
  local copies, waits for them, and re-layouts  8.75 us (1%)
    reduce_scatter x2, waiting for transfers between devices, scatter_parts(): lax.psum_scatter(flat, ('row', 'col'), scatter_dimension=0, tiled=True)  204 us
    pallas_call x1, Pallas kernels, attend_back(): pl.pallas_call(attend_back_kernel, grid_spec=pltpu.PrefetchScalarGridSpec...  83 us
    pallas_call x1, Pallas kernels, attend(): pl.pallas_call(attend_kernel, grid_spec=pltpu.PrefetchScalarGridSpec(num_...  72.3 us
    pallas_call x1, Pallas kernels, middle(): pl.pallas_call(mid_kernel, grid=(TSTEPS + 2 * TILES,), in_specs=[pl.Block...  68.3 us
    all_gather x2, waiting for transfers between devices, gather_parts(): every = lax.all_gather(packed, ('row', 'col'), axis=0, tiled=True)  62.9 us
    psum x1, blocking collectives, on_device(): vs = lax.psum(vs, ('col', 'row'))  39.7 us
    pallas_call x1, Pallas kernels, last(): pl.pallas_call(last_kernel, grid=(LSTEPS + 6,), in_specs=[whole, whole, w...  18.5 us
  transfers between devices with their start and end apart: 4, of which 4 were waited for; matrix products, arithmetic and copies ran while one was open for 1% of the time, Pallas kernels for 14%

profile of v1, /device:TPU:0, one launch (start us, length us, event | category | flops | bytes accessed | tf_op | source)
XLA Modules:
  0.0 592.8 jit_solution(4132103649341093904)
XLA Ops:
  7.3 0.0 all-gather.4.cloned.1.call-start
  7.3 1.5 pad_maximum_fusion.1
  8.8 0.0 all-gather.4.cloned.1.call-update
  8.8 0.0 all-gather.6.cloned.1.call-start
  8.9 1.7 pad_maximum_fusion
  10.6 0.0 reduce-scatter.3.cloned.1.call-start
  10.7 0.9 copy.36
  11.6 0.8 reshape.175.rand_ref
  12.6 5.5 all-gather.vec_ref
  18.1 56.1 %all-gather.4.cloned.1.call-done = bf16[1536,1152]{1,0:T(8,128)(2,1)} async-done(((bf16[48,1152]{1,0:T(8,128)(2,1)}), bf16[1536,1152]{1,0:T(8,128)(2,1)}) %all-gather.4.cloned.1.call-update) | async-done | bytes 3538960 | tf_op jit(solution)/shard_map/all_gather | solution.py:544
  74.2 10.4 %qkv.1 = (bf16[1024,768]{1,0:T(8,128)(2,1)}, bf16[1024,768]{1,0:T(8,128)(2,1)}, bf16[1024,768]{1,0:T(8,128)(2,1)}) custom-call(bf16[1024,768]{1,0:T(8,128)(2,1)} %hid_ref.3, bf16[2,768,1152]{2,1,0:T(8,128)(2,1)} %bitcast.16, f32[2,1,4608]{2,1,0:T(1,128)} %all-gather.vec_ref), custom_call_target="tpu_custom_call" | custom-call | tf_op jit(solution)/shard_map/qkv/pallas_call | solution.py:73
  84.6 72.3 %attend.1 = (bf16[1024,768]{1,0:T(8,128)(2,1)}, bf16[12,14,64,512]{3,2,1,0:T(8,128)(2,1)}, bf16[12,128,1024]{2,1,0:T(8,128)(2,1)}) custom-call(s32[504]{0:T(512)} %reshape.175.rand_ref, bf16[1024,768]{1,0:T(8,128)(2,1)} %get-tuple-element.34.q_ref, bf16[1024,768]{1,0:T(8,128)(2,1)} %get-tuple-element.35.k_ref, bf16[1024,768]{1,0:T(8,128)(2,1)} %get-tuple-element.36.v_ref), custom_call_target="tpu_custom_call" | custom-call | tf_op jit(solution)/shard_map/attend/pallas_call | solution.py:153
  156.9 6.8 %all-gather.6.cloned.1.call-done = bf16[1536,3456]{1,0:T(8,128)(2,1)} async-done(((bf16[48,3456]{1,0:T(8,128)(2,1)}), bf16[1536,3456]{1,0:T(8,128)(2,1)}) %all-gather.6.cloned.1.call-update) | async-done | bytes 10616848 | tf_op jit(solution)/shard_map/all_gather | solution.py:544
  163.7 68.3 %middle.1 = (f32[1024,768]{1,0:T(8,128)}, f32[1024,768]{1,0:T(8,128)}, bf16[1024,768]{1,0:T(8,128)(2,1)}, bf16[2,768,3456]{2,1,0:T(8,128)(2,1)}, f32[2,1,4608]{2,1,0:T(1,128)}) custom-call(bf16[1024,768]{1,0:T(8,128)(2,1)} %get-tuple-element.37.ctx_ref, bf16[1024,768]{1,0:T(8,128)(2,1)} %hid_ref.3, bf16[1024,768]{1,0:T(8,128)(2,1)} %cot_ref.1, ...), custom_call_target="tpu_custom_call" | custom-call | tf_op jit(solution)/shard_map/middle/pallas_call | solution.py:434
  231.9 83.0 %attend_back.1 = (bf16[1024,768]{1,0:T(8,128)(2,1)}, bf16[1024,768]{1,0:T(8,128)(2,1)}, bf16[1024,768]{1,0:T(8,128)(2,1)}) custom-call(s32[504]{0:T(512)} %reshape.175.rand_ref, bf16[1024,768]{1,0:T(8,128)(2,1)} %get-tuple-element.34.q_ref, bf16[1024,768]{1,0:T(8,128)(2,1)} %get-tuple-element.35.k_ref, bf16[1024,768]{1,0:T(8,128)(2,1)} %get-tuple-element.36.v_ref, ...), custom_call_target="tpu_custom_call" | custom-call | tf_op jit(solution)/shard_map/attend_back/pallas_call | solution.py:245
  314.9 18.5 %last.1 = (f32[1024,768]{1,0:T(8,128)}, bf16[2,768,1152]{2,1,0:T(8,128)(2,1)}, f32[2,1,768]{2,1,0:T(1,128)}) custom-call(bf16[1024,768]{1,0:T(8,128)(2,1)} %hid_ref.3, bf16[1024,768]{1,0:T(8,128)(2,1)} %get-tuple-element.42.dq_ref, bf16[1024,768]{1,0:T(8,128)(2,1)} %get-tuple-element.43.dk_ref, bf16[1024,768]{1,0:T(8,128)(2,1)} %get-tuple-element.44.dv_ref, ...), custom_call_target="tpu_custom_call" | custom-call | tf_op jit(solution)/shard_map/last/pallas_call | solution.py:515
  333.4 0.0 reduce-scatter.5.cloned.1.call-start
  333.5 0.5 reduce-scatter.5.cloned.1.call-update
  334.0 0.2 copy-done.1
  334.3 39.7 %psum.7 = f32[2,4608]{1,0:T(2,128)S(1)} all-reduce(f32[2,4608]{1,0:T(2,128)S(1)} %bitcast.21), channel_id=1, replica_groups=mesh['col'=16,'row'=2] {'col','row'}, use_global_device_ids=true, to_apply=%region_2.0 | all-reduce | flops 9216 | bytes 73728 | tf_op jit(solution)/shard_map/psum | solution.py:613
  374.1 0.6 fusion.6
  374.7 0.6 fusion.4
  375.3 0.6 fusion.2
  375.9 0.6 fusion
  376.5 0.6 dynamic-slice_reduce_fusion
  377.1 58.7 %reduce-scatter.3.cloned.1.call-done = bf16[48,1152]{1,0:T(8,128)(2,1)} async-done(((bf16[1536,1152]{1,0:T(8,128)(2,1)}), bf16[48,1152]{1,0:T(8,128)(2,1)}) %reduce-scatter.3.cloned.1.call-update) | async-done | bytes 110608 | tf_op jit(solution)/shard_map/reduce_scatter | solution.py:567
  435.8 1.5 fusion.8
  437.3 145.7 %reduce-scatter.5.cloned.1.call-done = bf16[48,3456]{1,0:T(8,128)(2,1)} async-done(((bf16[1536,3456]{1,0:T(8,128)(2,1)}), bf16[48,3456]{1,0:T(8,128)(2,1)}) %reduce-scatter.5.cloned.1.call-update) | async-done | bytes 331792 | tf_op jit(solution)/shard_map/reduce_scatter | solution.py:567
  583.1 1.1 convert_element_type.18
  584.2 0.7 slice_bitcast_fusion
  584.9 0.6 slice_bitcast_fusion.1
  585.5 0.7 slice.68
  (40 shorter events, 0.3 us)
Async XLA Ops:
  7.2 5.2 copy-start.4
  7.2 5.2 copy-start.5
  7.2 5.2 copy-start.6
  7.2 5.2 copy-start.3
  7.2 5.2 copy-start.7
  7.2 5.2 copy-start.8
  7.3 5.3 copy-start.9
  7.3 5.3 copy-start.10
  7.3 5.3 copy-start.11
  7.3 66.9 %all-gather.4.cloned.1.call-start = ((), (), s32[]{:S(2)}) async-start(), calls=%async_computation.2 | async-start | bytes 3649536 | tf_op jit(solution)/shard_map/all_gather | solution.py:544
  8.8 154.9 %all-gather.6.cloned.1.call-start = ((), (), s32[]{:S(2)}) async-start(), calls=%async_computation.3 | async-start | bytes 10948608 | tf_op jit(solution)/shard_map/all_gather | solution.py:544
  10.6 425.2 %reduce-scatter.3.cloned.1.call-start = ((), (), s32[]{:S(2)}) async-start(), calls=%async_computation.4 | async-start | bytes 3649536 | tf_op jit(solution)/shard_map/reduce_scatter | solution.py:567
  333.4 249.6 %reduce-scatter.5.cloned.1.call-start = ((), (), s32[]{:S(2)}) async-start(), calls=%async_computation.5 | async-start | bytes 10948608 | tf_op jit(solution)/shard_map/reduce_scatter | solution.py:567
  333.5 0.8 copy-start.1
  333.5 0.8 copy-start.2
  583.1 2.5 copy-start
Sparse Core Ops, SparseCore 0:
  11.5 62.6 all-gather.3
  77.7 85.9 all-gather.5
  333.5 102.2 reduce-scatter.2
  441.8 141.2 reduce-scatter.4

commit v2 on v1

--- a/solution.py
+++ b/solution.py
@@ -85,186 +85,104 @@
     )(x, w, vec)
 
 
-def softmax_bf16(s):
-    top = jnp.max(s, axis=-1, keepdims=True)
-    e = jnp.exp(s - top)
-    total = jnp.sum(e, axis=-1, keepdims=True)
-    return (e * (1.0 / total)).astype(bf16)
-
-
-def head_mask(a, rows):
-    lane = lax.broadcasted_iota(jnp.int32, (rows, 2 * HD), 1)
-    return (lane < HD) if a == 0 else (lane >= HD)
-
-
-def only_head(a, x):
-    return jnp.where(head_mask(a, x.shape[0]), x, jnp.zeros_like(x))
-
-
-def key_rows(ref, rand_ref, head, i):
-    near = ref[pl.ds(pl.multiple_of((i - 1) * BLK, BLK), 3 * BLK), :]
-    parts = [ref[0:BLK, :], ref[LENGTH - BLK :, :], near]
-    for n in range(RAND):
-        b = rand_ref[((i - 1) * H + head) * RAND + n]
-        parts.append(ref[pl.ds(pl.multiple_of(b * BLK, BLK), BLK), :])
-    return jnp.concatenate(parts, axis=0)
-
-
-def edge_mask(s, i):
-    col = lax.broadcasted_iota(jnp.int32, s.shape, 1)
-    start = jnp.where(i == 1, 2 * BLK, jnp.where(i == BLOCKS - 2, 4 * BLK, -BLK))
-    return jnp.where((col >= start) & (col < start + BLK), NEG, s)
-
-
-def attend_kernel(rand_ref, q_ref, k_ref, v_ref, c_ref, pm_ref, pe_ref):
-    pair = pl.program_id(0)
+QT = 256
+QTILES = LENGTH // QT
+
+
+def head_lanes(a, x):
+    lane = lax.broadcasted_iota(jnp.int32, x.shape, 1)
+    return jnp.where((lane < HD) if a == 0 else (lane >= HD), x, jnp.zeros_like(x))
+
+
+def both_heads(top, low):
+    row = lax.broadcasted_iota(jnp.int32, top.shape, 0)
+    return jnp.where(row < HD, top, low)
+
+
+def hidden_pairs(rand):
+    rows = jnp.arange(BLOCKS)[:, None]
+    cols = jnp.arange(BLOCKS)[None, :]
+    edge = (rows == 0) | (rows == BLOCKS - 1) | (cols == 0) | (cols == BLOCKS - 1)
+    near = jnp.abs(rows - cols) <= 1
+    chosen = (rand[:, :, :, None] == jnp.arange(BLOCKS)).any(axis=2)
+    chosen = jnp.pad(chosen.transpose(1, 2, 0), ((0, 0), (0, 0), (1, 1)))
+    table = jnp.where(chosen | (edge | near)[None], 0.0, NEG).astype(f32)
+    return jnp.repeat(table, BLK, axis=2)
+
+
+def attend_kernel(q_ref, k_ref, v_ref, hide_ref, c_ref, p_ref):
     kall = k_ref[...]
-    vall = v_ref[...]
-    qe = jnp.concatenate([q_ref[0:BLK, :], q_ref[LENGTH - BLK :, :]], axis=0)
-    ends = []
-    for a in range(2):
-        p = softmax_bf16(dot_nt(only_head(a, qe), kall))
-        pe_ref[a] = p
-        ends.append(dot(p, vall))
-    ce = jnp.where(head_mask(0, 2 * BLK), ends[0], ends[1]).astype(bf16)
-    c_ref[0:BLK, :] = ce[:BLK]
-    c_ref[LENGTH - BLK :, :] = ce[BLK:]
-
-    def block(i):
-        row = pl.multiple_of(i * BLK, BLK)
-        qi = q_ref[pl.ds(row, BLK), :]
+    vT = v_ref[...].T
+
+    @pl.loop(0, QTILES)
+    def _(n):
+        at = pl.ds(pl.multiple_of(n * QT, QT), QT)
+        q = q_ref[at, :]
         outs = []
         for a in range(2):
-            kk = key_rows(k_ref, rand_ref, pair * 2 + a, i)
-            vv = key_rows(v_ref, rand_ref, pair * 2 + a, i)
-            p = softmax_bf16(edge_mask(dot_nt(only_head(a, qi), kk), i))
-            pm_ref[a, i - 1] = p
-            outs.append(dot(p, vv))
-        c_ref[pl.ds(row, BLK), :] = jnp.where(head_mask(0, BLK), outs[0], outs[1]).astype(bf16)
-
-    @pl.loop(0, (BLOCKS - 2) // 2)
-    def _(n):
-        block(1 + 2 * n)
-        block(2 + 2 * n)
-
-
-def attend(q, k, v, rand):
-    pair = pl.BlockSpec((LENGTH, 2 * HD), lambda h, r: (0, h))
+            s = dot_nt(kall, head_lanes(a, q)).reshape(BLOCKS, BLK, QT)
+            s = (s + hide_ref[a, :, at][:, None, :]).reshape(LENGTH, QT)
+            e = jnp.exp(s - jnp.max(s, axis=0, keepdims=True))
+            p = (e * (1.0 / jnp.sum(e, axis=0, keepdims=True))).astype(bf16)
+            p_ref[a, :, at] = p
+            outs.append(dot(vT, p))
+        c_ref[at, :] = both_heads(*outs).T.astype(bf16)
+
+
+def attend(q, k, v, hide):
+    pair = pl.BlockSpec((LENGTH, 2 * HD), lambda h: (0, h))
     return pl.pallas_call(
         attend_kernel,
-        grid_spec=pltpu.PrefetchScalarGridSpec(
-            num_scalar_prefetch=1,
-            grid=(H // 2,),
-            in_specs=[pair, pair, pair],
-            out_specs=[
-                pair,
-                pl.BlockSpec((2, BLOCKS - 2, BLK, 8 * BLK), lambda h, r: (h, 0, 0, 0)),
-                pl.BlockSpec((2, 2 * BLK, LENGTH), lambda h, r: (h, 0, 0)),
-            ],
-        ),
+        grid=(H // 2,),
+        in_specs=[pair, pair, pair, pl.BlockSpec((2, BLOCKS, LENGTH), lambda h: (h, 0, 0))],
+        out_specs=[pair, pl.BlockSpec((2, LENGTH, LENGTH), lambda h: (h, 0, 0))],
         out_shape=[
             jax.ShapeDtypeStruct((LENGTH, D), bf16),
-            jax.ShapeDtypeStruct((H, BLOCKS - 2, BLK, 8 * BLK), bf16),
-            jax.ShapeDtypeStruct((H, 2 * BLK, LENGTH), bf16),
+            jax.ShapeDtypeStruct((H, LENGTH, LENGTH), bf16),
         ],
         compiler_params=params(),
         name="attend",
-    )(rand, q, k, v)
-
-
-def score_grad(p, dots):
-    pf = p.astype(f32)
-    along = jnp.sum(dots * pf, axis=-1, keepdims=True)
-    return (pf * (dots - along)).astype(bf16)
-
-
-def attend_back_kernel(
-    rand_ref, q_ref, k_ref, v_ref, d_ref, pm_ref, pe_ref, dq_ref, dk_ref, dv_ref, dk_s, dv_s
-):
-    pair = pl.program_id(0)
-    kall = k_ref[...]
+    )(q, k, v, hide)
+
+
+def attend_back_kernel(q_ref, k_ref, v_ref, d_ref, p_ref, dq_ref, dk_ref, dv_ref, ds_s):
     vall = v_ref[...]
-    qe = jnp.concatenate([q_ref[0:BLK, :], q_ref[LENGTH - BLK :, :]], axis=0)
-    de = jnp.concatenate([d_ref[0:BLK, :], d_ref[LENGTH - BLK :, :]], axis=0)
-    dss, dqs = [], []
-    for a in range(2):
-        ds = score_grad(pe_ref[a], dot_nt(only_head(a, de), vall))
-        dss.append(ds)
-        dqs.append(dot(ds, kall))
-    dqe = (jnp.where(head_mask(0, 2 * BLK), dqs[0], dqs[1]) * 0.125).astype(bf16)
-    dq_ref[0:BLK, :] = dqe[:BLK]
-    dq_ref[LENGTH - BLK :, :] = dqe[BLK:]
-    q2 = jnp.concatenate([only_head(0, qe), only_head(1, qe)], axis=0)
-    d2 = jnp.concatenate([only_head(0, de), only_head(1, de)], axis=0)
-    dk_s[...] = dot_tn(jnp.concatenate(dss, axis=0), q2)
-    dv_s[...] = dot_tn(jnp.concatenate([pe_ref[0], pe_ref[1]], axis=0), d2)
-
-    def block(i):
-        row = pl.multiple_of(i * BLK, BLK)
-        qi = q_ref[pl.ds(row, BLK), :]
-        di = d_ref[pl.ds(row, BLK), :]
-        dss, dqs, ps, qm, dm = [], [], [], [], []
+    kT = k_ref[...].T
+
+    @pl.loop(0, QTILES)
+    def _(n):
+        at = pl.ds(pl.multiple_of(n * QT, QT), QT)
+        d = d_ref[at, :]
+        outs = []
         for a in range(2):
-            kk = key_rows(k_ref, rand_ref, pair * 2 + a, i)
-            vv = key_rows(v_ref, rand_ref, pair * 2 + a, i)
-            p = pm_ref[a, i - 1]
-            dm.append(only_head(a, di))
-            qm.append(only_head(a, qi))
-            ds = score_grad(p, dot_nt(dm[a], vv))
-            ps.append(p)
-            dss.append(ds)
-            dqs.append(dot(ds, kk))
-        dq_ref[pl.ds(row, BLK), :] = (
-            jnp.where(head_mask(0, BLK), dqs[0], dqs[1]) * 0.125
-        ).astype(bf16)
-        q2 = jnp.concatenate(qm, axis=0)
-        d2 = jnp.concatenate(dm, axis=0)
-        fixed = 5 * BLK
-        for acc, left, right, each in ((dk_s, dss, q2, qm), (dv_s, ps, d2, dm)):
-            both = dot_tn(jnp.concatenate([x[:, :fixed] for x in left], axis=0), right)
-            acc[0:BLK, :] += both[0:BLK]
-            acc[LENGTH - BLK :, :] += both[BLK : 2 * BLK]
-            acc[pl.ds(pl.multiple_of((i - 1) * BLK, BLK), 3 * BLK), :] += both[2 * BLK :]
-            for a in range(2):
-                own = dot_tn(left[a][:, fixed:], each[a])
-                for n in range(RAND):
-                    b = rand_ref[((i - 1) * H + pair * 2 + a) * RAND + n]
-                    acc[pl.ds(pl.multiple_of(b * BLK, BLK), BLK), :] += own[n * BLK : (n + 1) * BLK]
-
-    @pl.loop(1, BLOCKS - 1)
-    def _(i):
-        block(i)
-
-    dk_ref[...] = dk_s[...].astype(bf16)
-    dv_ref[...] = dv_s[...].astype(bf16)
-
-
-def attend_back(q, k, v, d, pm, pe, rand):
-    pair = pl.BlockSpec((LENGTH, 2 * HD), lambda h, r: (0, h))
+            dots = dot_nt(vall, head_lanes(a, d))
+            p = p_ref[a, :, at].astype(f32)
+            ds = (p * (dots - jnp.sum(dots * p, axis=0, keepdims=True))).astype(bf16)
+            ds_s[a, :, at] = ds
+            outs.append(dot(kT, ds))
+        dq_ref[at, :] = (both_heads(*outs).T * 0.125).astype(bf16)
+
+    dk_ref[...] = (
+        dot(ds_s[0], head_lanes(0, q_ref[...])) + dot(ds_s[1], head_lanes(1, q_ref[...]))
+    ).astype(bf16)
+    dv_ref[...] = (
+        dot(p_ref[0], head_lanes(0, d_ref[...])) + dot(p_ref[1], head_lanes(1, d_ref[...]))
+    ).astype(bf16)
+
+
+def attend_back(q, k, v, d, p):
+    pair = pl.BlockSpec((LENGTH, 2 * HD), lambda h: (0, h))
     out = jax.ShapeDtypeStruct((LENGTH, D), bf16)
     return pl.pallas_call(
         attend_back_kernel,
-        grid_spec=pltpu.PrefetchScalarGridSpec(
-            num_scalar_prefetch=1,
-            grid=(H // 2,),
-            in_specs=[
-                pair,
-                pair,
-                pair,
-                pair,
-                pl.BlockSpec((2, BLOCKS - 2, BLK, 8 * BLK), lambda h, r: (h, 0, 0, 0)),
-                pl.BlockSpec((2, 2 * BLK, LENGTH), lambda h, r: (h, 0, 0)),
-            ],
-            out_specs=[pair, pair, pair],
-            scratch_shapes=[
-                pltpu.VMEM((LENGTH, 2 * HD), f32),
-                pltpu.VMEM((LENGTH, 2 * HD), f32),
-            ],
-        ),
+        grid=(H // 2,),
+        in_specs=[pair, pair, pair, pair, pl.BlockSpec((2, LENGTH, LENGTH), lambda h: (h, 0, 0))],
+        out_specs=[pair, pair, pair],
         out_shape=[out, out, out],
+        scratch_shapes=[pltpu.VMEM((2, LENGTH, LENGTH), bf16)],
         compiler_params=params(),
         name="attend_back",
-    )(rand, q, k, v, d, pm, pe)
+    )(q, k, v, d, p)
 
 
 TOK = 256
@@ -601,11 +519,11 @@
     vec = vec.reshape(2, 1, VEC_W)
     w1 = gather_parts([w_query, w_key, w_value], rows_n, cols_n)
     w2 = gather_parts([w_out.T, w_up, w_down.T], rows_n, cols_n)
-    rand = rand_blocks.reshape(-1)
+    hide = hidden_pairs(rand_blocks[0])
     q, k, v = qkv(hidden, w1, vec)
-    ctx, pm, pe = attend(q, k, v, rand)
+    ctx, p = attend(q, k, v, hide)
     output, resid, dctx, dw2, vs2 = middle(ctx, hidden, cotangent, w2, vec)
-    dq, dk, dv = attend_back(q, k, v, dctx, pm, pe, rand)
+    dq, dk, dv = attend_back(q, k, v, dctx, p)
     hgrad, dw1, vs1 = last(hidden, dq, dk, dv, resid, w1)
     g_out, g_up, g_down = scatter_parts(dw2, (HALF, FHALF, FHALF), rows_n, cols_n)
     g_q, g_k, g_v = scatter_parts(dw1, (HALF, HALF, HALF), rows_n, cols_n)

time: 593 us -> 569 us (0.960)
  Pallas kernels: 252 us -> 208 us
  waiting for transfers between devices: 268 us -> 285 us
    pallas_call x2, Pallas kernels: 155 us -> 111 us  [the longest x1 60.6 us: attend_back(): pl.pallas_call(attend_back_kernel, grid=(H // 2,), in_specs=[pair, pair,...]
    all_gather x2, waiting for transfers between devices: 62.9 us -> 82.6 us  [gather_parts(): every = lax.all_gather(packed, ('row', 'col'), axis=0, tiled=True)]
  transfers between devices with their start and end apart: 4 -> 4, of which waited for: 4 -> 4; matrix products, arithmetic and copies ran while one was open for 1% -> 2% of each run, Pallas kernels for 14% -> 11%
where the time goes in v2:
time: 569 us
  waiting for transfers between devices  285 us (50%)
  Pallas kernels  208 us (37%)
  blocking collectives  44.8 us (8%)
  between operations  14.1 us (2%)
  local copies, waits for them, and re-layouts  12 us (2%)
    reduce_scatter x2, waiting for transfers between devices, scatter_parts(): lax.psum_scatter(flat, ('row', 'col'), scatter_dimension=0, tiled=True)  202 us
    all_gather x2, waiting for transfers between devices, gather_parts(): every = lax.all_gather(packed, ('row', 'col'), axis=0, tiled=True)  82.6 us
    pallas_call x1, Pallas kernels, middle(): pl.pallas_call(mid_kernel, grid=(TSTEPS + 2 * TILES,), in_specs=[pl.Block...  68.3 us
    pallas_call x1, Pallas kernels, attend_back(): pl.pallas_call(attend_back_kernel, grid=(H // 2,), in_specs=[pair, pair,...  60.6 us
    pallas_call x1, Pallas kernels, attend(): pl.pallas_call(attend_kernel, grid=(H // 2,), in_specs=[pair, pair, pair,...  50.3 us
    psum x1, blocking collectives, on_device(): vs = lax.psum(vs, ('col', 'row'))  39.4 us
    pallas_call x1, Pallas kernels, last(): pl.pallas_call(last_kernel, grid=(LSTEPS + 6,), in_specs=[whole, whole, w...  18.4 us
  transfers between devices with their start and end apart: 4, of which 4 were waited for; matrix products, arithmetic and copies ran while one was open for 2% of the time, Pallas kernels for 11%

profile of v2, /device:TPU:0, one launch (start us, length us, event | category | flops | bytes accessed | tf_op | source)
XLA Modules:
  0.0 568.8 jit_solution(5529562803892311202)
XLA Ops:
  7.2 1.5 pad_maximum_fusion.1
  8.8 1.7 pad_maximum_fusion
  10.6 0.7 copy.43
  11.7 0.5 broadcast_in_dim.17
  12.3 1.3 reshape.256.hide_ref
  13.8 5.5 all-gather.vec_ref
  19.3 54.8 %all-gather.4.cloned.1.call-done = bf16[1536,1152]{1,0:T(8,128)(2,1)} async-done(((bf16[48,1152]{1,0:T(8,128)(2,1)}), bf16[1536,1152]{1,0:T(8,128)(2,1)}) %all-gather.4.cloned.1.call-update) | async-done | bytes 3538960 | tf_op jit(solution)/shard_map/all_gather | solution.py:462
  74.1 10.2 %qkv.1 = (bf16[1024,768]{1,0:T(8,128)(2,1)}, bf16[1024,768]{1,0:T(8,128)(2,1)}, bf16[1024,768]{1,0:T(8,128)(2,1)}) custom-call(bf16[1024,768]{1,0:T(8,128)(2,1)} %hid_ref.3, bf16[2,768,1152]{2,1,0:T(8,128)(2,1)} %bitcast.22, f32[2,1,4608]{2,1,0:T(1,128)} %all-gather.vec_ref), custom_call_target="tpu_custom_call" | custom-call | tf_op jit(solution)/shard_map/qkv/pallas_call | solution.py:73
  84.3 50.3 %attend.1 = (bf16[1024,768]{1,0:T(8,128)(2,1)}, bf16[12,1024,1024]{2,1,0:T(8,128)(2,1)}) custom-call(bf16[1024,768]{1,0:T(8,128)(2,1)} %get-tuple-element.33.q_ref, bf16[1024,768]{1,0:T(8,128)(2,1)} %get-tuple-element.34.k_ref, bf16[1024,768]{1,0:T(8,128)(2,1)} %get-tuple-element.35.v_ref, f32[12,16,1024]{2,1,0:T(8,128)} %reshape.256.hide_ref), custom_call_target="tpu_custom_call" | custom-call | tf_op jit(solution)/shard_map/attend/pallas_call | solution.py:134
  134.7 27.7 %all-gather.6.cloned.1.call-done = bf16[1536,3456]{1,0:T(8,128)(2,1)} async-done(((bf16[48,3456]{1,0:T(8,128)(2,1)}), bf16[1536,3456]{1,0:T(8,128)(2,1)}) %all-gather.6.cloned.1.call-update) | async-done | bytes 10616848 | tf_op jit(solution)/shard_map/all_gather | solution.py:462
  162.4 68.3 %middle.1 = (f32[1024,768]{1,0:T(8,128)}, f32[1024,768]{1,0:T(8,128)}, bf16[1024,768]{1,0:T(8,128)(2,1)}, bf16[2,768,3456]{2,1,0:T(8,128)(2,1)}, f32[2,1,4608]{2,1,0:T(1,128)}) custom-call(bf16[1024,768]{1,0:T(8,128)(2,1)} %get-tuple-element.36.ctx_ref, bf16[1024,768]{1,0:T(8,128)(2,1)} %hid_ref.3, bf16[1024,768]{1,0:T(8,128)(2,1)} %cot_ref.1, ...), custom_call_target="tpu_custom_call" | custom-call | tf_op jit(solution)/shard_map/middle/pallas_call | solution.py:352
  230.7 60.6 %attend_back.1 = (bf16[1024,768]{1,0:T(8,128)(2,1)}, bf16[1024,768]{1,0:T(8,128)(2,1)}, bf16[1024,768]{1,0:T(8,128)(2,1)}) custom-call(bf16[1024,768]{1,0:T(8,128)(2,1)} %get-tuple-element.33.q_ref, bf16[1024,768]{1,0:T(8,128)(2,1)} %get-tuple-element.34.k_ref, bf16[1024,768]{1,0:T(8,128)(2,1)} %get-tuple-element.35.v_ref, ...), custom_call_target="tpu_custom_call" | custom-call | tf_op jit(solution)/shard_map/attend_back/pallas_call | solution.py:176
  291.3 18.4 %last.1 = (f32[1024,768]{1,0:T(8,128)}, bf16[2,768,1152]{2,1,0:T(8,128)(2,1)}, f32[2,1,768]{2,1,0:T(1,128)}) custom-call(bf16[1024,768]{1,0:T(8,128)(2,1)} %hid_ref.3, bf16[1024,768]{1,0:T(8,128)(2,1)} %get-tuple-element.40.dq_ref, bf16[1024,768]{1,0:T(8,128)(2,1)} %get-tuple-element.41.dk_ref, bf16[1024,768]{1,0:T(8,128)(2,1)} %get-tuple-element.42.dv_ref, ...), custom_call_target="tpu_custom_call" | custom-call | tf_op jit(solution)/shard_map/last/pallas_call | solution.py:433
  309.8 0.5 reduce-scatter.5.cloned.1.call-update
  310.3 0.2 copy-done.1
  310.6 39.4 %psum.7 = f32[2,4608]{1,0:T(2,128)S(1)} all-reduce(f32[2,4608]{1,0:T(2,128)S(1)} %bitcast.27), channel_id=1, replica_groups=mesh['col'=16,'row'=2] {'col','row'}, use_global_device_ids=true, to_apply=%region_3.4 | all-reduce | flops 9216 | bytes 73728 | tf_op jit(solution)/shard_map/psum | solution.py:531
  350.0 0.6 fusion.4
  350.6 0.6 fusion.5
  351.2 0.6 fusion.6
  351.8 0.6 fusion.7
  352.4 0.6 fusion.8
  353.0 0.6 fusion.9
  353.6 0.6 fusion.3
  354.2 0.6 fusion.2
  354.8 0.6 dynamic-slice_reduce_fusion
  355.4 56.4 %reduce-scatter.3.cloned.1.call-done = bf16[48,1152]{1,0:T(8,128)(2,1)} async-done(((bf16[1536,1152]{1,0:T(8,128)(2,1)}), bf16[48,1152]{1,0:T(8,128)(2,1)}) %reduce-scatter.3.cloned.1.call-update) | async-done | bytes 110608 | tf_op jit(solution)/shard_map/reduce_scatter | solution.py:485
  411.8 1.5 fusion.11
  413.3 145.7 %reduce-scatter.5.cloned.1.call-done = bf16[48,3456]{1,0:T(8,128)(2,1)} async-done(((bf16[1536,3456]{1,0:T(8,128)(2,1)}), bf16[48,3456]{1,0:T(8,128)(2,1)}) %reduce-scatter.5.cloned.1.call-update) | async-done | bytes 331792 | tf_op jit(solution)/shard_map/reduce_scatter | solution.py:485
  559.1 1.1 convert_element_type.20
  560.2 0.7 slice_bitcast_fusion
  560.9 0.6 slice_bitcast_fusion.1
  561.5 0.7 slice.68
  (51 shorter events, 0.8 us)
Async XLA Ops:
  7.2 66.9 %all-gather.4.cloned.1.call-start = ((), (), s32[]{:S(2)}) async-start(), calls=%async_computation.2 | async-start | bytes 3649536 | tf_op jit(solution)/shard_map/all_gather | solution.py:462
  8.7 153.7 %all-gather.6.cloned.1.call-start = ((), (), s32[]{:S(2)}) async-start(), calls=%async_computation.3 | async-start | bytes 10948608 | tf_op jit(solution)/shard_map/all_gather | solution.py:462
  10.5 401.3 %reduce-scatter.3.cloned.1.call-start = ((), (), s32[]{:S(2)}) async-start(), calls=%async_computation.4 | async-start | bytes 3649536 | tf_op jit(solution)/shard_map/reduce_scatter | solution.py:485
  12.2 1.4 copy-start.4
  12.2 1.4 copy-start.5
  12.2 1.4 copy-start.6
  12.2 1.4 copy-start.3
  12.2 1.5 copy-start.7
  12.2 1.5 copy-start.8
  12.2 1.5 copy-start.9
  12.2 1.5 copy-start.10
  12.3 1.5 copy-start.11
  309.7 249.4 %reduce-scatter.5.cloned.1.call-start = ((), (), s32[]{:S(2)}) async-start(), calls=%async_computation.5 | async-start | bytes 10948608 | tf_op jit(solution)/shard_map/reduce_scatter | solution.py:485
  309.8 0.8 copy-start.1
  309.8 0.8 copy-start.2
  559.1 2.5 copy-start
Sparse Core Ops, SparseCore 0:
  11.5 62.6 all-gather.3
  77.0 85.3 all-gather.5
  309.8 101.9 reduce-scatter.2
  417.8 141.2 reduce-scatter.4

commit v3 on v2

--- a/solution.py
+++ b/solution.py
@@ -83,6 +83,242 @@
         compiler_params=params(),
         name="qkv",
     )(x, w, vec)
+
+
+MESH = pl.DeviceIdType.MESH
+
+
+class Place:
+    def __init__(self, zs):
+        c = lax.axis_index("col")
+        y = lax.axis_index("row")
+        self.zs = zs
+        self.core, self.x, self.y, self.z = c % 2, c // 2 % 2, y, c // 4
+        self.by_core = {"col": c + 1 - 2 * self.core, "row": y}
+        self.by_x = {"col": c + 2 - 4 * self.x, "row": y}
+        self.by_y = {"col": c, "row": 1 - y}
+        self.within = c % 4
+
+    def ahead(self, d):
+        return (self.z + d) % self.zs
+
+    def by_z(self, d):
+        return {"col": self.ahead(d) * 4 + self.within, "row": self.y}
+
+
+def greet(partners):
+    barrier = pltpu.get_barrier_semaphore()
+    for to in partners:
+        pl.semaphore_signal(barrier, inc=1, device_id=to, device_id_type=MESH)
+    pl.semaphore_wait(barrier, len(partners))
+
+
+def remote(src, dst, send, recv, i, to):
+    return pltpu.make_async_remote_copy(
+        src_ref=src,
+        dst_ref=dst,
+        send_sem=send.at[i],
+        recv_sem=recv.at[i],
+        device_id=to,
+        device_id_type=MESH,
+    )
+
+
+def add_low(a, b):
+    return (a.astype(f32) + b.astype(f32)).astype(bf16)
+
+
+def plane_scratch(zs, rows, width):
+    half = zs // 2
+    return [
+        pltpu.VMEM((2, zs, 2, rows, width), bf16),
+        pltpu.VMEM((2, zs, 2, rows, width), bf16),
+        pltpu.VMEM((2, half, rows, width), bf16),
+        pltpu.VMEM((half, 2, rows, width), bf16),
+        pltpu.VMEM((half, rows, width), bf16),
+        pltpu.VMEM((half, rows, width), bf16),
+        pltpu.SemaphoreType.DMA((5,)),
+        pltpu.SemaphoreType.DMA((5,)),
+        pltpu.SemaphoreType.DMA,
+    ]
+
+
+class PlaneSum:
+    def __init__(self, at, g, own, b1, b2x, b2y, b3y, b3x, send, recv, local):
+        half = at.zs // 2
+        self.at, self.half = at, half
+        self.own, self.b1, self.b2x, self.b2y, self.b3y, self.b3x = own, b1, b2x, b2y, b3y, b3x
+        self.g, self.send, self.recv, self.local = g, send, recv, local
+
+    def keep(self):
+        return pltpu.make_async_copy(self.g.at[:, :, :, self.at.core], self.own, self.local)
+
+    def to_core(self):
+        at = self.at
+        return remote(self.g.at[:, :, :, 1 - at.core], self.b1, self.send, self.recv, 0, at.by_core)
+
+    def second(self):
+        at, half, sems = self.at, self.half, (self.send, self.recv)
+        return (
+            remote(self.b1.at[:, 0:half, 1 - at.x], self.b2x, *sems, 1, at.by_x),
+            remote(self.b1.at[1 - at.y, half:], self.b2y, *sems, 2, at.by_y),
+        )
+
+    def third(self):
+        at, sems = self.at, (self.send, self.recv)
+        return (
+            remote(self.b2x.at[1 - at.y], self.b3y, *sems, 3, at.by_y),
+            remote(self.b2y.at[:, 1 - at.x], self.b3x, *sems, 4, at.by_x),
+        )
+
+    def stage1(self):
+        self.keep().start()
+        self.to_core().start()
+
+    def stage2(self):
+        self.keep().wait()
+        self.to_core().wait()
+        b1, own = self.b1, self.own
+
+        @pl.loop(0, self.at.zs)
+        def _(z):
+            for y in range(2):
+                for x in range(2):
+                    b1[y, z, x] = add_low(b1[y, z, x], own[y, z, x])
+
+        for copy in self.second():
+            copy.start()
+
+    def stage3(self):
+        for copy in self.second():
+            copy.wait()
+        b1, b2x, b2y, half = self.b1, self.b2x, self.b2y, self.half
+
+        @pl.loop(0, half)
+        def _(z):
+            for n in range(2):
+                b2x[n, z] = add_low(b2x[n, z], b1[n, z, self.at.x])
+                b2y[z, n] = add_low(b2y[z, n], b1[self.at.y, half + z, n])
+
+        for copy in self.third():
+            copy.start()
+
+    def finish(self, out):
+        for copy in self.third():
+            copy.wait()
+        half = self.half
+
+        @pl.loop(0, half)
+        def _(z):
+            out[z] = add_low(self.b3y[z], self.b2x[self.at.y, z])
+            out[half + z] = add_low(self.b3x[z], self.b2y[z, self.at.x])
+
+
+def line_scratch(zs, rows, width):
+    return [
+        pltpu.VMEM((zs - 1, rows, width), bf16),
+        pltpu.SemaphoreType.DMA((zs - 1,)),
+        pltpu.SemaphoreType.DMA((zs - 1,)),
+    ]
+
+
+class LineSum:
+    def __init__(self, at, h, held, send, recv):
+        self.at, self.h, self.held = at, h, held
+        self.copies = [
+            remote(h.at[at.ahead(d)], held.at[d - 1], send, recv, d - 1, at.by_z(d))
+            for d in range(1, at.zs)
+        ]
+
+    def start(self):
+        for copy in self.copies:
+            copy.start()
+
+    def finish(self, out):
+        for copy in self.copies:
+            copy.wait()
+        total = self.h[self.at.z].astype(f32)
+        for d in range(1, self.at.zs):
+            total = total + self.held[d - 1].astype(f32)
+        out[...] = total
+
+
+def final_kernel(zs, g_ref, h_ref, v_ref, o1_ref, o2_ref, vo_ref, mid, *scratch):
+    plane, (v1, v2, v3, v4, va, vb, vsend, vrecv), line1, line2 = (
+        scratch[:9],
+        scratch[9:17],
+        scratch[17:20],
+        scratch[20:23],
+    )
+    at = Place(zs)
+    greet([at.by_core, at.by_x, at.by_y] + [at.by_z(d) for d in range(1, zs)])
+    first = PlaneSum(at, g_ref, *plane)
+    second = LineSum(at, h_ref, *line2)
+    first.stage1()
+    vec1 = remote(v_ref, v1, vsend, vrecv, 0, at.by_core)
+    vec1.start()
+    second.start()
+    vec1.wait()
+    va[...] = v_ref[...] + v1[...]
+    vec2 = remote(va, v2, vsend, vrecv, 1, at.by_x)
+    vec2.start()
+    first.stage2()
+    vec2.wait()
+    vb[...] = va[...] + v2[...]
+    vec3 = remote(vb.at[1 - at.y], v3, vsend, vrecv, 2, at.by_y)
+    vec3.start()
+    first.stage3()
+    vec3.wait()
+    v4[0] = vb[at.y] + v3[...]
+    vec4 = [
+        remote(v4.at[0], v4.at[d], vsend, vrecv, 2 + d, at.by_z(d)) for d in range(1, zs)
+    ]
+    for copy in vec4:
+        copy.start()
+    first.finish(mid)
+    third = LineSum(at, mid, *line1)
+    third.start()
+    for copy in vec4:
+        copy.wait()
+    total = v4[at.z % zs]
+    for z in range(1, zs):
+        total = total + v4[(at.z + zs - z) % zs]
+    vo_ref[...] = total
+    second.finish(o2_ref)
+    third.finish(o1_ref)
+
+
+def final(zs, g, h, v):
+    rows, w1 = g.shape[4:]
+    w2 = h.shape[2]
+    width = v.shape[2]
+    vmem = pl.BlockSpec(memory_space=pltpu.VMEM)
+    return pl.pallas_call(
+        functools.partial(final_kernel, zs),
+        in_specs=[pl.BlockSpec(memory_space=pl.ANY), vmem, vmem],
+        out_specs=[vmem, vmem, vmem],
+        out_shape=[
+            jax.ShapeDtypeStruct((rows, w1), f32),
+            jax.ShapeDtypeStruct((rows, w2), f32),
+            jax.ShapeDtypeStruct((1, width), f32),
+        ],
+        scratch_shapes=[
+            pltpu.VMEM((zs, rows, w1), bf16),
+            *plane_scratch(zs, rows, w1),
+            pltpu.VMEM((2, 1, width), f32),
+            pltpu.VMEM((2, 1, width), f32),
+            pltpu.VMEM((1, width), f32),
+            pltpu.VMEM((zs, 1, width), f32),
+            pltpu.VMEM((2, 1, width), f32),
+            pltpu.VMEM((2, 1, width), f32),
+            pltpu.SemaphoreType.DMA((zs + 2,)),
+            pltpu.SemaphoreType.DMA((zs + 2,)),
+            *line_scratch(zs, rows, w1),
+            *line_scratch(zs, rows, w2),
+        ],
+        compiler_params=params(collective_id=1, has_side_effects=True),
+        name="final",
+    )(g, h, v)
 
 
 QT = 256
@@ -145,6 +381,30 @@
     )(q, k, v, hide)
 
 
+def attend_sum_kernel(zs, q_ref, k_ref, v_ref, d_ref, p_ref, g_ref, dq_ref, dk_ref, dv_ref, h_ref, ds_s, *plane):
+    step = pl.program_id(0)
+    at = Place(zs)
+
+    @pl.when(step == 0)
+    def _():
+        greet([at.by_core, at.by_x, at.by_y])
+        PlaneSum(at, g_ref, *plane).stage1()
+
+    @pl.when(step == 2)
+    def _():
+        PlaneSum(at, g_ref, *plane).stage2()
+
+    @pl.when(step == 5)
+    def _():
+        PlaneSum(at, g_ref, *plane).stage3()
+
+    attend_back_kernel(q_ref, k_ref, v_ref, d_ref, p_ref, dq_ref, dk_ref, dv_ref, ds_s)
+
+    @pl.when(step == 5)
+    def _():
+        PlaneSum(at, g_ref, *plane).finish(h_ref)
+
+
 def attend_back_kernel(q_ref, k_ref, v_ref, d_ref, p_ref, dq_ref, dk_ref, dv_ref, ds_s):
     vall = v_ref[...]
     kT = k_ref[...].T
@@ -170,9 +430,28 @@
     ).astype(bf16)
 
 
-def attend_back(q, k, v, d, p):
+def attend_back(q, k, v, d, p, zs=0, g=None):
     pair = pl.BlockSpec((LENGTH, 2 * HD), lambda h: (0, h))
     out = jax.ShapeDtypeStruct((LENGTH, D), bf16)
+    if zs:
+        held = (zs,) + g.shape[4:]
+        return pl.pallas_call(
+            functools.partial(attend_sum_kernel, zs),
+            grid=(H // 2,),
+            in_specs=[
+                pair,
+                pair,
+                pair,
+                pair,
+                pl.BlockSpec((2, LENGTH, LENGTH), lambda h: (h, 0, 0)),
+                pl.BlockSpec(memory_space=pl.ANY),
+            ],
+            out_specs=[pair, pair, pair, pl.BlockSpec(held, lambda h: (0, 0, 0))],
+            out_shape=[out, out, out, jax.ShapeDtypeStruct(held, bf16)],
+            scratch_shapes=[pltpu.VMEM((2, LENGTH, LENGTH), bf16), *plane_scratch(*held)],
+            compiler_params=params(collective_id=2, has_side_effects=True),
+            name="attend_sum",
+        )(q, k, v, d, p, g)
     return pl.pallas_call(
         attend_back_kernel,
         grid=(H // 2,),
@@ -523,12 +802,30 @@
     q, k, v = qkv(hidden, w1, vec)
     ctx, p = attend(q, k, v, hide)
     output, resid, dctx, dw2, vs2 = middle(ctx, hidden, cotangent, w2, vec)
-    dq, dk, dv = attend_back(q, k, v, dctx, p)
+    zs = cols_n // 4
+    staged = rows_n == 2 and cols_n % 8 == 0
+    if staged:
+        spread = (2, zs, 2, 2, D // cols_n)
+        g2 = dw2.reshape(spread + (REST_W,))
+        dq, dk, dv, h2 = attend_back(q, k, v, dctx, p, zs, g2)
+    else:
+        dq, dk, dv = attend_back(q, k, v, dctx, p)
     hgrad, dw1, vs1 = last(hidden, dq, dk, dv, resid, w1)
+    vs = jnp.concatenate([vs1, vs2[:, :, 2 * HALF :]], axis=2)
+    if staged:
+        m1, m2, vs = final(zs, dw1.reshape(spread + (QKV_W,)), h2, vs)
+        g_q, g_k, g_v = (m1[:, n * HALF : (n + 1) * HALF] for n in range(3))
+        g_out = m2[:, :HALF].T
+        g_up = m2[:, HALF : HALF + FHALF]
+        g_down = m2[:, HALF + FHALF :].T
+        sums, at = [], 0
+        for width in VEC_HALVES:
+            sums.append(vs[0, at : at + width])
+            at += width
+        return (output, hgrad, g_q, g_k, g_v, g_out, g_up, g_down, *sums)
     g_out, g_up, g_down = scatter_parts(dw2, (HALF, FHALF, FHALF), rows_n, cols_n)
     g_q, g_k, g_v = scatter_parts(dw1, (HALF, HALF, HALF), rows_n, cols_n)
-    vs = jnp.concatenate([vs1, vs2[:, :, 2 * HALF :]], axis=2).reshape(2, VEC_W)
-    vs = lax.psum(vs, ("col", "row"))
+    vs = lax.psum(vs.reshape(2, VEC_W), ("col", "row"))
     row = lax.axis_index("row")
     sums, at = [], 0
     for half in VEC_HALVES:

time: 569 us -> 382 us (0.67)
  waiting for transfers between devices: 285 us -> 82.6 us
  Pallas kernels: 208 us -> 263 us
  blocking collectives: 44.8 us -> 5.49 us
    reduce_scatter x2 -> x0, waiting for transfers between devices: 202 us -> none  [scatter_parts(): lax.psum_scatter(flat, ('row', 'col'), scatter_dimension=0, tiled=True)]
    pallas_call x1 -> x2, Pallas kernels: 60.6 us -> 116 us  [the longest x1 72.7 us: attend_back(): pl.pallas_call(functools.partial(attend_sum_kernel, zs), grid=(H // 2,),...]
    psum x1 -> x0, blocking collectives: 39.4 us -> none  [on_device(): vs = lax.psum(vs, ('col', 'row'))]
  transfers between devices with their start and end apart: 4 -> 2, of which waited for: 4 -> 2; matrix products, arithmetic and copies ran while one was open for 2% -> 1% of each run, Pallas kernels for 11% -> 16%
where the time goes in v3:
time: 382 us
  Pallas kernels  263 us (69%)
  waiting for transfers between devices  82.6 us (22%)
  between operations  14.3 us (4%)
  local copies, waits for them, and re-layouts  11.2 us (3%)
  blocking collectives  5.49 us (1%)
  other arithmetic  4.81 us (1%)
    all_gather x2, waiting for transfers between devices, gather_parts(): every = lax.all_gather(packed, ('row', 'col'), axis=0, tiled=True)  82.6 us
    pallas_call x1, Pallas kernels, attend_back(): pl.pallas_call(functools.partial(attend_sum_kernel, zs), grid=(H // 2,),...  72.7 us
    pallas_call x1, Pallas kernels, middle(): pl.pallas_call(mid_kernel, grid=(TSTEPS + 2 * TILES,), in_specs=[pl.Block...  68.3 us
    pallas_call x1, Pallas kernels, attend(): pl.pallas_call(attend_kernel, grid=(H // 2,), in_specs=[pair, pair, pair,...  50.3 us
    pallas_call x1, Pallas kernels, final(): pl.pallas_call(functools.partial(final_kernel, zs), in_specs=[pl.BlockSpe...  43.1 us
    pallas_call x1, Pallas kernels, last(): pl.pallas_call(last_kernel, grid=(LSTEPS + 6,), in_specs=[whole, whole, w...  18.4 us
    pallas_call x1, Pallas kernels, qkv(): pl.pallas_call(qkv_kernel, grid=(2, 3), in_specs=[pl.BlockSpec((LENGTH, D...  10.2 us
  transfers between devices with their start and end apart: 2, of which 2 were waited for; matrix products, arithmetic and copies ran while one was open for 1% of the time, Pallas kernels for 16%

profile of v3, /device:TPU:0, one launch (start us, length us, event | category | flops | bytes accessed | tf_op | source)
XLA Modules:
  0.0 381.6 jit_solution(13475712400049276664)
XLA Ops:
  7.2 0.0 all-gather.4.cloned.1.call-start
  7.2 1.5 pad_maximum_fusion.1
  8.7 0.0 all-gather.4.cloned.1.call-update
  8.7 0.0 all-gather.6.cloned.1.call-start
  8.8 1.7 pad_maximum_fusion
  10.5 0.0 all-gather.6.cloned.1.call-update
  10.5 0.7 copy.40
  11.3 0.1 fusion
  11.4 0.1 fusion.1
  11.5 0.1 copy.37
  11.6 0.5 broadcast_in_dim.17
  12.1 0.0 copy-start.2
  12.1 0.0 copy-start.3
  12.2 0.0 copy-start.5
  12.2 0.0 copy-start.6
  12.2 1.3 reshape.253.hide_ref
  13.8 5.5 %all-gather.vec_ref = f32[2,1,4608]{2,1,0:T(1,128)} all-gather(f32[1,1,4608]{2,1,0:T(1,128)S(1)} %bitcast_convert_fusion), channel_id=1, replica_groups=mesh['col'=16,'row'=2] {'row'}, dimensions={0}, use_global_device_ids=true | all-gather | bytes 55296 | tf_op jit(solution)/shard_map/all_gather | solution.py:790
  19.2 54.9 %all-gather.4.cloned.1.call-done = bf16[1536,1152]{1,0:T(8,128)(2,1)} async-done(((bf16[48,1152]{1,0:T(8,128)(2,1)}), bf16[1536,1152]{1,0:T(8,128)(2,1)}) %all-gather.4.cloned.1.call-update) | async-done | bytes 3538960 | tf_op jit(solution)/shard_map/all_gather | solution.py:741
  74.1 10.2 %qkv.1 = (bf16[1024,768]{1,0:T(8,128)(2,1)}, bf16[1024,768]{1,0:T(8,128)(2,1)}, bf16[1024,768]{1,0:T(8,128)(2,1)}) custom-call(bf16[1024,768]{1,0:T(8,128)(2,1)} %hid_ref.3, bf16[2,768,1152]{2,1,0:T(8,128)(2,1)} %bitcast.19, f32[2,1,4608]{2,1,0:T(1,128)} %all-gather.vec_ref), custom_call_target="tpu_custom_call" | custom-call | tf_op jit(solution)/shard_map/qkv/pallas_call | solution.py:73
  84.3 50.3 %attend.1 = (bf16[1024,768]{1,0:T(8,128)(2,1)}, bf16[12,1024,1024]{2,1,0:T(8,128)(2,1)}) custom-call(bf16[1024,768]{1,0:T(8,128)(2,1)} %get-tuple-element.37.q_ref, bf16[1024,768]{1,0:T(8,128)(2,1)} %get-tuple-element.38.k_ref, bf16[1024,768]{1,0:T(8,128)(2,1)} %get-tuple-element.39.v_ref, f32[12,16,1024]{2,1,0:T(8,128)} %reshape.253.hide_ref), custom_call_target="tpu_custom_call" | custom-call | tf_op jit(solution)/shard_map/attend/pallas_call | solution.py:370
  134.7 27.7 %all-gather.6.cloned.1.call-done = bf16[1536,3456]{1,0:T(8,128)(2,1)} async-done(((bf16[48,3456]{1,0:T(8,128)(2,1)}), bf16[1536,3456]{1,0:T(8,128)(2,1)}) %all-gather.6.cloned.1.call-update) | async-done | bytes 10616848 | tf_op jit(solution)/shard_map/all_gather | solution.py:741
  162.4 68.3 %middle.1 = (f32[1024,768]{1,0:T(8,128)}, f32[1024,768]{1,0:T(8,128)}, bf16[1024,768]{1,0:T(8,128)(2,1)}, bf16[2,768,3456]{2,1,0:T(8,128)(2,1)}, f32[2,1,4608]{2,1,0:T(1,128)}) custom-call(bf16[1024,768]{1,0:T(8,128)(2,1)} %get-tuple-element.40.ctx_ref, bf16[1024,768]{1,0:T(8,128)(2,1)} %hid_ref.3, bf16[1024,768]{1,0:T(8,128)(2,1)} %cot_ref.1, ...), custom_call_target="tpu_custom_call" | custom-call | tf_op jit(solution)/shard_map/middle/pallas_call | solution.py:631
  230.7 0.8 slice.48
  231.4 72.7 %attend_sum.1 = (bf16[1024,768]{1,0:T(8,128)(2,1)}, bf16[1024,768]{1,0:T(8,128)(2,1)}, bf16[1024,768]{1,0:T(8,128)(2,1)}, bf16[4,48,3456]{2,1,0:T(8,128)(2,1)}) custom-call(bf16[1024,768]{1,0:T(8,128)(2,1)} %get-tuple-element.37.q_ref, bf16[1024,768]{1,0:T(8,128)(2,1)} %get-tuple-element.38.k_ref, bf16[1024,768]{1,0:T(8,128)(2,1)} %get-tuple-element.39.v_ref, ...), custom_call_target="tpu_custom_call" | custom-call | tf_op jit(solution)/shard_map/attend_sum/pallas_call | solution.py:438
  304.1 18.4 %last.1 = (f32[1024,768]{1,0:T(8,128)}, bf16[2,768,1152]{2,1,0:T(8,128)(2,1)}, f32[2,1,768]{2,1,0:T(1,128)}) custom-call(bf16[1024,768]{1,0:T(8,128)(2,1)} %hid_ref.3, bf16[1024,768]{1,0:T(8,128)(2,1)} %get-tuple-element.45.dq_ref, bf16[1024,768]{1,0:T(8,128)(2,1)} %get-tuple-element.46.dk_ref, bf16[1024,768]{1,0:T(8,128)(2,1)} %get-tuple-element.47.dv_ref, ...), custom_call_target="tpu_custom_call" | custom-call | tf_op jit(solution)/shard_map/last/pallas_call | solution.py:712
  322.6 1.3 pad_maximum_fusion.2.v_ref
  323.9 43.1 %final.1 = (f32[48,1152]{1,0:T(8,128)}, f32[48,3456]{1,0:T(8,128)}, f32[1,4608]{1,0:T(1,128)}) custom-call(bf16[2,4,2,2,48,1152]{5,4,3,2,1,0:T(8,128)(2,1)} %bitcast.23, bf16[4,48,3456]{2,1,0:T(8,128)(2,1)} %get-tuple-element.51.h_ref, f32[2,1,4608]{2,1,0:T(1,128)} %pad_maximum_fusion.2.v_ref), custom_call_target="tpu_custom_call" | custom-call | tf_op jit(solution)/shard_map/final/pallas_call | solution.py:296
  367.0 1.3 slice_reduce_fusion
  368.3 1.3 slice_reduce_fusion.1
  369.7 1.5 slice_bitcast_fusion.1
  371.2 1.9 slice_bitcast_fusion
  373.1 1.6 fusion.3
  (27 shorter events, 0.2 us)
Async XLA Ops:
  7.2 66.9 %all-gather.4.cloned.1.call-start = ((), (), s32[]{:S(2)}) async-start(), calls=%async_computation | async-start | bytes 3649536 | tf_op jit(solution)/shard_map/all_gather | solution.py:741
  8.7 153.7 %all-gather.6.cloned.1.call-start = ((), (), s32[]{:S(2)}) async-start(), calls=%async_computation.1 | async-start | bytes 10948608 | tf_op jit(solution)/shard_map/all_gather | solution.py:741
  12.1 1.4 copy-start.1
  12.1 1.4 copy-start.2
  12.1 1.4 copy-start.3
  12.1 1.4 copy-start
  12.2 1.5 copy-start.4
  12.2 1.5 copy-start.5
  12.2 1.5 copy-start.6
  12.2 1.5 copy-start.7
  12.2 1.5 copy-start.8
Sparse Core Ops, SparseCore 0:
  11.5 62.6 all-gather.3
  77.0 85.3 all-gather.5

commit v4 on v3

--- a/solution.py
+++ b/solution.py
@@ -321,6 +321,145 @@
     )(g, h, v)
 
 
+class PlaneGather:
+    def __init__(self, at, h, g, send, recv):
+        self.at, self.h, self.g, self.send, self.recv = at, h, g, send, recv
+
+    def move(self, i, to, src, *where):
+        dst = self.g.at[where]
+        return remote(dst if src is None else src, dst, self.send, self.recv, i, to)
+
+    def stage1(self):
+        at, half = self.at, self.at.zs // 2
+        y, x, core = at.y, at.x, at.core
+        every, low, high = slice(None), slice(0, half), slice(half, at.zs)
+        return (
+            self.move(0, at.by_y, self.h.at[low], y, low, x, core),
+            self.move(1, at.by_x, self.h.at[high], y, high, x, core),
+            self.move(2, at.by_core, self.h, y, every, x, core),
+        )
+
+    def stage2(self):
+        at, half = self.at, self.at.zs // 2
+        y, x, core = at.y, at.x, at.core
+        every, low, high = slice(None), slice(0, half), slice(half, at.zs)
+        return (
+            self.move(3, at.by_x, None, every, low, x, core),
+            self.move(4, at.by_y, None, y, high, every, core),
+            self.move(5, at.by_core, None, 1 - y, low, x, core),
+            self.move(6, at.by_core, None, y, high, 1 - x, core),
+        )
+
+    def stage3(self):
+        at, half = self.at, self.at.zs // 2
+        y, x, core = at.y, at.x, at.core
+        every, low, high = slice(None), slice(0, half), slice(half, at.zs)
+        return (
+            self.move(7, at.by_core, None, every, low, 1 - x, core),
+            self.move(8, at.by_core, None, 1 - y, high, every, core),
+        )
+
+
+def start_all(copies):
+    for copy in copies:
+        copy.start()
+
+
+def wait_all(copies):
+    for copy in copies:
+        copy.wait()
+
+
+def front_kernel(
+    zs, x_ref, s1_ref, s2_ref, vec_ref, q_ref, k_ref, v_ref, g_ref, h_ref, vo_ref, line,
+    psend, precv, lsend, lrecv, vsend, vrecv, local,
+):
+    at = Place(zs)
+    greet([at.by_core, at.by_x, at.by_y] + [at.by_z(d) for d in range(1, zs)])
+    along = [
+        remote(s1_ref, line.at[at.z], lsend, lrecv, d - 1, at.by_z(d)) for d in range(1, zs)
+    ]
+    start_all(along)
+    vec = remote(vec_ref, vo_ref.at[at.y], vsend, vrecv, 0, at.by_y)
+    vec.start()
+    mine = [
+        pltpu.make_async_copy(s1_ref, line.at[at.z], local.at[0]),
+        pltpu.make_async_copy(s2_ref, h_ref.at[at.z], local.at[1]),
+        pltpu.make_async_copy(vec_ref, vo_ref.at[at.y], local.at[2]),
+    ]
+    start_all(mine)
+    wait_all(mine)
+    wait_all(along)
+    after = [
+        remote(s2_ref, h_ref.at[at.z], lsend, lrecv, zs - 2 + d, at.by_z(d)) for d in range(1, zs)
+    ]
+    start_all(after)
+    gather = PlaneGather(at, line, g_ref, psend, precv)
+    keep = pltpu.make_async_copy(line, g_ref.at[at.y, :, at.x, at.core], local.at[3])
+    keep.start()
+    one = gather.stage1()
+    start_all(one)
+    keep.wait()
+    wait_all(one)
+    two = gather.stage2()
+    start_all(two)
+    wait_all(two)
+    three = gather.stage3()
+    start_all(three)
+    vec.wait()
+    wait_all(three)
+
+    @pl.loop(0, LENGTH // QROWS)
+    def _(n):
+        rows = pl.ds(pl.multiple_of(n * QROWS, QROWS), QROWS)
+        x = x_ref[rows, :]
+        for r in range(2):
+            w = g_ref[r].reshape(D, QKV_W)
+            out = slice(r * HALF, (r + 1) * HALF)
+            q = dot(x, w[:, :HALF]) + vo_ref[r, :, V_QB : V_QB + HALF]
+            q_ref[rows, out] = (q.astype(bf16).astype(f32) * 0.125).astype(bf16)
+            k_ref[rows, out] = dot(x, w[:, HALF : 2 * HALF]).astype(bf16)
+            v = dot(x, w[:, 2 * HALF :]) + vo_ref[r, :, V_VB : V_VB + HALF]
+            v_ref[rows, out] = v.astype(bf16)
+
+    wait_all(after)
+
+
+QROWS = 256
+
+
+def front(zs, x, s1, s2, vec):
+    rows = s1.shape[0]
+    w1, w2 = s1.shape[1], s2.shape[1]
+    vmem = pl.BlockSpec(memory_space=pltpu.VMEM)
+    out = jax.ShapeDtypeStruct((LENGTH, D), bf16)
+    return pl.pallas_call(
+        functools.partial(front_kernel, zs),
+        in_specs=[vmem] * 4,
+        out_specs=[vmem] * 6,
+        out_shape=[
+            out,
+            out,
+            out,
+            jax.ShapeDtypeStruct((2, zs, 2, 2, rows, w1), bf16),
+            jax.ShapeDtypeStruct((zs, rows, w2), bf16),
+            jax.ShapeDtypeStruct((2, 1, VEC_W), f32),
+        ],
+        scratch_shapes=[
+            pltpu.VMEM((zs, rows, w1), bf16),
+            pltpu.SemaphoreType.DMA((9,)),
+            pltpu.SemaphoreType.DMA((9,)),
+            pltpu.SemaphoreType.DMA((2 * zs - 2,)),
+            pltpu.SemaphoreType.DMA((2 * zs - 2,)),
+            pltpu.SemaphoreType.DMA((1,)),
+            pltpu.SemaphoreType.DMA((1,)),
+            pltpu.SemaphoreType.DMA((4,)),
+        ],
+        compiler_params=params(collective_id=3, has_side_effects=True),
+        name="front",
+    )(x, s1, s2, vec)
+
+
 QT = 256
 QTILES = LENGTH // QT
 
@@ -365,8 +504,66 @@
         c_ref[at, :] = both_heads(*outs).T.astype(bf16)
 
 
-def attend(q, k, v, hide):
+def attend_gather_kernel(zs, q_ref, k_ref, v_ref, hide_ref, h_ref, c_ref, p_ref, g_ref, send, recv, local):
+    step = pl.program_id(0)
+    at = Place(zs)
+    gather = PlaneGather(at, h_ref, g_ref, send, recv)
+
+    def keep():
+        return pltpu.make_async_copy(h_ref, g_ref.at[at.y, :, at.x, at.core], local)
+
+    @pl.when(step == 0)
+    def _():
+        greet([at.by_core, at.by_x, at.by_y])
+        start_all(gather.stage1())
+        keep().start()
+
+    @pl.when(step == 2)
+    def _():
+        keep().wait()
+        wait_all(gather.stage1())
+        start_all(gather.stage2())
+
+    attend_kernel(q_ref, k_ref, v_ref, hide_ref, c_ref, p_ref)
+
+    @pl.when(step == H // 2 - 1)
+    def _():
+        wait_all(gather.stage2())
+        start_all(gather.stage3())
+        wait_all(gather.stage3())
+
+
+def attend(q, k, v, hide, zs=0, h2=None):
     pair = pl.BlockSpec((LENGTH, 2 * HD), lambda h: (0, h))
+    if zs:
+        return pl.pallas_call(
+            functools.partial(attend_gather_kernel, zs),
+            grid=(H // 2,),
+            in_specs=[
+                pair,
+                pair,
+                pair,
+                pl.BlockSpec((2, BLOCKS, LENGTH), lambda h: (h, 0, 0)),
+                pl.BlockSpec(memory_space=pltpu.VMEM),
+            ],
+            out_specs=[
+                pair,
+                pl.BlockSpec((2, LENGTH, LENGTH), lambda h: (h, 0, 0)),
+                pl.BlockSpec(memory_space=pl.ANY),
+            ],
+            out_shape=[
+                jax.ShapeDtypeStruct((LENGTH, D), bf16),
+                jax.ShapeDtypeStruct((H, LENGTH, LENGTH), bf16),
+                jax.ShapeDtypeStruct((2, zs, 2, 2) + h2.shape[1:], bf16),
+            ],
+            scratch_shapes=[
+                pltpu.SemaphoreType.DMA((9,)),
+                pltpu.SemaphoreType.DMA((9,)),
+                pltpu.SemaphoreType.DMA,
+            ],
+            compiler_params=params(collective_id=4, has_side_effects=True),
+            name="attend_gather",
+        )(q, k, v, hide, h2)
     return pl.pallas_call(
         attend_kernel,
         grid=(H // 2,),
@@ -787,23 +984,31 @@
     w_down,
     *vectors,
 ):
-    vec = lax.all_gather(jnp.concatenate(vectors).astype(f32), "row", axis=0, tiled=False)
-    if rows_n != 2:
-        pieces, at = [], 0
-        for half in VEC_HALVES:
-            width = half * 2 // rows_n
-            pieces.append(vec[:, at : at + width].reshape(2, half))
-            at += width
-        vec = jnp.concatenate(pieces, axis=1)
-    vec = vec.reshape(2, 1, VEC_W)
-    w1 = gather_parts([w_query, w_key, w_value], rows_n, cols_n)
-    w2 = gather_parts([w_out.T, w_up, w_down.T], rows_n, cols_n)
-    hide = hidden_pairs(rand_blocks[0])
-    q, k, v = qkv(hidden, w1, vec)
-    ctx, p = attend(q, k, v, hide)
-    output, resid, dctx, dw2, vs2 = middle(ctx, hidden, cotangent, w2, vec)
     zs = cols_n // 4
     staged = rows_n == 2 and cols_n % 8 == 0
+    hide = hidden_pairs(rand_blocks[0])
+    if staged:
+        vec = jnp.concatenate(vectors).astype(f32)[None]
+        s1 = jnp.concatenate([w_query, w_key, w_value], axis=1)
+        s2 = jnp.concatenate([w_out.T, w_up, w_down.T], axis=1)
+        q, k, v, w1, h2, vec = front(zs, hidden, s1, s2, vec)
+        ctx, p, w2 = attend(q, k, v, hide, zs, h2)
+        w1, w2 = w1.reshape(2, D, QKV_W), w2.reshape(2, D, REST_W)
+    else:
+        vec = lax.all_gather(jnp.concatenate(vectors).astype(f32), "row", axis=0, tiled=False)
+        if rows_n != 2:
+            pieces, at = [], 0
+            for half in VEC_HALVES:
+                width = half * 2 // rows_n
+                pieces.append(vec[:, at : at + width].reshape(2, half))
+                at += width
+            vec = jnp.concatenate(pieces, axis=1)
+        vec = vec.reshape(2, 1, VEC_W)
+        w1 = gather_parts([w_query, w_key, w_value], rows_n, cols_n)
+        w2 = gather_parts([w_out.T, w_up, w_down.T], rows_n, cols_n)
+        q, k, v = qkv(hidden, w1, vec)
+        ctx, p = attend(q, k, v, hide)
+    output, resid, dctx, dw2, vs2 = middle(ctx, hidden, cotangent, w2, vec)
     if staged:
         spread = (2, zs, 2, 2, D // cols_n)
         g2 = dw2.reshape(spread + (REST_W,))

time: 382 us -> 335 us (0.88)
  waiting for transfers between devices: 82.6 us -> 0 us
  Pallas kernels: 263 us -> 312 us
  between operations: 14.3 us -> 0.75 us
  blocking collectives: 5.49 us -> 0 us
  local copies, waits for them, and re-layouts: 11.2 us -> 16.5 us
    all_gather x2 -> x0, waiting for transfers between devices: 82.6 us -> none  [gather_parts(): every = lax.all_gather(packed, ('row', 'col'), axis=0, tiled=True)]
    pallas_call x2, Pallas kernels: 60.6 us -> 102 us  [the longest x1 58.1 us: attend(): pl.pallas_call(functools.partial(attend_gather_kernel, zs), grid=(H // 2,...]
    pallas_call x1, Pallas kernels: 43.1 us -> 49.9 us  [final(): pl.pallas_call(functools.partial(final_kernel, zs), in_specs=[pl.BlockSpe...]
    all_gather x1 -> x0, blocking collectives: 5.49 us -> none  [on_device(): lax.all_gather(jnp.concatenate(vectors).astype(f32), 'row', axis=0, tiled...]
    unnamed x27 -> x11, local copies, waits for them, and re-layouts: 0.87 us -> 6.24 us
  transfers between devices with their start and end apart: 2 -> 0, of which waited for: 2 -> 0; matrix products, arithmetic and copies ran while one was open for 1% -> 0% of each run, Pallas kernels for 16% -> 0%
where the time goes in v4:
time: 335 us
  Pallas kernels  312 us (93%)
  local copies, waits for them, and re-layouts  16.5 us (5%)
  other arithmetic  5.43 us (2%)
    pallas_call x1, Pallas kernels, attend_back(): pl.pallas_call(functools.partial(attend_sum_kernel, zs), grid=(H // 2,),...  72.9 us
    pallas_call x1, Pallas kernels, middle(): pl.pallas_call(mid_kernel, grid=(TSTEPS + 2 * TILES,), in_specs=[pl.Block...  68.5 us
    pallas_call x1, Pallas kernels, attend(): pl.pallas_call(functools.partial(attend_gather_kernel, zs), grid=(H // 2,...  58.1 us
    pallas_call x1, Pallas kernels, final(): pl.pallas_call(functools.partial(final_kernel, zs), in_specs=[pl.BlockSpe...  49.9 us
    pallas_call x1, Pallas kernels, front(): pl.pallas_call(functools.partial(front_kernel, zs), in_specs=[vmem] * 4,...  44.1 us
    pallas_call x1, Pallas kernels, last(): pl.pallas_call(last_kernel, grid=(LSTEPS + 6,), in_specs=[whole, whole, w...  18.4 us

profile of v4, /device:TPU:0, one launch (start us, length us, event | category | flops | bytes accessed | tf_op | source)
XLA Modules:
  0.0 334.6 jit_solution(13568994213454895317)
XLA Ops:
  0.7 0.1 fusion.1
  0.8 0.7 constant_dynamic-update-slice_fusion.8
  1.4 0.7 constant_dynamic-update-slice_fusion.7
  2.1 0.7 constant_dynamic-update-slice_fusion.6
  2.8 0.7 constant_dynamic-update-slice_fusion.5
  3.5 0.7 constant_dynamic-update-slice_fusion.4
  4.2 0.7 constant_dynamic-update-slice_fusion.3
  4.9 0.7 constant_dynamic-update-slice_fusion.2
  5.6 0.7 constant_dynamic-update-slice_fusion.1
  6.3 0.7 constant_dynamic-update-slice_fusion
  7.0 0.6 convert_element_type.12.vec_ref
  7.6 0.7 copy.39
  8.3 0.1 fusion
  8.5 0.1 copy.36
  8.6 1.5 pad_maximum_fusion.1.s1_ref
  10.0 1.7 pad_maximum_fusion.s2_ref
  11.8 0.5 broadcast_in_dim.18
  12.3 1.3 reshape.248.hide_ref
  13.6 44.1 %front.1 = (bf16[1024,768]{1,0:T(8,128)(2,1)}, bf16[1024,768]{1,0:T(8,128)(2,1)}, bf16[1024,768]{1,0:T(8,128)(2,1)}, bf16[2,4,2,2,48,1152]{5,4,3,2,1,0:T(8,128)(...) custom-call(bf16[1024,768]{1,0:T(8,128)(2,1)} %hid_ref.3, bf16[48,1152]{1,0:T(8,128)(2,1)} %pad_maximum_fusion.1.s1_ref, ...), custom_call_target="tpu_custom_call" | custom-call | tf_op jit(solution)/shard_map/front/pallas_call | solution.py:436
  57.6 58.1 %attend_gather.1 = (bf16[1024,768]{1,0:T(8,128)(2,1)}, bf16[12,1024,1024]{2,1,0:T(8,128)(2,1)}, bf16[2,4,2,2,48,3456]{5,4,3,2,1,0:T(8,128)(2,1)}) custom-call(bf16[1024,768]{1,0:T(8,128)(2,1)} %get-tuple-element.41.q_ref, bf16[1024,768]{1,0:T(8,128)(2,1)} %get-tuple-element.42.k_ref, bf16[1024,768]{1,0:T(8,128)(2,1)} %get-tuple-element.43.v_ref, ...), custom_call_target="tpu_custom_call" | custom-call | tf_op jit(solution)/shard_map/attend_gather/pallas_call | solution.py:539
  115.7 68.5 %middle.1 = (f32[1024,768]{1,0:T(8,128)}, f32[1024,768]{1,0:T(8,128)}, bf16[1024,768]{1,0:T(8,128)(2,1)}, bf16[2,768,3456]{2,1,0:T(8,128)(2,1)}, f32[2,1,4608]{2,1,0:T(1,128)}) custom-call(bf16[1024,768]{1,0:T(8,128)(2,1)} %get-tuple-element.45.ctx_ref, bf16[1024,768]{1,0:T(8,128)(2,1)} %hid_ref.3, bf16[1024,768]{1,0:T(8,128)(2,1)} %cot_ref.1, ...), custom_call_target="tpu_custom_call" | custom-call | tf_op jit(solution)/shard_map/middle/pallas_call | solution.py:828
  184.2 72.9 %attend_sum.1 = (bf16[1024,768]{1,0:T(8,128)(2,1)}, bf16[1024,768]{1,0:T(8,128)(2,1)}, bf16[1024,768]{1,0:T(8,128)(2,1)}, bf16[4,48,3456]{2,1,0:T(8,128)(2,1)}) custom-call(bf16[1024,768]{1,0:T(8,128)(2,1)} %get-tuple-element.41.q_ref, bf16[1024,768]{1,0:T(8,128)(2,1)} %get-tuple-element.42.k_ref, bf16[1024,768]{1,0:T(8,128)(2,1)} %get-tuple-element.43.v_ref, ...), custom_call_target="tpu_custom_call" | custom-call | tf_op jit(solution)/shard_map/attend_sum/pallas_call | solution.py:635
  257.2 0.0 copy-start
  257.2 18.4 %last.1 = (f32[1024,768]{1,0:T(8,128)}, bf16[2,768,1152]{2,1,0:T(8,128)(2,1)}, f32[2,1,768]{2,1,0:T(1,128)}) custom-call(bf16[1024,768]{1,0:T(8,128)(2,1)} %hid_ref.3, bf16[1024,768]{1,0:T(8,128)(2,1)} %get-tuple-element.52.dq_ref, bf16[1024,768]{1,0:T(8,128)(2,1)} %get-tuple-element.53.dk_ref, bf16[1024,768]{1,0:T(8,128)(2,1)} %get-tuple-element.54.dv_ref, ...), custom_call_target="tpu_custom_call" | custom-call | tf_op jit(solution)/shard_map/last/pallas_call | solution.py:909
  275.6 0.0 copy-done
  275.6 1.3 pad_maximum_fusion.2.v_ref
  277.0 49.9 %final.1 = (f32[48,1152]{1,0:T(8,128)}, f32[48,3456]{1,0:T(8,128)}, f32[1,4608]{1,0:T(1,128)}) custom-call(bf16[2,4,2,2,48,1152]{5,4,3,2,1,0:T(8,128)(2,1)} %bitcast.19, bf16[4,48,3456]{2,1,0:T(8,128)(2,1)} %get-tuple-element.59.h_ref, f32[2,1,4608]{2,1,0:T(1,128)} %pad_maximum_fusion.2.v_ref), custom_call_target="tpu_custom_call" | custom-call | tf_op jit(solution)/shard_map/final/pallas_call | solution.py:296
  326.9 1.6 fusion.3
  328.6 1.3 slice_reduce_fusion
  329.9 1.3 slice_reduce_fusion.1
  331.2 1.5 slice_bitcast_fusion.1
  332.7 1.9 slice_bitcast_fusion
  (4 shorter events, 0.0 us)
Async XLA Ops:
  257.2 18.4 %copy-start = (f32[2,1,4608]{2,1,0:T(1,128)S(1)}, f32[2,1,4608]{2,1,0:T(1,128)}, u32[]{:S(2)}) copy-start(f32[2,1,4608]{2,1,0:T(1,128)} %get-tuple-element.61) | copy-start | bytes 110596

commit v5 on v4

--- a/solution.py
+++ b/solution.py
@@ -172,19 +172,22 @@
         )
 
     def stage1(self):
-        self.keep().start()
+        if self.own is not None:
+            self.keep().start()
         self.to_core().start()
 
     def stage2(self):
-        self.keep().wait()
+        if self.own is not None:
+            self.keep().wait()
         self.to_core().wait()
-        b1, own = self.b1, self.own
+        b1, own, core = self.b1, self.own, self.at.core
 
         @pl.loop(0, self.at.zs)
         def _(z):
             for y in range(2):
                 for x in range(2):
-                    b1[y, z, x] = add_low(b1[y, z, x], own[y, z, x])
+                    mine = self.g[y, z, x, core] if own is None else own[y, z, x]
+                    b1[y, z, x] = add_low(b1[y, z, x], mine)
 
         for copy in self.second():
             copy.start()
@@ -241,84 +244,6 @@
         for d in range(1, self.at.zs):
             total = total + self.held[d - 1].astype(f32)
         out[...] = total
-
-
-def final_kernel(zs, g_ref, h_ref, v_ref, o1_ref, o2_ref, vo_ref, mid, *scratch):
-    plane, (v1, v2, v3, v4, va, vb, vsend, vrecv), line1, line2 = (
-        scratch[:9],
-        scratch[9:17],
-        scratch[17:20],
-        scratch[20:23],
-    )
-    at = Place(zs)
-    greet([at.by_core, at.by_x, at.by_y] + [at.by_z(d) for d in range(1, zs)])
-    first = PlaneSum(at, g_ref, *plane)
-    second = LineSum(at, h_ref, *line2)
-    first.stage1()
-    vec1 = remote(v_ref, v1, vsend, vrecv, 0, at.by_core)
-    vec1.start()
-    second.start()
-    vec1.wait()
-    va[...] = v_ref[...] + v1[...]
-    vec2 = remote(va, v2, vsend, vrecv, 1, at.by_x)
-    vec2.start()
-    first.stage2()
-    vec2.wait()
-    vb[...] = va[...] + v2[...]
-    vec3 = remote(vb.at[1 - at.y], v3, vsend, vrecv, 2, at.by_y)
-    vec3.start()
-    first.stage3()
-    vec3.wait()
-    v4[0] = vb[at.y] + v3[...]
-    vec4 = [
-        remote(v4.at[0], v4.at[d], vsend, vrecv, 2 + d, at.by_z(d)) for d in range(1, zs)
-    ]
-    for copy in vec4:
-        copy.start()
-    first.finish(mid)
-    third = LineSum(at, mid, *line1)
-    third.start()
-    for copy in vec4:
-        copy.wait()
-    total = v4[at.z % zs]
-    for z in range(1, zs):
-        total = total + v4[(at.z + zs - z) % zs]
-    vo_ref[...] = total
-    second.finish(o2_ref)
-    third.finish(o1_ref)
-
-
-def final(zs, g, h, v):
-    rows, w1 = g.shape[4:]
-    w2 = h.shape[2]
-    width = v.shape[2]
-    vmem = pl.BlockSpec(memory_space=pltpu.VMEM)
-    return pl.pallas_call(
-        functools.partial(final_kernel, zs),
-        in_specs=[pl.BlockSpec(memory_space=pl.ANY), vmem, vmem],
-        out_specs=[vmem, vmem, vmem],
-        out_shape=[
-            jax.ShapeDtypeStruct((rows, w1), f32),
-            jax.ShapeDtypeStruct((rows, w2), f32),
-            jax.ShapeDtypeStruct((1, width), f32),
-        ],
-        scratch_shapes=[
-            pltpu.VMEM((zs, rows, w1), bf16),
-            *plane_scratch(zs, rows, w1),
-            pltpu.VMEM((2, 1, width), f32),
-            pltpu.VMEM((2, 1, width), f32),
-            pltpu.VMEM((1, width), f32),
-            pltpu.VMEM((zs, 1, width), f32),
-            pltpu.VMEM((2, 1, width), f32),
-            pltpu.VMEM((2, 1, width), f32),
-            pltpu.SemaphoreType.DMA((zs + 2,)),
-            pltpu.SemaphoreType.DMA((zs + 2,)),
-            *line_scratch(zs, rows, w1),
-            *line_scratch(zs, rows, w2),
-        ],
-        compiler_params=params(collective_id=1, has_side_effects=True),
-        name="final",
-    )(g, h, v)
 
 
 class PlaneGather:
@@ -371,27 +296,39 @@
 
 
 def front_kernel(
-    zs, x_ref, s1_ref, s2_ref, vec_ref, q_ref, k_ref, v_ref, g_ref, h_ref, vo_ref, line,
-    psend, precv, lsend, lrecv, vsend, vrecv, local,
+    zs, x_ref, wq_ref, wk_ref, wv_ref, wo_ref, wu_ref, wd_ref, *refs,
 ):
+    vector_refs, refs = refs[:9], refs[9:]
+    q_ref, k_ref, v_ref, g_ref, h_ref, vo_ref, line, s2, vec_s = refs[:9]
+    psend, precv, lsend, lrecv, vsend, vrecv, local = refs[9:]
     at = Place(zs)
+    mine = [
+        pltpu.make_async_copy(ref, line.at[at.z, :, n * HALF : (n + 1) * HALF], local.at[n])
+        for n, ref in enumerate((wq_ref, wk_ref, wv_ref))
+    ]
+    start_all(mine)
     greet([at.by_core, at.by_x, at.by_y] + [at.by_z(d) for d in range(1, zs)])
+    wait_all(mine)
     along = [
-        remote(s1_ref, line.at[at.z], lsend, lrecv, d - 1, at.by_z(d)) for d in range(1, zs)
+        remote(line.at[at.z], line.at[at.z], lsend, lrecv, d - 1, at.by_z(d))
+        for d in range(1, zs)
     ]
     start_all(along)
-    vec = remote(vec_ref, vo_ref.at[at.y], vsend, vrecv, 0, at.by_y)
+    off = 0
+    for ref in vector_refs:
+        width = ref.shape[0]
+        vec_s[:, off : off + width] = ref[...].astype(f32).reshape(1, width)
+        off += width
+    s2[:, :HALF] = wo_ref[...].T
+    s2[:, HALF : HALF + FHALF] = wu_ref[...]
+    s2[:, HALF + FHALF :] = wd_ref[...].T
+    vo_ref[at.y] = vec_s[...]
+    h_ref[at.z] = s2[...]
+    vec = remote(vec_s, vo_ref.at[at.y], vsend, vrecv, 0, at.by_y)
     vec.start()
-    mine = [
-        pltpu.make_async_copy(s1_ref, line.at[at.z], local.at[0]),
-        pltpu.make_async_copy(s2_ref, h_ref.at[at.z], local.at[1]),
-        pltpu.make_async_copy(vec_ref, vo_ref.at[at.y], local.at[2]),
-    ]
-    start_all(mine)
-    wait_all(mine)
     wait_all(along)
     after = [
-        remote(s2_ref, h_ref.at[at.z], lsend, lrecv, zs - 2 + d, at.by_z(d)) for d in range(1, zs)
+        remote(s2, h_ref.at[at.z], lsend, lrecv, zs - 2 + d, at.by_z(d)) for d in range(1, zs)
     ]
     start_all(after)
     gather = PlaneGather(at, line, g_ref, psend, precv)
@@ -428,14 +365,14 @@
 QROWS = 256
 
 
-def front(zs, x, s1, s2, vec):
-    rows = s1.shape[0]
-    w1, w2 = s1.shape[1], s2.shape[1]
+def front(zs, x, weights, vectors):
+    rows = weights[0].shape[0]
+    w1, w2 = QKV_W, REST_W
     vmem = pl.BlockSpec(memory_space=pltpu.VMEM)
     out = jax.ShapeDtypeStruct((LENGTH, D), bf16)
     return pl.pallas_call(
         functools.partial(front_kernel, zs),
-        in_specs=[vmem] * 4,
+        in_specs=[vmem] * 16,
         out_specs=[vmem] * 6,
         out_shape=[
             out,
@@ -447,6 +384,8 @@
         ],
         scratch_shapes=[
             pltpu.VMEM((zs, rows, w1), bf16),
+            pltpu.VMEM((rows, w2), bf16),
+            pltpu.VMEM((1, VEC_W), f32),
             pltpu.SemaphoreType.DMA((9,)),
             pltpu.SemaphoreType.DMA((9,)),
             pltpu.SemaphoreType.DMA((2 * zs - 2,)),
@@ -457,7 +396,7 @@
         ],
         compiler_params=params(collective_id=3, has_side_effects=True),
         name="front",
-    )(x, s1, s2, vec)
+    )(x, *weights, *vectors)
 
 
 QT = 256
@@ -933,6 +872,134 @@
     )(hid, dq, dk, dv, resid, w)
 
 
+def last_sum_kernel(
+    zs, hid_ref, dq_ref, dk_ref, dv_ref, resid_ref, w_ref, h_ref, v_ref,
+    hg_ref, o1_ref, o2_ref, vo_ref,
+    hT, g, w, resid, vs, mid, local, *scratch,
+):
+    plane, (v1, v2, v3, v4, va, vb, vsend, vrecv), line1, line2 = (
+        scratch[:7],
+        scratch[7:15],
+        scratch[15:18],
+        scratch[18:21],
+    )
+    at = Place(zs)
+    loads = [
+        pltpu.make_async_copy(w_ref, w, local.at[0]),
+        pltpu.make_async_copy(resid_ref, resid, local.at[1]),
+    ]
+    start_all(loads)
+    greet([at.by_core, at.by_x, at.by_y] + [at.by_z(d) for d in range(1, zs)])
+    first = PlaneSum(at, g, None, *plane, None)
+    second = LineSum(at, h_ref, *line2)
+    second.start()
+
+    hT[...] = hid_ref[...].T
+    half = zs // 2
+
+    @pl.loop(0, 2)
+    def _(n):
+        rows = hT[pl.ds(pl.multiple_of(n * HALF, HALF), HALF), :]
+        for r in range(2):
+            for m, ref in enumerate((dq_ref, dk_ref, dv_ref)):
+                tile = dot(rows, ref[:, r * HALF : (r + 1) * HALF]).astype(bf16)
+                g[r, pl.ds(n * half, half), :, :, :, m * HALF : (m + 1) * HALF] = tile.reshape(
+                    (half,) + g.shape[2:5] + (HALF,)
+                )
+
+    first.stage1()
+    vs[...] = v_ref[...]
+    for ref, off in ((dq_ref, V_QB), (dv_ref, V_VB)):
+        total = jnp.sum(ref[...].astype(f32), axis=0, keepdims=True)
+        vs[0, :, off : off + HALF] = total[:, :HALF]
+        vs[1, :, off : off + HALF] = total[:, HALF:]
+    vec1 = remote(vs, v1, vsend, vrecv, 0, at.by_core)
+    vec1.start()
+    wait_all(loads)
+
+    def input_grad(n):
+        rows = pl.ds(pl.multiple_of(n * QROWS, QROWS), QROWS)
+        acc = resid[rows, :]
+        for m, ref in enumerate((dq_ref, dk_ref, dv_ref)):
+            for r in range(2):
+                acc = acc + dot_nt(
+                    ref[rows, r * HALF : (r + 1) * HALF], w[r, :, m * HALF : (m + 1) * HALF]
+                )
+        hg_ref[rows, :] = acc
+
+    tiles = LENGTH // QROWS
+    pl.loop(0, tiles // 2)(input_grad)
+    vec1.wait()
+    va[...] = vs[...] + v1[...]
+    vec2 = remote(va, v2, vsend, vrecv, 1, at.by_x)
+    vec2.start()
+    first.stage2()
+    pl.loop(tiles // 2, tiles)(input_grad)
+    vec2.wait()
+    vb[...] = va[...] + v2[...]
+    vec3 = remote(vb.at[1 - at.y], v3, vsend, vrecv, 2, at.by_y)
+    vec3.start()
+    first.stage3()
+    vec3.wait()
+    v4[0] = vb[at.y] + v3[...]
+    vec4 = [
+        remote(v4.at[0], v4.at[d], vsend, vrecv, 2 + d, at.by_z(d)) for d in range(1, zs)
+    ]
+    start_all(vec4)
+    second.finish(o2_ref)
+    first.finish(mid)
+    third = LineSum(at, mid, *line1)
+    third.start()
+    wait_all(vec4)
+    total = v4[at.z % zs]
+    for z in range(1, zs):
+        total = total + v4[(at.z + zs - z) % zs]
+    vo_ref[...] = total
+    third.finish(o1_ref)
+
+
+def last_sum(zs, hid, dq, dk, dv, resid, w, h, v):
+    rows = D // (4 * zs)
+    w1 = w.shape[2]
+    w2 = h.shape[2]
+    width = v.shape[2]
+    vmem = pl.BlockSpec(memory_space=pltpu.VMEM)
+    far = pl.BlockSpec(memory_space=pl.ANY)
+    return pl.pallas_call(
+        functools.partial(last_sum_kernel, zs),
+        in_specs=[vmem, vmem, vmem, vmem, far, far, vmem, vmem],
+        out_specs=[vmem] * 4,
+        out_shape=[
+            jax.ShapeDtypeStruct((LENGTH, D), f32),
+            jax.ShapeDtypeStruct((rows, w1), f32),
+            jax.ShapeDtypeStruct((rows, w2), f32),
+            jax.ShapeDtypeStruct((1, width), f32),
+        ],
+        scratch_shapes=[
+            pltpu.VMEM((D, LENGTH), bf16),
+            pltpu.VMEM((2, zs, 2, 2, rows, w1), bf16),
+            pltpu.VMEM(w.shape, bf16),
+            pltpu.VMEM((LENGTH, D), f32),
+            pltpu.VMEM((2, 1, width), f32),
+            pltpu.VMEM((zs, rows, w1), bf16),
+            pltpu.SemaphoreType.DMA((2,)),
+            *plane_scratch(zs, rows, w1)[1:-1],
+            pltpu.VMEM((2, 1, width), f32),
+            pltpu.VMEM((2, 1, width), f32),
+            pltpu.VMEM((1, width), f32),
+            pltpu.VMEM((zs, 1, width), f32),
+            pltpu.VMEM((2, 1, width), f32),
+            pltpu.VMEM((2, 1, width), f32),
+            pltpu.SemaphoreType.DMA((zs + 2,)),
+            pltpu.SemaphoreType.DMA((zs + 2,)),
+            *line_scratch(zs, rows, w1),
+            *line_scratch(zs, rows, w2),
+        ],
+        compiler_params=params(collective_id=1, has_side_effects=True),
+        name="last_sum",
+    )(hid, dq, dk, dv, resid, w, h, v)
+
+
 def gather_parts(parts, rows_n, cols_n):
     packed = jnp.concatenate(parts, axis=1)
     every = lax.all_gather(packed, ("row", "col"), axis=0, tiled=True)
@@ -988,10 +1055,8 @@
     staged = rows_n == 2 and cols_n % 8 == 0
     hide = hidden_pairs(rand_blocks[0])
     if staged:
-        vec = jnp.concatenate(vectors).astype(f32)[None]
-        s1 = jnp.concatenate([w_query, w_key, w_value], axis=1)
-        s2 = jnp.concatenate([w_out.T, w_up, w_down.T], axis=1)
-        q, k, v, w1, h2, vec = front(zs, hidden, s1, s2, vec)
+        weights = (w_query, w_key, w_value, w_out, w_up, w_down)
+        q, k, v, w1, h2, vec = front(zs, hidden, weights, vectors)
         ctx, p, w2 = attend(q, k, v, hide, zs, h2)
         w1, w2 = w1.reshape(2, D, QKV_W), w2.reshape(2, D, REST_W)
     else:
@@ -1010,15 +1075,9 @@
         ctx, p = attend(q, k, v, hide)
     output, resid, dctx, dw2, vs2 = middle(ctx, hidden, cotangent, w2, vec)
     if staged:
-        spread = (2, zs, 2, 2, D // cols_n)
-        g2 = dw2.reshape(spread + (REST_W,))
+        g2 = dw2.reshape(2, zs, 2, 2, D // cols_n, REST_W)
         dq, dk, dv, h2 = attend_back(q, k, v, dctx, p, zs, g2)
-    else:
-        dq, dk, dv = attend_back(q, k, v, dctx, p)
-    hgrad, dw1, vs1 = last(hidden, dq, dk, dv, resid, w1)
-    vs = jnp.concatenate([vs1, vs2[:, :, 2 * HALF :]], axis=2)
-    if staged:
-        m1, m2, vs = final(zs, dw1.reshape(spread + (QKV_W,)), h2, vs)
+        hgrad, m1, m2, vs = last_sum(zs, hidden, dq, dk, dv, resid, w1, h2, vs2)
         g_q, g_k, g_v = (m1[:, n * HALF : (n + 1) * HALF] for n in range(3))
         g_out = m2[:, :HALF].T
         g_up = m2[:, HALF : HALF + FHALF]
@@ -1028,6 +1087,9 @@
             sums.append(vs[0, at : at + width])
             at += width
         return (output, hgrad, g_q, g_k, g_v, g_out, g_up, g_down, *sums)
+    dq, dk, dv = attend_back(q, k, v, dctx, p)
+    hgrad, dw1, vs1 = last(hidden, dq, dk, dv, resid, w1)
+    vs = jnp.concatenate([vs1, vs2[:, :, 2 * HALF :]], axis=2)
     g_out, g_up, g_down = scatter_parts(dw2, (HALF, FHALF, FHALF), rows_n, cols_n)
     g_q, g_k, g_v = scatter_parts(dw1, (HALF, HALF, HALF), rows_n, cols_n)
     vs = lax.psum(vs.reshape(2, VEC_W), ("col", "row"))

time: 335 us -> 316 us (0.943)
  Pallas kernels: 312 us -> 297 us
  other arithmetic: 5.43 us -> 0.27 us
    pallas_call x3 -> x2, Pallas kernels: 112 us -> 97.1 us  [the longest x1 52.8 us: last_sum(): pl.pallas_call(functools.partial(last_sum_kernel, zs), in_specs=[vmem, vm...]
    concatenate x3 -> x0, other arithmetic: 4.54 us -> none  [the longest x1 1.73 us: on_device(): s2 = jnp.concatenate([w_out.T, w_up, w_down.T], axis=1)]
    unnamed x11 -> x4, local copies, waits for them, and re-layouts: 6.24 us -> 7.83 us
where the time goes in v5:
time: 316 us; the launch traced here: 315 us
  Pallas kernels  297 us (94%)
  local copies, waits for them, and re-layouts  17.4 us (6%)
    pallas_call x1, Pallas kernels, attend_back(): pl.pallas_call(functools.partial(attend_sum_kernel, zs), grid=(H // 2,),...  73 us
    pallas_call x1, Pallas kernels, middle(): pl.pallas_call(mid_kernel, grid=(TSTEPS + 2 * TILES,), in_specs=[pl.Block...  68.5 us
    pallas_call x1, Pallas kernels, attend(): pl.pallas_call(functools.partial(attend_gather_kernel, zs), grid=(H // 2,...  58.1 us
    pallas_call x1, Pallas kernels, last_sum(): pl.pallas_call(functools.partial(last_sum_kernel, zs), in_specs=[vmem, vm...  52.8 us
    pallas_call x1, Pallas kernels, front(): pl.pallas_call(functools.partial(front_kernel, zs), in_specs=[vmem] * 16,...  44.3 us
    unnamed x4, local copies, waits for them, and re-layouts  7.83 us

profile of v5, /device:TPU:0, one launch (start us, length us, event | category | flops | bytes accessed | tf_op | source)
XLA Modules:
  0.0 315.0 jit_solution(8025421334562389889)
XLA Ops:
  0.7 0.1 fusion.1
  0.8 0.7 copy.43
  1.5 0.1 fusion
  1.7 0.1 copy.40
  1.8 1.5 copy.38.wo_ref
  3.3 1.8 copy.39.wd_ref
  5.1 0.5 broadcast_in_dim.17
  5.6 1.3 reshape.125.hide_ref
  6.9 44.3 %front.1 = (bf16[1024,768]{1,0:T(8,128)(2,1)}, bf16[1024,768]{1,0:T(8,128)(2,1)}, bf16[1024,768]{1,0:T(8,128)(2,1)}, bf16[2,4,2,2,48,1152]{5,4,3,2,1,0:T(8,128)(...) custom-call(bf16[1024,768]{1,0:T(8,128)(2,1)} %hid_ref.3, bf16[48,384]{1,0:T(8,128)(2,1)} %wq_ref.1, ...), custom_call_target="tpu_custom_call" | custom-call | tf_op jit(solution)/shard_map/front/pallas_call | solution.py:373
  51.2 58.1 %attend_gather.1 = (bf16[1024,768]{1,0:T(8,128)(2,1)}, bf16[12,1024,1024]{2,1,0:T(8,128)(2,1)}, bf16[2,4,2,2,48,3456]{5,4,3,2,1,0:T(8,128)(2,1)}) custom-call(bf16[1024,768]{1,0:T(8,128)(2,1)} %get-tuple-element.39.q_ref, bf16[1024,768]{1,0:T(8,128)(2,1)} %get-tuple-element.40.k_ref, bf16[1024,768]{1,0:T(8,128)(2,1)} %get-tuple-element.41.v_ref, ...), custom_call_target="tpu_custom_call" | custom-call | tf_op jit(solution)/shard_map/attend_gather/pallas_call | solution.py:478
  109.4 68.5 %middle.1 = (f32[1024,768]{1,0:T(8,128)}, f32[1024,768]{1,0:T(8,128)}, bf16[1024,768]{1,0:T(8,128)(2,1)}, bf16[2,768,3456]{2,1,0:T(8,128)(2,1)}, f32[2,1,4608]{2,1,0:T(1,128)}) custom-call(bf16[1024,768]{1,0:T(8,128)(2,1)} %get-tuple-element.43.ctx_ref, bf16[1024,768]{1,0:T(8,128)(2,1)} %hid_ref.3, bf16[1024,768]{1,0:T(8,128)(2,1)} %cot_ref.1, ...), custom_call_target="tpu_custom_call" | custom-call | tf_op jit(solution)/shard_map/middle/pallas_call | solution.py:767
  177.8 73.0 %attend_sum.1 = (bf16[1024,768]{1,0:T(8,128)(2,1)}, bf16[1024,768]{1,0:T(8,128)(2,1)}, bf16[1024,768]{1,0:T(8,128)(2,1)}, bf16[4,48,3456]{2,1,0:T(8,128)(2,1)}) custom-call(bf16[1024,768]{1,0:T(8,128)(2,1)} %get-tuple-element.39.q_ref, bf16[1024,768]{1,0:T(8,128)(2,1)} %get-tuple-element.40.k_ref, bf16[1024,768]{1,0:T(8,128)(2,1)} %get-tuple-element.41.v_ref, ...), custom_call_target="tpu_custom_call" | custom-call | tf_op jit(solution)/shard_map/attend_sum/pallas_call | solution.py:574
  250.8 52.8 %last_sum.1 = (f32[1024,768]{1,0:T(8,128)}, f32[48,1152]{1,0:T(8,128)}, f32[48,3456]{1,0:T(8,128)}, f32[1,4608]{1,0:T(1,128)}) custom-call(bf16[1024,768]{1,0:T(8,128)(2,1)} %hid_ref.3, bf16[1024,768]{1,0:T(8,128)(2,1)} %get-tuple-element.50.dq_ref, bf16[1024,768]{1,0:T(8,128)(2,1)} %get-tuple-element.51.dk_ref, bf16[1024,768]{1,0:T(8,128)(2,1)} %get-tuple-element.52.dv_ref, ...), custom_call_target="tpu_custom_call" | custom-call | tf_op jit(solution)/shard_map/last_sum/pallas_call | solution.py:968
  303.6 1.3 slice_reduce_fusion
  304.9 1.3 slice_reduce_fusion.1
  306.2 1.5 slice_bitcast_fusion.1
  307.7 1.9 slice_bitcast_fusion
  309.6 1.6 fusion.3
  311.3 3.8 %copy.45 = f32[1024,768]{1,0:T(8,128)} copy(f32[1024,768]{1,0:T(8,128)} %get-tuple-element.94) | data formatting | bytes 6291456
  (3 shorter events, 0.0 us)

commit v6 on v5

--- a/solution.py
+++ b/solution.py
@@ -128,6 +128,10 @@
     return (a.astype(f32) + b.astype(f32)).astype(bf16)
 
 
+def chunks_of(zs):
+    return 2 if zs % 4 == 0 else 1
+
+
 def plane_scratch(zs, rows, width):
     half = zs // 2
     return [
@@ -137,81 +141,91 @@
         pltpu.VMEM((half, 2, rows, width), bf16),
         pltpu.VMEM((half, rows, width), bf16),
         pltpu.VMEM((half, rows, width), bf16),
-        pltpu.SemaphoreType.DMA((5,)),
-        pltpu.SemaphoreType.DMA((5,)),
+        pltpu.SemaphoreType.DMA((6 * chunks_of(zs),)),
+        pltpu.SemaphoreType.DMA((6 * chunks_of(zs),)),
         pltpu.SemaphoreType.DMA,
     ]
 
 
 class PlaneSum:
     def __init__(self, at, g, own, b1, b2x, b2y, b3y, b3x, send, recv, local):
-        half = at.zs // 2
-        self.at, self.half = at, half
+        self.at, self.half, self.chunks = at, at.zs // 2, chunks_of(at.zs)
         self.own, self.b1, self.b2x, self.b2y, self.b3y, self.b3x = own, b1, b2x, b2y, b3y, b3x
         self.g, self.send, self.recv, self.local = g, send, recv, local
+        self.size = self.half // self.chunks
+
+    def spans(self, i):
+        lo = i * self.size
+        return slice(lo, lo + self.size), slice(self.half + lo, self.half + lo + self.size)
 
     def keep(self):
         return pltpu.make_async_copy(self.g.at[:, :, :, self.at.core], self.own, self.local)
 
-    def to_core(self):
+    def first(self, i):
         at = self.at
-        return remote(self.g.at[:, :, :, 1 - at.core], self.b1, self.send, self.recv, 0, at.by_core)
-
-    def second(self):
-        at, half, sems = self.at, self.half, (self.send, self.recv)
+        return [
+            remote(
+                self.g.at[:, span, :, 1 - at.core], self.b1.at[:, span],
+                self.send, self.recv, 6 * i + n, at.by_core,
+            )
+            for n, span in enumerate(self.spans(i))
+        ]
+
+    def second(self, i):
+        at, sems = self.at, (self.send, self.recv)
+        low, high = self.spans(i)
         return (
-            remote(self.b1.at[:, 0:half, 1 - at.x], self.b2x, *sems, 1, at.by_x),
-            remote(self.b1.at[1 - at.y, half:], self.b2y, *sems, 2, at.by_y),
+            remote(self.b1.at[:, low, 1 - at.x], self.b2x.at[:, low], *sems, 6 * i + 2, at.by_x),
+            remote(self.b1.at[1 - at.y, high], self.b2y.at[low], *sems, 6 * i + 3, at.by_y),
         )
 
-    def third(self):
+    def third(self, i):
         at, sems = self.at, (self.send, self.recv)
+        low, _ = self.spans(i)
         return (
-            remote(self.b2x.at[1 - at.y], self.b3y, *sems, 3, at.by_y),
-            remote(self.b2y.at[:, 1 - at.x], self.b3x, *sems, 4, at.by_x),
+            remote(self.b2x.at[1 - at.y, low], self.b3y.at[low], *sems, 6 * i + 4, at.by_y),
+            remote(self.b2y.at[low, 1 - at.x], self.b3x.at[low], *sems, 6 * i + 5, at.by_x),
         )
 
     def stage1(self):
         if self.own is not None:
             self.keep().start()
-        self.to_core().start()
-
-    def stage2(self):
-        if self.own is not None:
+        for i in range(self.chunks):
+            start_all(self.first(i))
+
+    def stage2(self, i):
+        if self.own is not None and i == 0:
             self.keep().wait()
-        self.to_core().wait()
+        wait_all(self.first(i))
         b1, own, core = self.b1, self.own, self.at.core
 
-        @pl.loop(0, self.at.zs)
-        def _(z):
-            for y in range(2):
-                for x in range(2):
-                    mine = self.g[y, z, x, core] if own is None else own[y, z, x]
-                    b1[y, z, x] = add_low(b1[y, z, x], mine)
-
-        for copy in self.second():
-            copy.start()
-
-    def stage3(self):
-        for copy in self.second():
-            copy.wait()
+        @pl.loop(i * self.size, (i + 1) * self.size)
+        def _(n):
+            for z in (n, self.half + n):
+                for y in range(2):
+                    for x in range(2):
+                        mine = self.g[y, z, x, core] if own is None else own[y, z, x]
+                        b1[y, z, x] = add_low(b1[y, z, x], mine)
+
+        start_all(self.second(i))
+
+    def stage3(self, i):
+        wait_all(self.second(i))
         b1, b2x, b2y, half = self.b1, self.b2x, self.b2y, self.half
 
-        @pl.loop(0, half)
+        @pl.loop(i * self.size, (i + 1) * self.size)
         def _(z):
             for n in range(2):
                 b2x[n, z] = add_low(b2x[n, z], b1[n, z, self.at.x])
                 b2y[z, n] = add_low(b2y[z, n], b1[self.at.y, half + z, n])
 
-        for copy in self.third():
-            copy.start()
-
-    def finish(self, out):
-        for copy in self.third():
-            copy.wait()
+        start_all(self.third(i))
+
+    def finish(self, i, out):
+        wait_all(self.third(i))
         half = self.half
 
-        @pl.loop(0, half)
+        @pl.loop(i * self.size, (i + 1) * self.size)
         def _(z):
             out[z] = add_low(self.b3y[z], self.b2x[self.at.y, z])
             out[half + z] = add_low(self.b3x[z], self.b2y[z, self.at.x])
@@ -247,21 +261,23 @@
 
 
 class PlaneGather:
-    def __init__(self, at, h, g, send, recv):
+    def __init__(self, at, h, g, send, recv, cols=slice(None), sem=0):
         self.at, self.h, self.g, self.send, self.recv = at, h, g, send, recv
+        self.cols, self.h_cols, self.sem = cols, cols, sem
 
     def move(self, i, to, src, *where):
-        dst = self.g.at[where]
-        return remote(dst if src is None else src, dst, self.send, self.recv, i, to)
+        dst = self.g.at[where + (slice(None), self.cols)]
+        src = dst if src is None else self.h.at[src, :, self.h_cols]
+        return remote(src, dst, self.send, self.recv, self.sem + i, to)
 
     def stage1(self):
         at, half = self.at, self.at.zs // 2
         y, x, core = at.y, at.x, at.core
         every, low, high = slice(None), slice(0, half), slice(half, at.zs)
         return (
-            self.move(0, at.by_y, self.h.at[low], y, low, x, core),
-            self.move(1, at.by_x, self.h.at[high], y, high, x, core),
-            self.move(2, at.by_core, self.h, y, every, x, core),
+            self.move(0, at.by_y, low, y, low, x, core),
+            self.move(1, at.by_x, high, y, high, x, core),
+            self.move(2, at.by_core, every, y, every, x, core),
         )
 
     def stage2(self):
@@ -319,16 +335,19 @@
         width = ref.shape[0]
         vec_s[:, off : off + width] = ref[...].astype(f32).reshape(1, width)
         off += width
-    s2[:, :HALF] = wo_ref[...].T
+    s2[:, :HALF] = wo_ref[...]
     s2[:, HALF : HALF + FHALF] = wu_ref[...]
-    s2[:, HALF + FHALF :] = wd_ref[...].T
+    s2[:, HALF + FHALF :] = wd_ref[...]
     vo_ref[at.y] = vec_s[...]
     h_ref[at.z] = s2[...]
     vec = remote(vec_s, vo_ref.at[at.y], vsend, vrecv, 0, at.by_y)
     vec.start()
     wait_all(along)
     after = [
-        remote(s2, h_ref.at[at.z], lsend, lrecv, zs - 2 + d, at.by_z(d)) for d in range(1, zs)
+        remote(
+            s2.at[:, :EARLY], h_ref.at[at.z, :, :EARLY], lsend, lrecv, zs - 2 + d, at.by_z(d)
+        )
+        for d in range(1, zs)
     ]
     start_all(after)
     gather = PlaneGather(at, line, g_ref, psend, precv)
@@ -363,6 +382,7 @@
 
 
 QROWS = 256
+EARLY = HALF + FHALF
 
 
 def front(zs, x, weights, vectors):
@@ -443,33 +463,68 @@
         c_ref[at, :] = both_heads(*outs).T.astype(bf16)
 
 
-def attend_gather_kernel(zs, q_ref, k_ref, v_ref, hide_ref, h_ref, c_ref, p_ref, g_ref, send, recv, local):
+def attend_gather_kernel(
+    zs, q_ref, k_ref, v_ref, hide_ref, h_ref, c_ref, p_ref, g_ref, rest, send, recv, lsend, lrecv, local
+):
     step = pl.program_id(0)
     at = Place(zs)
-    gather = PlaneGather(at, h_ref, g_ref, send, recv)
-
-    def keep():
-        return pltpu.make_async_copy(h_ref, g_ref.at[at.y, :, at.x, at.core], local)
+    early = PlaneGather(at, h_ref, g_ref, send, recv, slice(0, EARLY))
+    late = PlaneGather(at, rest, g_ref, send, recv, slice(EARLY, REST_W), 9)
+    late.h_cols = slice(None)
+
+    def keep(part):
+        cols = part.cols
+        src = part.h.at[:, :, part.h_cols]
+        return pltpu.make_async_copy(
+            src, g_ref.at[at.y, :, at.x, at.core, :, cols], local.at[0 if part is early else 1]
+        )
+
+    def fetch():
+        return pltpu.make_async_copy(h_ref.at[at.z, :, EARLY:], rest.at[at.z], local.at[2])
+
+    def along():
+        return [
+            remote(h_ref.at[at.z, :, EARLY:], rest.at[at.z], lsend, lrecv, d - 1, at.by_z(d))
+            for d in range(1, zs)
+        ]
 
     @pl.when(step == 0)
     def _():
-        greet([at.by_core, at.by_x, at.by_y])
-        start_all(gather.stage1())
-        keep().start()
+        greet([at.by_core, at.by_x, at.by_y] + [at.by_z(d) for d in range(1, zs)])
+        start_all(early.stage1())
+        start_all(along())
+        keep(early).start()
+        fetch().start()
+
+    @pl.when(step == 1)
+    def _():
+        keep(early).wait()
+        wait_all(early.stage1())
+        start_all(early.stage2())
 
     @pl.when(step == 2)
     def _():
-        keep().wait()
-        wait_all(gather.stage1())
-        start_all(gather.stage2())
+        fetch().wait()
+        wait_all(along())
+        keep(late).start()
+        start_all(late.stage1())
+
+    @pl.when(step == 4)
+    def _():
+        keep(late).wait()
+        wait_all(late.stage1())
+        start_all(late.stage2())
+        wait_all(early.stage2())
+        start_all(early.stage3())
 
     attend_kernel(q_ref, k_ref, v_ref, hide_ref, c_ref, p_ref)
 
     @pl.when(step == H // 2 - 1)
     def _():
-        wait_all(gather.stage2())
-        start_all(gather.stage3())
-        wait_all(gather.stage3())
+        wait_all(early.stage3())
+        wait_all(late.stage2())
+        start_all(late.stage3())
+        wait_all(late.stage3())
 
 
 def attend(q, k, v, hide, zs=0, h2=None):
@@ -496,9 +551,12 @@
                 jax.ShapeDtypeStruct((2, zs, 2, 2) + h2.shape[1:], bf16),
             ],
             scratch_shapes=[
-                pltpu.SemaphoreType.DMA((9,)),
-                pltpu.SemaphoreType.DMA((9,)),
-                pltpu.SemaphoreType.DMA,
+                pltpu.VMEM(h2.shape[:2] + (REST_W - EARLY,), bf16),
+                pltpu.SemaphoreType.DMA((18,)),
+                pltpu.SemaphoreType.DMA((18,)),
+                pltpu.SemaphoreType.DMA((zs - 1,)),
+                pltpu.SemaphoreType.DMA((zs - 1,)),
+                pltpu.SemaphoreType.DMA((3,)),
             ],
             compiler_params=params(collective_id=4, has_side_effects=True),
             name="attend_gather",
@@ -526,19 +584,22 @@
         greet([at.by_core, at.by_x, at.by_y])
         PlaneSum(at, g_ref, *plane).stage1()
 
-    @pl.when(step == 2)
-    def _():
-        PlaneSum(at, g_ref, *plane).stage2()
-
-    @pl.when(step == 5)
-    def _():
-        PlaneSum(at, g_ref, *plane).stage3()
+    for i in range(chunks_of(zs)):
+
+        @pl.when(step == 1 + i)
+        def _(i=i):
+            PlaneSum(at, g_ref, *plane).stage2(i)
+
+        @pl.when(step == 3 + 2 * i)
+        def _(i=i):
+            PlaneSum(at, g_ref, *plane).stage3(i)
 
     attend_back_kernel(q_ref, k_ref, v_ref, d_ref, p_ref, dq_ref, dk_ref, dv_ref, ds_s)
 
-    @pl.when(step == 5)
-    def _():
-        PlaneSum(at, g_ref, *plane).finish(h_ref)
+    @pl.when(step == H // 2 - 1)
+    def _():
+        for i in range(chunks_of(zs)):
+            PlaneSum(at, g_ref, *plane).finish(i, h_ref)
 
 
 def attend_back_kernel(q_ref, k_ref, v_ref, d_ref, p_ref, dq_ref, dk_ref, dv_ref, ds_s):
@@ -933,13 +994,15 @@
     va[...] = vs[...] + v1[...]
     vec2 = remote(va, v2, vsend, vrecv, 1, at.by_x)
     vec2.start()
-    first.stage2()
+    for i in range(first.chunks):
+        first.stage2(i)
     pl.loop(tiles // 2, tiles)(input_grad)
     vec2.wait()
     vb[...] = va[...] + v2[...]
     vec3 = remote(vb.at[1 - at.y], v3, vsend, vrecv, 2, at.by_y)
     vec3.start()
-    first.stage3()
+    for i in range(first.chunks):
+        first.stage3(i)
     vec3.wait()
     v4[0] = vb[at.y] + v3[...]
     vec4 = [
@@ -947,7 +1010,8 @@
     ]
     start_all(vec4)
     second.finish(o2_ref)
-    first.finish(mid)
+    for i in range(first.chunks):
+        first.finish(i, mid)
     third = LineSum(at, mid, *line1)
     third.start()
     wait_all(vec4)
@@ -1055,7 +1119,7 @@
     staged = rows_n == 2 and cols_n % 8 == 0
     hide = hidden_pairs(rand_blocks[0])
     if staged:
-        weights = (w_query, w_key, w_value, w_out, w_up, w_down)
+        weights = (w_query, w_key, w_value, w_out.T, w_up, w_down.T)
         q, k, v, w1, h2, vec = front(zs, hidden, weights, vectors)
         ctx, p, w2 = attend(q, k, v, hide, zs, h2)
         w1, w2 = w1.reshape(2, D, QKV_W), w2.reshape(2, D, REST_W)

time: 316 us -> 302 us (0.956)
  Pallas kernels: 297 us -> 287 us
  local copies, waits for them, and re-layouts: 17.4 us -> 14.1 us
    pallas_call x1, Pallas kernels: 73 us -> 64.9 us  [attend_back(): pl.pallas_call(functools.partial(attend_sum_kernel, zs), grid=(H // 2,),...]
    pallas_call x1, Pallas kernels: 52.8 us -> 49.2 us  [last_sum(): pl.pallas_call(functools.partial(last_sum_kernel, zs), in_specs=[vmem, vm...]
    unnamed x4 -> x2, local copies, waits for them, and re-layouts: 7.83 us -> 4.48 us
where the time goes in v6:
time: 302 us
  Pallas kernels  287 us (95%)
  local copies, waits for them, and re-layouts  14.1 us (5%)
    pallas_call x1, Pallas kernels, middle(): pl.pallas_call(mid_kernel, grid=(TSTEPS + 2 * TILES,), in_specs=[pl.Block...  68.5 us
    pallas_call x1, Pallas kernels, attend_back(): pl.pallas_call(functools.partial(attend_sum_kernel, zs), grid=(H // 2,),...  64.9 us
    pallas_call x1, Pallas kernels, attend(): pl.pallas_call(functools.partial(attend_gather_kernel, zs), grid=(H // 2,...  60.4 us
    pallas_call x1, Pallas kernels, last_sum(): pl.pallas_call(functools.partial(last_sum_kernel, zs), in_specs=[vmem, vm...  49.2 us
    pallas_call x1, Pallas kernels, front(): pl.pallas_call(functools.partial(front_kernel, zs), in_specs=[vmem] * 16,...  43.8 us

profile of v6, /device:TPU:0, one launch (start us, length us, event | category | flops | bytes accessed | tf_op | source)
XLA Modules:
  0.0 301.9 jit_solution(3311124413153479583)
XLA Ops:
  0.7 0.1 fusion.1
  0.8 0.7 copy.39
  1.5 0.1 fusion
  1.7 0.1 copy.36
  1.8 0.5 broadcast_in_dim.17
  2.2 1.3 reshape.125.hide_ref
  3.6 43.8 %front.1 = (bf16[1024,768]{1,0:T(8,128)(2,1)}, bf16[1024,768]{1,0:T(8,128)(2,1)}, bf16[1024,768]{1,0:T(8,128)(2,1)}, bf16[2,4,2,2,48,1152]{5,4,3,2,1,0:T(8,128)(...) custom-call(bf16[1024,768]{1,0:T(8,128)(2,1)} %hid_ref.3, bf16[48,384]{1,0:T(8,128)(2,1)} %wq_ref.1, ...), custom_call_target="tpu_custom_call" | custom-call | tf_op jit(solution)/shard_map/front/pallas_call | solution.py:393
  47.4 60.4 %attend_gather.1 = (bf16[1024,768]{1,0:T(8,128)(2,1)}, bf16[12,1024,1024]{2,1,0:T(8,128)(2,1)}, bf16[2,4,2,2,48,3456]{5,4,3,2,1,0:T(8,128)(2,1)}) custom-call(bf16[1024,768]{1,0:T(8,128)(2,1)} %get-tuple-element.39.q_ref, bf16[1024,768]{1,0:T(8,128)(2,1)} %get-tuple-element.40.k_ref, bf16[1024,768]{1,0:T(8,128)(2,1)} %get-tuple-element.41.v_ref, ...), custom_call_target="tpu_custom_call" | custom-call | tf_op jit(solution)/shard_map/attend_gather/pallas_call | solution.py:533
  107.8 68.5 %middle.1 = (f32[1024,768]{1,0:T(8,128)}, f32[1024,768]{1,0:T(8,128)}, bf16[1024,768]{1,0:T(8,128)(2,1)}, bf16[2,768,3456]{2,1,0:T(8,128)(2,1)}, f32[2,1,4608]{2,1,0:T(1,128)}) custom-call(bf16[1024,768]{1,0:T(8,128)(2,1)} %get-tuple-element.43.ctx_ref, bf16[1024,768]{1,0:T(8,128)(2,1)} %hid_ref.3, bf16[1024,768]{1,0:T(8,128)(2,1)} %cot_ref.1, ...), custom_call_target="tpu_custom_call" | custom-call | tf_op jit(solution)/shard_map/middle/pallas_call | solution.py:828
  176.3 64.9 %attend_sum.1 = (bf16[1024,768]{1,0:T(8,128)(2,1)}, bf16[1024,768]{1,0:T(8,128)(2,1)}, bf16[1024,768]{1,0:T(8,128)(2,1)}, bf16[4,48,3456]{2,1,0:T(8,128)(2,1)}) custom-call(bf16[1024,768]{1,0:T(8,128)(2,1)} %get-tuple-element.39.q_ref, bf16[1024,768]{1,0:T(8,128)(2,1)} %get-tuple-element.40.k_ref, bf16[1024,768]{1,0:T(8,128)(2,1)} %get-tuple-element.41.v_ref, ...), custom_call_target="tpu_custom_call" | custom-call | tf_op jit(solution)/shard_map/attend_sum/pallas_call | solution.py:635
  241.2 49.2 %last_sum.1 = (f32[1024,768]{1,0:T(8,128)}, f32[48,1152]{1,0:T(8,128)}, f32[48,3456]{1,0:T(8,128)}, f32[1,4608]{1,0:T(1,128)}) custom-call(bf16[1024,768]{1,0:T(8,128)(2,1)} %hid_ref.3, bf16[1024,768]{1,0:T(8,128)(2,1)} %get-tuple-element.50.dq_ref, bf16[1024,768]{1,0:T(8,128)(2,1)} %get-tuple-element.51.dk_ref, bf16[1024,768]{1,0:T(8,128)(2,1)} %get-tuple-element.52.dv_ref, ...), custom_call_target="tpu_custom_call" | custom-call | tf_op jit(solution)/shard_map/last_sum/pallas_call | solution.py:1032
  290.4 1.3 slice_reduce_fusion
  291.7 1.3 slice_reduce_fusion.1
  293.1 1.5 slice_bitcast_fusion.1
  294.6 1.9 slice_bitcast_fusion
  296.5 1.6 fusion.3
  298.1 3.8 %copy.41 = f32[1024,768]{1,0:T(8,128)} copy(f32[1024,768]{1,0:T(8,128)} %get-tuple-element.94) | data formatting | bytes 6291456
  (3 shorter events, 0.0 us)
